TPU v7x, 32 devices: a whole 2x2x4 slice. The times are simulated.
32 devices in a mesh: lat: 8 (over z, y), lon: 4 (over x, core).
Axes of the slice: x: 2, y: 2, z: 4, core: 2. Of those that a mesh axis runs over, the one named last changes fastest.
Arguments:
- grid_latent: bfloat16 [16384, 512], P(('lat', 'lon')), may hold values from -6 to 6
- grid_feat: bfloat16 [4, 65536], P(None, ('lat', 'lon')), may hold values from -6 to 6
- grid_sender: int32 [65536], P(('lat', 'lon')), may hold values from 0 to 511
- grid_owner: int32 [65536, 1], P(('lat', 'lon')), may hold values from 0 to 7; in each aligned block of 2048 rows (0 to 2047, 2048 to 4095, ...) at most 512 rows name the same one
- grid_node: int32 [65536], P(('lat', 'lon')), may hold values from 0 to 511
- mesh_latent: bfloat16 [4096, 512], P('lat', 'lon'), may hold values from -6 to 6
- mesh_edge: bfloat16 [32768, 512], P(('lat', 'lon')), may hold values from -6 to 6
- halo_send: int32 [64, 64], P('lat'), may hold values from 0 to 511
- mesh_sender: int32 [32768], P(('lat', 'lon')), may hold values from 0 to 1023
- mesh_receiver: int32 [32768], P(('lat', 'lon')), may hold values from 0 to 511
- enc_edge_in: bfloat16 [512, 512], P(None, 'lon'), may hold values from -0.25 to 0.25
- enc_feat_proj: bfloat16 [4, 512], replicated, may hold values from -3 to 3
- enc_edge_out: bfloat16 [512, 512], P(None, 'lon'), may hold values from -0.25 to 0.25
- enc_edge_bias: float32 [2, 512], replicated, may hold values from -1.5 to 1.5
- enc_edge_gain: float32 [512], replicated, may hold values from 0.25 to 1.75
- enc_node_in: bfloat16 [1024, 512], P(None, 'lon'), may hold values from -0.1875 to 0.1875
- enc_node_out: bfloat16 [512, 512], P('lon'), may hold values from -0.25 to 0.25
- enc_node_bias: float32 [2, 512], replicated, may hold values from -1.5 to 1.5
- enc_node_gain: float32 [512], replicated, may hold values from 0.25 to 1.75
- proc_edge_in: bfloat16 [1536, 512], P(None, 'lon'), may hold values from -0.15625 to 0.15625
- proc_edge_out: bfloat16 [512, 512], P(None, 'lon'), may hold values from -0.25 to 0.25
- proc_edge_bias: float32 [2, 512], replicated, may hold values from -1.5 to 1.5
- proc_edge_gain: float32 [512], replicated, may hold values from 0.25 to 1.75
- proc_node_in: bfloat16 [1024, 512], P(None, 'lon'), may hold values from -0.1875 to 0.1875
- proc_node_out: bfloat16 [512, 512], P('lon'), may hold values from -0.25 to 0.25
- proc_node_bias: float32 [2, 512], replicated, may hold values from -1.5 to 1.5
- proc_node_gain: float32 [512], replicated, may hold values from 0.25 to 1.75
Outputs:
- mesh_update: bfloat16 [4096, 512], P('lat', 'lon')
- edge_update: bfloat16 [32768, 512], P(('lat', 'lon'))
Inputs may be any that keep to these rules, and one draw needn't show every extreme that they name: `grid_sender`: a row among the 512 grid rows of the device that holds the edge. `grid_owner`: among the 2048 edges of one device, at most 512 name the same partition, a bound that some block reaches. `halo_send`: nodes of the listing partition.
All inputs are finite; a program needn't handle non-finite values.
Results may differ from a plain program's by a relative error of at most 0.017.
Values may be sent and summed in bfloat16 or wider, within the bound.
No kernel may reach another device: no remote copies, remote signals or barrier semaphores. Data moves between devices by JAX's collectives and lax.ppermute only.
A program may use at most 128 MiB of HBM per device.

v0:
```python
import jax
import jax.numpy as jnp
from jax import lax
from jax.sharding import PartitionSpec as P


def layer_norm(values, norm_gain, offsets):
    average = jnp.mean(values, axis=-1, keepdims=True)
    centred = values - average
    spread = jnp.mean(centred * centred, axis=-1, keepdims=True)
    return centred * lax.rsqrt(spread + 1e-05) * norm_gain + offsets


def encoder_edges(source_rows, feat_term, weight_in, weight_out):
    piece_in = lax.all_gather(weight_in, "lon", axis=1, tiled=True)
    piece_out = lax.all_gather(weight_out, "lon", axis=1, tiled=True)
    pre_act = jnp.dot(source_rows, piece_in, preferred_element_type=jnp.float32)
    pre_act = pre_act + feat_term
    hidden = jax.nn.silu(pre_act).astype(jnp.bfloat16)
    return lax.dot_general(
        hidden, piece_out, (((1,), (1,)), ((), ())), preferred_element_type=jnp.float32
    )


def node_network(base, aggregate, weight_in, weight_out, biases, norm_gain):
    inputs = jnp.concatenate([base, aggregate], 1)
    columns = weight_in.shape[1]
    hidden_bias = lax.dynamic_slice_in_dim(biases[0], lax.axis_index("lon") * columns, columns)
    hidden = jax.nn.silu(
        jnp.dot(inputs, weight_in, preferred_element_type=jnp.float32) + hidden_bias
    ).astype(jnp.bfloat16)
    raw_out = lax.psum(
        jnp.dot(hidden, weight_out, preferred_element_type=jnp.float32).astype(jnp.bfloat16), "lon"
    ).astype(jnp.float32)
    return (base.astype(jnp.float32) + layer_norm(raw_out, norm_gain, biases[1])).astype(
        jnp.bfloat16
    )


def local(
    grid_latent,
    grid_feat,
    grid_sender,
    grid_owner,
    grid_node,
    mesh_latent,
    mesh_edge,
    halo_send,
    mesh_sender,
    mesh_receiver,
    enc_edge_in,
    enc_feat_proj,
    enc_edge_out,
    enc_edge_bias,
    enc_edge_gain,
    enc_node_in,
    enc_node_out,
    enc_node_bias,
    enc_node_gain,
    proc_edge_in,
    proc_edge_out,
    proc_edge_bias,
    proc_edge_gain,
    proc_node_in,
    proc_node_out,
    proc_node_bias,
    proc_node_gain,
):
    lat_count = lax.axis_size("lat")
    lon_index = lax.axis_index("lon")
    feature_width = grid_latent.shape[1]
    quarter = mesh_latent.shape[1]
    mesh_rows = mesh_latent.shape[0]
    edge_count = grid_sender.shape[0]
    capacity = max(2, 2 * edge_count // lat_count)
    slot_total = lat_count * capacity
    owners = grid_owner[:, 0]
    owner_hits = (owners[:, None] == jnp.arange(lat_count, dtype=jnp.int32)[None, :]).astype(
        jnp.int32
    )
    slot_rank = jnp.sum((jnp.cumsum(owner_hits, axis=0) - owner_hits) * owner_hits, axis=1)
    slot_index = owners * capacity + slot_rank
    node_slots = (
        jnp.full((slot_total,), -1, jnp.int32)
        .at[slot_index]
        .set(grid_node)
        .reshape(lat_count, capacity)
    )
    row_buffer = (
        jnp.zeros((slot_total, feature_width), jnp.bfloat16)
        .at[slot_index]
        .set(grid_latent[grid_sender])
    )
    feat_buffer = (
        jnp.zeros((slot_total, grid_feat.shape[0]), jnp.bfloat16).at[slot_index].set(grid_feat.T)
    )
    got_rows, got_feats, node_ids = (
        lax.all_to_all(
            row_buffer.reshape(lat_count, capacity, feature_width),
            "lat",
            split_axis=0,
            concat_axis=0,
            tiled=True,
        ),
        lax.all_to_all(
            feat_buffer.reshape(lat_count, capacity, grid_feat.shape[0]),
            "lat",
            split_axis=0,
            concat_axis=0,
            tiled=True,
        ),
        lax.all_to_all(node_slots, "lat", split_axis=0, concat_axis=0, tiled=True),
    )
    got_rows = got_rows.reshape(slot_total, feature_width)
    got_feats = got_feats.reshape(slot_total, grid_feat.shape[0])
    feat_term = (
        jnp.dot(got_feats, enc_feat_proj, preferred_element_type=jnp.float32) + enc_edge_bias[0]
    )
    raw_out = encoder_edges(got_rows, feat_term, enc_edge_in, enc_edge_out)
    arrived = layer_norm(raw_out, enc_edge_gain, enc_edge_bias[1])
    node_ids = node_ids.reshape(slot_total)
    segment_ids = jnp.where(node_ids < 0, mesh_rows, node_ids).astype(jnp.int32)
    partial_sum = jax.ops.segment_sum(arrived, segment_ids, num_segments=mesh_rows + 1)[:mesh_rows]
    gathered = lax.psum(partial_sum.astype(jnp.bfloat16), "lon")
    mesh_full = lax.all_gather(mesh_latent, "lon", axis=1, tiled=True)
    mesh_mid = node_network(
        mesh_full, gathered, enc_node_in, enc_node_out, enc_node_bias, enc_node_gain
    )
    outgoing = mesh_mid[halo_send]
    received = lax.all_to_all(outgoing, "lat", split_axis=0, concat_axis=0, tiled=True)
    table = jnp.concatenate([mesh_mid, received.reshape(-1, feature_width)], 0)
    sender_rows = table[mesh_sender]
    receiver_rows = mesh_mid[mesh_receiver]
    piece_in = lax.all_gather(proc_edge_in, "lon", axis=1, tiled=True)
    piece_out = lax.all_gather(proc_edge_out, "lon", axis=1, tiled=True)
    pre_act = jnp.dot(mesh_edge, piece_in[:feature_width], preferred_element_type=jnp.float32)
    pre_act = pre_act + jnp.dot(
        sender_rows, piece_in[feature_width : 2 * feature_width], preferred_element_type=jnp.float32
    )
    pre_act = pre_act + jnp.dot(
        receiver_rows, piece_in[2 * feature_width :], preferred_element_type=jnp.float32
    )
    pre_act = pre_act + proc_edge_bias[0]
    hidden = jax.nn.silu(pre_act).astype(jnp.bfloat16)
    edge_raw = lax.dot_general(
        hidden, piece_out, (((1,), (1,)), ((), ())), preferred_element_type=jnp.float32
    )
    edge_update = (
        mesh_edge.astype(jnp.float32) + layer_norm(edge_raw, proc_edge_gain, proc_edge_bias[1])
    ).astype(jnp.bfloat16)
    edge_onehot = (
        jnp.arange(mesh_rows, dtype=jnp.int32)[:, None] == mesh_receiver[None, :]
    ).astype(jnp.bfloat16)
    incoming = lax.psum(
        jnp.dot(edge_onehot, edge_update, preferred_element_type=jnp.float32).astype(jnp.bfloat16),
        "lon",
    )
    mesh_new = node_network(
        mesh_mid, incoming, proc_node_in, proc_node_out, proc_node_bias, proc_node_gain
    )
    mesh_update = lax.dynamic_slice_in_dim(mesh_new, lon_index * quarter, quarter, 1)
    return (mesh_update, edge_update)


def solution(mesh):
    placed = (
        P(("lat", "lon"), None),
        P(None, ("lat", "lon")),
        P(("lat", "lon")),
        P(("lat", "lon"), None),
        P(("lat", "lon")),
        P("lat", "lon"),
        P(("lat", "lon"), None),
        P("lat", None),
        P(("lat", "lon")),
        P(("lat", "lon")),
        P(None, "lon"),
        P(),
        P(None, "lon"),
        P(),
        P(),
        P(None, "lon"),
        P("lon", None),
        P(),
        P(),
        P(None, "lon"),
        P(None, "lon"),
        P(),
        P(),
        P(None, "lon"),
        P("lon", None),
        P(),
        P(),
    )
    return jax.shard_map(
        local,
        mesh=mesh,
        in_specs=placed,
        out_specs=(P("lat", "lon"), P(("lat", "lon"), None)),
        check_vma=False,
    )
```

profile of v0, /device:TPU:0, one launch (start us, length us, event | category | flops | bytes accessed | tf_op | source)
XLA Modules:
  0.0 416.4 jit_solution(599329200880381121)
XLA Ops:
  7.9 2.3 reduce-window.6
  12.2 8.8 %scatter_custom_fusion = s32[4096]{0:T(1024)} fusion(s32[2048]{0:T(1024)S(1)} %bitcast.71, s32[2048]{0:T(1024)} %param.31, s32[]{:T(128)} %constant.19.clone.1), kind=kCustom, calls=%fused_computation.87 | custom fusion | bytes 16896 | tf_op jit(solution)/shard_map/scatter | solution.py:86
  21.0 7.3 %all-to-all-start = ((s32[8,1,512]{2,1,0:T(1,128)}), s32[8,1,512]{2,1,0:T(1,128)S(1)}, u32[]{:S(2)}, u32[]{:S(2)}) async-start(s32[8,1,512]{2,1,0:T(1,128)} %bitcast.5), calls=%async_computation | async-start | bytes 32768 | tf_op jit(solution)/shard_map/all_to_all | solution.py:112
  29.0 21.3 %scatter_custom_fusion.1 = bf16[4096,512]{1,0:T(8,128)(2,1)} fusion(s32[2048]{0:T(1024)S(1)} %bitcast.72, bf16[512,512]{1,0:T(8,128)(2,1)S(1)} %copy-done, s32[2048]{0:T(1024)S(1)} %fusion.53, bf16[]{:T(256)} %constant.23.clone.1), kind=kCustom, calls=%fused_computation.11 | custom fusion | bytes 4194306 | tf_op jit(solution)/shard_map/scatter | solution.py:92
  50.3 6.1 %all-to-all-start.1 = ((bf16[8,512,512]{2,1,0:T(8,128)(2,1)}), bf16[8,512,512]{2,1,0:T(8,128)(2,1)}, u32[]{:S(2)}, u32[]{:S(2)}) async-start(bf16[8,512,512]{2,1,0:T(8,128)(2,1)} %bitcast.57), calls=%async_computation.1 | async-start | bytes 8388608 | tf_op jit(solution)/shard_map/all_to_all | solution.py:98
  56.8 6.1 %scatter_custom_fusion.2 = bf16[4096,4]{1,0:T(8,128)(2,1)S(1)} fusion(s32[2048]{0:T(1024)S(1)} %bitcast.73, bf16[2048,4]{1,0:T(8,128)(2,1)S(1)} %copy.41, bf16[]{:T(256)} %constant.23.clone.1), kind=kCustom, calls=%fused_computation.56 | custom fusion | bytes 32770 | tf_op jit(solution)/shard_map/scatter | solution.py:95
  63.9 7.2 %all_gather.16 = bf16[512,512]{1,0:T(8,128)(2,1)S(1)} all-gather(bf16[512,128]{1,0:T(8,128)(2,1)S(1)} %copy-done.8), channel_id=1, replica_groups=mesh['lat'=8,'lon'=4] {'lon'}, dimensions={1}, use_global_device_ids=true | all-gather | bytes 655360 | tf_op jit(solution)/shard_map/all_gather | solution.py:15
  71.1 7.3 %all_gather.17 = bf16[512,512]{1,0:T(8,128)(2,1)S(1)} all-gather(bf16[512,128]{1,0:T(8,128)(2,1)S(1)} %copy-done.9), channel_id=1, replica_groups=mesh['lat'=8,'lon'=4] {'lon'}, dimensions={1}, use_global_device_ids=true | all-gather | bytes 655360 | tf_op jit(solution)/shard_map/all_gather | solution.py:16
  78.4 70.7 %all-to-all-done.1 = bf16[8,512,512]{2,1,0:T(8,128)(2,1)} async-done(((bf16[8,512,512]{2,1,0:T(8,128)(2,1)}), bf16[8,512,512]{2,1,0:T(8,128)(2,1)}, u32[]{:S(2)}, u32[]{:S(2)}) %all-to-all-start.1) | async-done | bytes 4194336 | tf_op jit(solution)/shard_map/all_to_all | solution.py:98
  149.2 3.6 all-to-all-start.2
  153.0 7.7 %fusion.76 = f32[4096,512]{1,0:T(8,128)} fusion(bf16[4096,512]{1,0:T(8,128)(2,1)} %bitcast.9, bf16[512,512]{1,0:T(8,128)(2,1)S(1)} %all_gather.16), kind=kOutput, calls=%fused_computation.114 | convolution fusion | flops 2147483648 | bytes 13107200 | tf_op jit(solution)/shard_map/dot_general | solution.py:17
  160.8 8.9 %fusion.72 = (f32[4096]{0:T(1024)S(1)}, f32[4096,512]{0,1:T(8,128)}) fusion(bf16[512,512]{1,0:T(8,128)(2,1)S(1)} %all_gather.17, f32[4096,512]{1,0:T(8,128)} %fusion.76, bf16[4096,4]{0,1:T(4,128)(2,1)S(1)} %bitcast.64, bf16[4,512]{1,0:T(4,128)(2,1)S(1)} %copy-done.27, f32[512]{0:T(512)S(1)} %bitcast.74), kind=kOutput, calls=%fused_computation.112 | convolution fusion | flops 2181033984 | bytes 17356800 | tf_op jit(solution)/shard_map/dot_general | solution.py:20
  169.7 4.5 %multiply_reduce_fusion = f32[4096]{0:T(1024)S(1)} fusion(f32[4096,512]{0,1:T(8,128)} %get-tuple-element.21, f32[4096]{0:T(1024)S(1)} %broadcast_multiply_fusion), kind=kLoop, calls=%fused_computation.9 | loop fusion | flops 6287360 | bytes 8421376 | tf_op jit(solution)/shard_map/reduce_sum | solution.py:10
  175.5 5.1 %multiply_add_fusion = f32[4096,512]{0,1:T(8,128)} fusion(f32[4096,512]{0,1:T(8,128)S(1)} %copy-done.2, f32[512]{0:T(512)S(1)} %bitcast.70, f32[512]{0:T(512)S(1)} %copy-done.21, f32[4096]{0:T(1024)S(1)} %add_rsqrt_fusion, f32[4096]{0:T(1024)S(1)} %broadcast_multiply_fusion), kind=kLoop, calls=%fused_computation.8 | loop fusion | flops 8388608 | bytes 16814080 | tf_op jit(solution)/shard_map/add | solution.py:11
  180.6 9.0 %copy.43 = f32[4096,512]{1,0:T(8,128)} copy(f32[4096,512]{0,1:T(8,128)} %multiply_add_fusion) | data formatting | bytes 16777216 | tf_op jit(solution)/shard_map/add | solution.py:11
  189.6 27.6 %scatter_custom_fusion.3 = f32[513,512]{1,0:T(8,128)S(1)} fusion(s32[4096]{0:T(1024)S(1)} %bitcast.67, f32[4096,512]{1,0:T(8,128)} %copy.43, f32[]{:T(128)} %constant.18.clone.1), kind=kCustom, calls=%fused_computation.49 | custom fusion | flops 2097152 | bytes 1051136 | tf_op jit(solution)/shard_map/scatter-add | solution.py:123
  218.2 7.0 %all_gather.15 = bf16[512,512]{1,0:T(8,128)(2,1)S(1)} all-gather(bf16[512,128]{1,0:T(8,128)(2,1)S(1)} %copy-done.10), channel_id=1, replica_groups=mesh['lat'=8,'lon'=4] {'lon'}, dimensions={1}, use_global_device_ids=true | all-gather | bytes 655360 | tf_op jit(solution)/shard_map/all_gather | solution.py:125
  225.2 27.3 %all-reduce.5.cloned.1.call-done = bf16[512,512]{1,0:T(8,128)(2,1)} async-done(((bf16[512,512]{1,0:T(8,128)(2,1)}), bf16[512,512]{1,0:T(8,128)(2,1)}) %all-reduce.5.cloned.1.call-update) | async-done | bytes 524304 | tf_op jit(solution)/shard_map/psum | solution.py:124
  252.5 2.4 convolution_convert_fusion.1
  257.1 31.5 %all-reduce.7.cloned.1.call-done = bf16[512,512]{1,0:T(8,128)(2,1)} async-done(((bf16[512,512]{1,0:T(8,128)(2,1)}), bf16[512,512]{1,0:T(8,128)(2,1)}) %all-reduce.7.cloned.1.call-update) | async-done | bytes 524304 | tf_op jit(solution)/shard_map/psum | solution.py:32
  292.6 2.6 gather_fusion
  295.2 5.5 %all-to-all-start.3 = ((bf16[8,64,512]{2,1,0:T(8,128)(2,1)}), bf16[8,64,512]{2,1,0:T(8,128)(2,1)S(1)}, u32[]{:S(2)}, u32[]{:S(2)}) async-start(bf16[8,64,512]{2,1,0:T(8,128)(2,1)} %bitcast.17), calls=%async_computation.3 | async-start | bytes 1048576 | tf_op jit(solution)/shard_map/all_to_all | solution.py:130
  300.8 10.7 %all_gather.19 = bf16[512,512]{1,0:T(8,128)(2,1)} all-gather(bf16[512,128]{1,0:T(8,128)(2,1)S(1)} %copy-done.11), channel_id=1, replica_groups=mesh['lat'=8,'lon'=4] {'lon'}, dimensions={1}, use_global_device_ids=true | all-gather | bytes 655360 | tf_op jit(solution)/shard_map/all_gather | solution.py:135
  312.9 3.1 fusion.29
  316.0 5.1 %gather_fusion.2 = bf16[1024,512]{1,0:T(8,128)(2,1)} fusion(bf16[512,512]{1,0:T(8,128)(2,1)S(1)} %fusion.13, s32[1024]{0:T(1024)S(1)} %fusion.57), kind=kCustom, calls=%fused_computation.3 | custom fusion | bytes 2101248 | tf_op jit(solution)/shard_map/gather | solution.py:133
  321.2 4.0 gather_fusion.1
  325.2 3.1 fusion.27
  328.3 4.3 %fusion.73 = (f32[1024]{0:T(1024)S(1)}, f32[1024,512]{0,1:T(8,128)S(1)}) fusion(bf16[512,512]{1,0:T(8,128)(2,1)S(1)} %copy-done.7, f32[1024,512]{1,0:T(8,128)} %fusion.29, f32[1024,512]{1,0:T(8,128)} %fusion.27, bf16[1024,512]{1,0:T(8,128)(2,1)} %gather_fusion.2, f32[512]{0:T(512)S(1)} %bitcast.75, bf16[1536,512]{1,0:T(8,128)(2,1)} %all-gather.2.cloned.1.call-done), kind=kOutput, calls=%fused_computation.113 | convolution fusion | flops 1078459392 | bytes 8394752 | tf_op jit(solution)/shard_map/dot_general | solution.py:145
  335.3 1.5 fusion.6
  337.0 33.5 %all-reduce.9.cloned.1.call-done = bf16[512,512]{1,0:T(8,128)(2,1)} async-done(((bf16[512,512]{1,0:T(8,128)(2,1)}), bf16[512,512]{1,0:T(8,128)(2,1)}) %all-reduce.9.cloned.1.call-update) | async-done | bytes 524304 | tf_op jit(solution)/shard_map/psum | solution.py:154
  370.4 2.4 convolution_convert_fusion
  375.1 31.5 %all-reduce.11.cloned.1.call-done = bf16[512,512]{1,0:T(8,128)(2,1)} async-done(((bf16[512,512]{1,0:T(8,128)(2,1)}), bf16[512,512]{1,0:T(8,128)(2,1)}) %all-reduce.11.cloned.1.call-update) | async-done | bytes 524304 | tf_op jit(solution)/shard_map/psum | solution.py:32
  (113 shorter events, 23.2 us)
Async XLA Ops:
  7.2 21.9 %copy-start = (bf16[512,512]{1,0:T(8,128)(2,1)S(1)}, bf16[512,512]{1,0:T(8,128)(2,1)}, u32[]{:S(2)}) copy-start(bf16[512,512]{1,0:T(8,128)(2,1)} %param.27) | copy-start | bytes 1572868
  21.0 29.3 %all-to-all-start = ((s32[8,1,512]{2,1,0:T(1,128)}), s32[8,1,512]{2,1,0:T(1,128)S(1)}, u32[]{:S(2)}, u32[]{:S(2)}) async-start(s32[8,1,512]{2,1,0:T(1,128)} %bitcast.5), calls=%async_computation | async-start | bytes 32768 | tf_op jit(solution)/shard_map/all_to_all | solution.py:112
  50.3 6.2 %copy-start.12 = (bf16[4,2048]{1,0:T(4,128)(2,1)S(1)}, bf16[4,2048]{1,0:T(4,128)(2,1)}, u32[]{:S(2)}) copy-start(bf16[4,2048]{1,0:T(4,128)(2,1)} %param.28) | copy-start | bytes 49156
  50.3 98.9 %all-to-all-start.1 = ((bf16[8,512,512]{2,1,0:T(8,128)(2,1)}), bf16[8,512,512]{2,1,0:T(8,128)(2,1)}, u32[]{:S(2)}, u32[]{:S(2)}) async-start(bf16[8,512,512]{2,1,0:T(8,128)(2,1)} %bitcast.57), calls=%async_computation.1 | async-start | bytes 8388608 | tf_op jit(solution)/shard_map/all_to_all | solution.py:98
  56.4 7.5 %copy-start.8 = (bf16[512,128]{1,0:T(8,128)(2,1)S(1)}, bf16[512,128]{1,0:T(8,128)(2,1)}, u32[]{:S(2)}) copy-start(bf16[512,128]{1,0:T(8,128)(2,1)} %param.37) | copy-start | bytes 393220
  56.4 14.7 %copy-start.9 = (bf16[512,128]{1,0:T(8,128)(2,1)S(1)}, bf16[512,128]{1,0:T(8,128)(2,1)}, u32[]{:S(2)}) copy-start(bf16[512,128]{1,0:T(8,128)(2,1)} %param.39) | copy-start | bytes 393220
  56.5 21.9 %copy-start.13 = (f32[2,512]{1,0:T(2,128)S(1)}, f32[2,512]{1,0:T(2,128)}, u32[]{:S(2)}) copy-start(f32[2,512]{1,0:T(2,128)} %param.40) | copy-start | bytes 12292
  56.5 21.9 %copy-start.14 = (f32[2,512]{1,0:T(2,128)S(1)}, f32[2,512]{1,0:T(2,128)}, u32[]{:S(2)}) copy-start(f32[2,512]{1,0:T(2,128)} %param.44) | copy-start | bytes 12292
  149.2 11.6 %all-to-all-start.2 = ((bf16[8,512,4]{1,2,0:T(4,128)(2,1)}), bf16[8,512,4]{1,2,0:T(4,128)(2,1)S(1)}, u32[]{:S(2)}, u32[]{:S(2)}) async-start(bf16[8,512,4]{1,2,0:T(4,128)(2,1)} %copy.42), calls=%async_computation.2 | async-start | bytes 65536 | tf_op jit(solution)/shard_map/all_to_all | solution.py:105
  152.8 99.7 %all-reduce.5.cloned.1.call-start = ((), (), s32[]{:S(2)}) async-start(), calls=%async_computation.4 | async-start | bytes 1048576 | tf_op jit(solution)/shard_map/psum | solution.py:124
  153.0 7.8 %copy-start.27 = (bf16[4,512]{1,0:T(4,128)(2,1)S(1)}, bf16[4,512]{1,0:T(4,128)(2,1)}, u32[]{:S(2)}) copy-start(bf16[4,512]{1,0:T(4,128)(2,1)} %param.38) | copy-start | bytes 12292
  169.7 5.8 %copy-start.2 = (f32[4096,512]{0,1:T(8,128)S(1)}, f32[4096,512]{0,1:T(8,128)}, u32[]{:S(2)}) copy-start(f32[4096,512]{0,1:T(8,128)} %get-tuple-element.21) | copy-start | bytes 25165828
  169.7 5.8 %copy-start.21 = (f32[512]{0:T(512)S(1)}, f32[512]{0:T(512)}, u32[]{:S(2)}) copy-start(f32[512]{0:T(512)} %param.41) | copy-start | bytes 6148
  189.6 28.5 %copy-start.10 = (bf16[512,128]{1,0:T(8,128)(2,1)S(1)}, bf16[512,128]{1,0:T(8,128)(2,1)}, u32[]{:S(2)}) copy-start(bf16[512,128]{1,0:T(8,128)(2,1)} %param.32) | copy-start | bytes 393220
  189.6 62.9 %copy-start.23 = (bf16[1024,128]{1,0:T(8,128)(2,1)S(1)}, bf16[1024,128]{1,0:T(8,128)(2,1)}, u32[]{:S(2)}) copy-start(bf16[1024,128]{1,0:T(8,128)(2,1)} %param.42) | copy-start | bytes 786436
  189.6 62.9 %copy-start.25 = (bf16[128,512]{1,0:T(8,128)(2,1)S(1)}, bf16[128,512]{1,0:T(8,128)(2,1)}, u32[]{:S(2)}) copy-start(bf16[128,512]{1,0:T(8,128)(2,1)} %param.43) | copy-start | bytes 393220
  218.1 70.5 %all-reduce.7.cloned.1.call-start = ((), (), s32[]{:S(2)}) async-start(), calls=%async_computation.5 | async-start | bytes 1048576 | tf_op jit(solution)/shard_map/psum | solution.py:32
  225.2 30.4 %copy-start.15 = (s32[8,64]{1,0:T(8,128)S(1)}, s32[8,64]{1,0:T(8,128)}, u32[]{:S(2)}) copy-start(s32[8,64]{1,0:T(8,128)} %param.34) | copy-start | bytes 6148
  225.2 30.5 %copy-start.3 = (bf16[1024,512]{1,0:T(8,128)(2,1)S(1)}, bf16[1024,512]{1,0:T(8,128)(2,1)}, u32[]{:S(2)}) copy-start(bf16[1024,512]{1,0:T(8,128)(2,1)} %param.33) | copy-start | bytes 3145732
  254.9 36.3 %copy-start.22 = (f32[512]{0:T(512)S(1)}, f32[512]{0:T(512)}, u32[]{:S(2)}) copy-start(f32[512]{0:T(512)} %param.45) | copy-start | bytes 6148
  254.9 58.0 %all-gather.2.cloned.1.call-start = ((), (), s32[]{:S(2)}) async-start(), calls=%async_computation.6 | async-start | bytes 1966080 | tf_op jit(solution)/shard_map/all_gather | solution.py:134
  292.5 8.2 %copy-start.11 = (bf16[512,128]{1,0:T(8,128)(2,1)S(1)}, bf16[512,128]{1,0:T(8,128)(2,1)}, u32[]{:S(2)}) copy-start(bf16[512,128]{1,0:T(8,128)(2,1)} %param.47) | copy-start | bytes 393220
  292.5 19.0 %copy-start.18 = (s32[1024]{0:T(1024)S(1)}, s32[1024]{0:T(1024)}, u32[]{:S(2)}) copy-start(s32[1024]{0:T(1024)} %param.36) | copy-start | bytes 12292
  292.6 19.0 %copy-start.17 = (f32[2,512]{1,0:T(2,128)S(1)}, f32[2,512]{1,0:T(2,128)}, u32[]{:S(2)}) copy-start(f32[2,512]{1,0:T(2,128)} %param.48) | copy-start | bytes 12292
  295.2 25.9 %all-to-all-start.3 = ((bf16[8,64,512]{2,1,0:T(8,128)(2,1)}), bf16[8,64,512]{2,1,0:T(8,128)(2,1)S(1)}, u32[]{:S(2)}, u32[]{:S(2)}) async-start(bf16[8,64,512]{2,1,0:T(8,128)(2,1)} %bitcast.17), calls=%async_computation.3 | async-start | bytes 1048576 | tf_op jit(solution)/shard_map/all_to_all | solution.py:130
  300.7 69.7 %all-reduce.9.cloned.1.call-start = ((), (), s32[]{:S(2)}) async-start(), calls=%async_computation.7 | async-start | bytes 1048576 | tf_op jit(solution)/shard_map/psum | solution.py:154
  325.2 3.1 copy-start.7
  335.3 35.1 %copy-start.24 = (bf16[1024,128]{1,0:T(8,128)(2,1)S(1)}, bf16[1024,128]{1,0:T(8,128)(2,1)}, u32[]{:S(2)}) copy-start(bf16[1024,128]{1,0:T(8,128)(2,1)} %param.50) | copy-start | bytes 786436
  335.3 35.1 %copy-start.26 = (bf16[128,512]{1,0:T(8,128)(2,1)S(1)}, bf16[128,512]{1,0:T(8,128)(2,1)}, u32[]{:S(2)}) copy-start(bf16[128,512]{1,0:T(8,128)(2,1)} %param.51) | copy-start | bytes 393220
  336.8 69.7 %all-reduce.11.cloned.1.call-start = ((), (), s32[]{:S(2)}) async-start(), calls=%async_computation.8 | async-start | bytes 1048576 | tf_op jit(solution)/shard_map/psum | solution.py:32
  336.9 36.8 %copy-start.6 = (bf16[1024,512]{0,1:T(8,128)(2,1)S(1)}, bf16[1024,512]{0,1:T(8,128)(2,1)}, u32[]{:S(2)}) copy-start(bf16[1024,512]{0,1:T(8,128)(2,1)} %copy-done.5) | copy-start | bytes 3145732
  372.9 36.9 %copy-start.1 = (bf16[512,512]{1,0:T(8,128)(2,1)S(1)}, bf16[512,512]{1,0:T(8,128)(2,1)}, u32[]{:S(2)}) copy-start(bf16[512,512]{1,0:T(8,128)(2,1)} %param.27) | copy-start | bytes 1572868
  (5 other events, 7.2 us)
Sparse Core Ops, SparseCore 0:
  218.2 34.2 all-reduce.4
  255.0 33.5 all-reduce.6
  290.2 22.7 all-gather.1
  337.0 33.3 all-reduce.8
  373.0 33.4 all-reduce.10
where the time goes:
time: 418 us; the launch traced here: 416 us
  waiting for transfers between devices  196 us (47%)
  local copies, waits for them, and re-layouts  66.1 us (16%)
  other arithmetic  50.8 us (12%)
  matrix products  33.5 us (8%)
  blocking collectives  32.3 us (8%)
  starting transfers between devices  23.2 us (6%)
  between operations  14.2 us (3%)
    all_to_all x1, waiting for transfers between devices, local(): lax.all_to_all(row_buffer.reshape(lat_count, capacity, feature_width), 'l...  70.7 us
    psum x2, waiting for transfers between devices, node_network(): lax.psum(jnp.dot(hidden, weight_out, preferred_element_type=jnp.float32)....  63 us
    psum x1, waiting for transfers between devices, local(): lax.psum(jnp.dot(edge_onehot, edge_update, preferred_element_type=jnp.flo...  33.5 us
    scatter-add x1, other arithmetic, local(): jax.ops.segment_sum(arrived, segment_ids, num_segments=mesh_rows + 1)  27.6 us
    psum x1, waiting for transfers between devices, local(): gathered = lax.psum(partial_sum.astype(jnp.bfloat16), 'lon')  27.3 us
    scatter x1, local copies, waits for them, and re-layouts, local(): row_buffer = jnp.zeros((slot_total, feature_width), jnp.bfloat16).at[slot...  21.3 us
    all_gather x1, blocking collectives, local(): piece_out = lax.all_gather(proc_edge_out, 'lon', axis=1, tiled=True)  10.7 us
    add x1, local copies, waits for them, and re-layouts, layer_norm(): return centred * lax.rsqrt(spread + 1e-05) * norm_gain + offsets  8.98 us
  transfers between devices with their start and end apart: 9, of which 6 were waited for; matrix products, arithmetic and copies ran while one was open for 13% of the time, Pallas kernels for 0%

commit v1 on v0

v1 whole, which is shorter than its diff:
```python
import functools
import jax
import jax.numpy as jnp
from jax import lax
from jax.experimental import pallas as pl
from jax.experimental.pallas import tpu as pltpu
from jax.sharding import PartitionSpec as P

F32 = jnp.float32
BF16 = jnp.bfloat16
I32 = jnp.int32
SPLIT = 32
CHUNK = 256
META = 16

VMEM = pl.BlockSpec(memory_space=pltpu.VMEM)
SMEM = pl.BlockSpec(memory_space=pltpu.SMEM)


def dot(a, b, ca=1, cb=0):
    return lax.dot_general(a, b, (((ca,), (cb,)), ((), ())), preferred_element_type=F32)


def cost(flops, nbytes):
    return pl.CostEstimate(flops=int(flops), bytes_accessed=int(nbytes), transcendentals=0)


def call(kernel, out_shape, n_in, flops, scratch=(), smem=0, n_out=1):
    return pl.pallas_call(
        kernel,
        out_shape=out_shape,
        in_specs=[SMEM] * smem + [VMEM] * (n_in - smem),
        out_specs=VMEM if n_out == 1 else [VMEM] * n_out,
        scratch_shapes=list(scratch),
        cost_estimate=cost(flops, 4 << 20),
        compiler_params=pltpu.CompilerParams(vmem_limit_bytes=56 << 20),
    )


def silu(t):
    return t / (1.0 + jnp.exp(-t))


def normed(raw, gain, offset, axis):
    width = raw.shape[axis]
    average = jnp.sum(raw, axis=axis, keepdims=True) * (1.0 / width)
    centred = raw - average
    spread = jnp.sum(centred * centred, axis=axis, keepdims=True) * (1.0 / width)
    return centred * lax.rsqrt(spread + 1e-05) * gain + offset


def sort_kernel(lat_count, mesh_rows, owner_ref, sender_ref, node_ref, feat_ref, key_ref, send_ref, feats_ref, start_ref):
    edges = owner_ref.shape[1]
    owner = owner_ref[...]
    parts = lax.broadcasted_iota(I32, (lat_count, edges), 0)
    hits = jnp.where(parts == owner, 1.0, 0.0)
    lane = lax.broadcasted_iota(I32, (lat_count, edges), 1)
    count = hits
    step = 1
    while step < edges:
        count = count + jnp.where(lane >= step, pltpu.roll(count, step, 1), 0.0)
        step *= 2
    first = jnp.sum(jnp.where(owner < parts, 1.0, 0.0), axis=1, keepdims=True)
    place = jnp.sum(hits * (first + count - hits), axis=0, keepdims=True).astype(I32)
    start_ref[...] = jnp.broadcast_to(first, start_ref.shape).astype(I32)
    sender = sender_ref[...]
    node = node_ref[...]
    digits = [sender // SPLIT, sender % SPLIT, node // SPLIT, node % SPLIT, owner]
    rows = [d.astype(F32) for d in digits] + [feat_ref[...].astype(F32)]
    used = len(digits) + feat_ref.shape[0]
    meta = jnp.concatenate(rows + [jnp.ones((META - used, edges), F32)], 0).astype(BF16)
    block = 512

    @pl.loop(0, edges // block)
    def _(i):
        spot = lax.broadcasted_iota(I32, (block, edges), 0) + i * block
        perm = jnp.where(spot == place, 1.0, 0.0).astype(BF16)
        moved = dot(meta, perm, 1, 1)
        at = pl.ds(pl.multiple_of(i * block, block), block)
        ints = moved.astype(I32)
        send_ref[:, at] = ints[0:1] * SPLIT + ints[1:2]
        key_ref[:, at] = ints[4:5] * mesh_rows + ints[2:3] * SPLIT + ints[3:4]
        feats_ref[:, at] = moved.astype(BF16)


def message_kernel(n_feat, lon_ref, rows_ref, send_ref, feats_ref, proj_ref, bias_ref, gain_ref, w0, w1, w2, w3, out_ref, win, wout, proj):
    width = rows_ref.shape[1]
    quarter = w0.shape[1]
    lon = lon_ref[0]
    for j, w in enumerate((w0, w1, w2, w3)):
        win[:, j * quarter : (j + 1) * quarter] = w[0:width, :]
        wout[:, j * quarter : (j + 1) * quarter] = w[width : 2 * width, :]
        at = pl.ds(pl.multiple_of((lon ^ j) * quarter, quarter), quarter)
        bias = bias_ref[0:1, at]
        high = bias.astype(BF16).astype(F32)
        mid = (bias - high).astype(BF16).astype(F32)
        low = bias - high - mid
        used = META - 5 - n_feat
        proj[:, j * quarter : (j + 1) * quarter] = jnp.concatenate(
            [jnp.zeros((5, quarter), F32), proj_ref[:, at].astype(F32), high, mid, low, jnp.zeros((used - 3, quarter), F32)], 0
        ).astype(BF16)
    rows = rows_ref[...]
    table = dot(win[...], rows, 0, 1).astype(BF16)
    columns = jnp.transpose(gain_ref[...])
    gain, offset = columns[:, 0:1], columns[:, 1:2]
    edges = send_ref.shape[1]
    block = CHUNK

    @pl.loop(0, edges // block)
    def _(i):
        at = pl.ds(pl.multiple_of(i * block, block), block)
        source = lax.broadcasted_iota(I32, (rows.shape[0], block), 0)
        pick = jnp.where(source == send_ref[:, at], 1.0, 0.0).astype(BF16)
        pre = dot(table, pick) + dot(proj[...], feats_ref[:, at], 0, 0)
        hidden = silu(pre).astype(BF16)
        raw = dot(wout[...], hidden)
        out_ref[i] = normed(raw, gain, offset, 0).astype(BF16)


def sums_kernel(mesh_rows, edges, start_ref, core_ref, key_ref, msg_ref, out_ref):
    part = pl.program_id(0)
    parts = pl.num_programs(0)
    begin = start_ref[part]
    end = jnp.where(part + 1 < parts, start_ref[jnp.minimum(part + 1, parts - 1)], edges)
    quarter = out_ref.shape[2]
    core = core_ref[0]
    half = 2 * quarter
    row = lax.broadcasted_iota(I32, (half, CHUNK), 0)
    node = row + jnp.where(row >= quarter, quarter, 0) + core * quarter + part * mesh_rows

    def body(i, total):
        pick = jnp.where(node == key_ref[i], 1.0, 0.0).astype(BF16)
        return total + dot(pick, msg_ref[i], 1, 1)

    total = lax.fori_loop(
        begin // CHUNK, (end + CHUNK - 1) // CHUNK, body, jnp.zeros((half, msg_ref.shape[1]), F32)
    ).astype(BF16)
    out_ref[0, 0] = total[:quarter]
    out_ref[0, 1] = total[quarter:]


def node_sums(starts, core, keys, messages, lat_count, mesh_rows, edges):
    quarter = mesh_rows // 4
    chunks, width, _ = messages.shape
    return pl.pallas_call(
        functools.partial(sums_kernel, mesh_rows, edges),
        out_shape=jax.ShapeDtypeStruct((lat_count, 2, quarter, width), BF16),
        grid=(lat_count,),
        in_specs=[SMEM, SMEM, pl.BlockSpec((chunks, 1, CHUNK), lambda p: (0, 0, 0)), pl.BlockSpec((chunks, width, CHUNK), lambda p: (0, 0, 0))],
        out_specs=pl.BlockSpec((1, 2, quarter, width), lambda p: (p, 0, 0, 0)),
        cost_estimate=cost(edges * mesh_rows * width * 2, 8 << 20),
        compiler_params=pltpu.CompilerParams(vmem_limit_bytes=48 << 20),
    )(starts, core, keys, messages)


def node_kernel(full_base, lon_ref, *refs):
    n_base = 1 if full_base else 4
    bases = refs[:n_base]
    agg_ref, bias_ref, gain_ref, w0, w1, w2, w3, out_ref, base, win, wout = refs[n_base:]
    width = agg_ref.shape[-1]
    quarter = w0.shape[1]
    lon = lon_ref[0]
    biases = []
    for j, w in enumerate((w0, w1, w2, w3)):
        win[:, j * quarter : (j + 1) * quarter] = w[0 : 2 * width, :]
        for m in range(width // quarter):
            wout[j * quarter : (j + 1) * quarter, m * quarter : (m + 1) * quarter] = w[
                2 * width + m * quarter : 2 * width + (m + 1) * quarter, :
            ]
        at = pl.ds(pl.multiple_of((lon ^ j) * quarter, quarter), quarter)
        biases.append(bias_ref[0:1, at])
        if not full_base:
            base[:, at] = bases[j][...]
    if full_base:
        base[...] = bases[0][...]
    total = agg_ref[0].astype(F32)
    for k in range(1, agg_ref.shape[0]):
        total = total + agg_ref[k].astype(F32)
    own = base[...]
    pre = dot(own, win[0:width, :]) + dot(total.astype(BF16), win[width:, :]) + jnp.concatenate(biases, 1)
    raw = dot(silu(pre).astype(BF16), wout[...])
    out_ref[...] = (own.astype(F32) + normed(raw, gain_ref[...], bias_ref[1:2, :], 1)).astype(BF16)


def node_network(lon, bases, aggregate, biases, gain, pieces):
    rows, width = aggregate.shape[1:]
    kernel = functools.partial(node_kernel, len(bases) == 1)
    scratch = [pltpu.VMEM((rows, width), BF16), pltpu.VMEM((2 * width, width), BF16), pltpu.VMEM((width, width), BF16)]
    return call(
        kernel, jax.ShapeDtypeStruct((rows, width), BF16), 8 + len(bases), 6 * rows * width * width, scratch, 1
    )(lon, *bases, aggregate, biases, gain[None, :], *pieces)


def pick_kernel(index_ref, table_ref, out_ref):
    lane = lax.broadcasted_iota(I32, (index_ref.shape[0], table_ref.shape[0]), 1)
    pick = jnp.where(lane == index_ref[...], 1.0, 0.0).astype(BF16)
    out_ref[...] = dot(pick, table_ref[...]).astype(BF16)


def near_kernel(lon_ref, edge_ref, mid_ref, sender_ref, receiver_ref, bias_ref, w0, w1, w2, w3, out_ref, win):
    width = mid_ref.shape[1]
    quarter = w0.shape[1]
    lon = lon_ref[0]
    biases = []
    for j, w in enumerate((w0, w1, w2, w3)):
        win[:, j * quarter : (j + 1) * quarter] = w[0 : 3 * width, :]
        at = pl.ds(pl.multiple_of((lon ^ j) * quarter, quarter), quarter)
        biases.append(bias_ref[0:1, at])
    bias = jnp.concatenate(biases, 1)
    rows = mid_ref.shape[0]
    sent = dot(mid_ref[...], win[width : 2 * width, :]).astype(BF16)
    got = dot(mid_ref[...], win[2 * width :, :]).astype(BF16)
    edges = edge_ref.shape[0]
    block = 256

    @pl.loop(0, edges // block)
    def _(i):
        at = pl.ds(pl.multiple_of(i * block, block), block)
        lane = lax.broadcasted_iota(I32, (block, rows), 1)
        pick_s = jnp.where(lane == sender_ref[at, :], 1.0, 0.0).astype(BF16)
        pick_r = jnp.where(lane == receiver_ref[at, :], 1.0, 0.0).astype(BF16)
        out_ref[at, :] = dot(edge_ref[at, :], win[0:width, :]) + dot(pick_s, sent) + dot(pick_r, got) + bias


def far_kernel(pre_ref, edge_ref, halo_ref, sender_ref, receiver_ref, bias_ref, gain_ref, w0, w1, w2, w3, new_ref, sum_ref, total, win, wout):
    width = halo_ref.shape[1]
    quarter = w0.shape[1]
    for j, w in enumerate((w0, w1, w2, w3)):
        win[:, j * quarter : (j + 1) * quarter] = w[width : 2 * width, :]
        wout[:, j * quarter : (j + 1) * quarter] = w[3 * width : 4 * width, :]
    rows = halo_ref.shape[0]
    mesh_rows = sum_ref.shape[0]
    sent = dot(halo_ref[...], win[...]).astype(BF16)
    edges = edge_ref.shape[0]
    block = 256
    total[...] = jnp.zeros_like(total)

    @pl.loop(0, edges // block)
    def _(i):
        at = pl.ds(pl.multiple_of(i * block, block), block)
        lane = lax.broadcasted_iota(I32, (block, rows), 1) + mesh_rows
        pick = jnp.where(lane == sender_ref[at, :], 1.0, 0.0).astype(BF16)
        hidden = silu(pre_ref[at, :] + dot(pick, sent)).astype(BF16)
        raw = dot(hidden, wout[...], 1, 1)
        new = (edge_ref[at, :].astype(F32) + normed(raw, gain_ref[...], bias_ref[1:2, :], 1)).astype(BF16)
        new_ref[at, :] = new
        node = lax.broadcasted_iota(I32, (mesh_rows, block), 0)
        onto = jnp.where(node == receiver_ref[:, at], 1.0, 0.0).astype(BF16)
        total[...] += dot(onto, new)

    sum_ref[...] = total[...].astype(BF16)


def take(values, index, axis):
    return lax.dynamic_index_in_dim(values, index, axis, keepdims=False)


def plus(*values):
    total = values[0].astype(F32)
    for v in values[1:]:
        total = total + v.astype(F32)
    return total.astype(BF16)


def local(
    grid_latent,
    grid_feat,
    grid_sender,
    grid_owner,
    grid_node,
    mesh_latent,
    mesh_edge,
    halo_send,
    mesh_sender,
    mesh_receiver,
    enc_edge_in,
    enc_feat_proj,
    enc_edge_out,
    enc_edge_bias,
    enc_edge_gain,
    enc_node_in,
    enc_node_out,
    enc_node_bias,
    enc_node_gain,
    proc_edge_in,
    proc_edge_out,
    proc_edge_bias,
    proc_edge_gain,
    proc_node_in,
    proc_node_out,
    proc_node_bias,
    proc_node_gain,
):
    lat_count = lax.axis_size("lat")
    lat = lax.axis_index("lat")
    lon = lax.axis_index("lon")
    core, side = lon % 2, lon // 2
    low = lat % 2
    lon1 = lon.astype(I32)[None]
    width = grid_latent.shape[1]
    quarter = mesh_latent.shape[1]
    mesh_rows = mesh_latent.shape[0]
    node_rows = mesh_rows // 4
    edges = grid_sender.shape[0]

    def hop(values, axis, flip):
        size = lax.axis_size(axis)
        return lax.ppermute(values, axis, [(i, i ^ flip) for i in range(size)])

    def spread(shard):
        across = hop(shard, "lon", 2)
        return (shard, hop(shard, "lon", 1), across, hop(across, "lon", 1))

    def lie(weight):
        return jnp.concatenate([weight[:, m * quarter : (m + 1) * quarter] for m in range(weight.shape[1] // quarter)], 0)

    enc_pieces = spread(jnp.concatenate([enc_edge_in, enc_edge_out], 0))
    node_pieces = spread(jnp.concatenate([enc_node_in, lie(enc_node_out)], 0))
    edge_pieces = spread(jnp.concatenate([proc_edge_in, proc_edge_out], 0))
    last_pieces = spread(jnp.concatenate([proc_node_in, lie(proc_node_out)], 0))

    def own_rows(flip):
        rows = lax.dynamic_slice_in_dim(mesh_latent, (lon ^ flip) * node_rows, node_rows, 0)
        return rows if flip == 0 else hop(rows, "lon", flip)

    base_pieces = tuple(own_rows(flip) for flip in range(4))

    keys, senders, feats, starts = call(
        functools.partial(sort_kernel, lat_count, mesh_rows),
        [
            jax.ShapeDtypeStruct((1, edges), I32),
            jax.ShapeDtypeStruct((1, edges), I32),
            jax.ShapeDtypeStruct((META, edges), BF16),
            jax.ShapeDtypeStruct((lat_count, 128), I32),
        ],
        4,
        2 * META * edges * edges * 8,
        n_out=4,
    )(grid_owner.reshape(1, edges), grid_sender[None, :], grid_node[None, :], grid_feat)
    starts = starts[:, 0]
    keys = keys.reshape(edges // CHUNK, 1, CHUNK)
    enc_norm = jnp.concatenate(
        [enc_edge_gain[None, :], enc_edge_bias[1:2], jnp.zeros((6, width), F32)], 0
    )
    messages = call(
        functools.partial(message_kernel, grid_feat.shape[0]),
        jax.ShapeDtypeStruct((edges // CHUNK, width, CHUNK), BF16),
        11,
        4 * edges * width * width,
        [pltpu.VMEM((width, width), BF16), pltpu.VMEM((width, width), BF16), pltpu.VMEM((META, width), BF16)],
        1,
    )(lon1, grid_latent, senders, feats, enc_feat_proj, enc_edge_bias, enc_norm, *enc_pieces)

    away = node_sums(starts, (1 - core).astype(I32)[None], keys, messages, lat_count, mesh_rows, edges)
    came = hop(away, "lon", 1)
    kept = node_sums(starts, core.astype(I32)[None], keys, messages, lat_count, mesh_rows, edges)
    tall = lat_count // 2
    shape = (tall, 2, 2, node_rows, width)
    came, kept = came.reshape(shape), kept.reshape(shape)
    half = node_rows // 2

    def cut(rows, low_at=None, side_at=None):
        def of(v):
            v = v[:, :, :, rows]
            return take(v, side_at, 2) if low_at is None else take(v, low_at, 1)

        return plus(of(kept), of(came))

    first, second = slice(0, half), slice(half, node_rows)
    got_x = hop(cut(first, side_at=1 - side), "lon", 2)
    got_y = hop(cut(second, low_at=1 - low), "lat", 1)
    sum_x = plus(cut(first, side_at=side), got_x)
    got_xy = hop(take(sum_x, 1 - low, 1), "lat", 1)
    sum_y = plus(cut(second, low_at=low), got_y)
    got_yx = hop(take(sum_y, 1 - side, 1), "lon", 2)
    summed = jnp.concatenate([plus(take(sum_x, low, 1), got_xy), plus(take(sum_y, side, 1), got_yx)], 1)
    groups = [[2 * i + b for i in range(tall)] for b in range(2)]
    partial = lax.all_to_all(summed, "lat", 0, 0, axis_index_groups=groups, tiled=True)

    mid = node_network(lon1, base_pieces, partial, enc_node_bias, enc_node_gain, node_pieces)
    mid_all = lax.all_gather(mid, "lon", axis=0, tiled=True)

    listed = halo_send.size
    halo_cap = halo_send.shape[1]
    outgoing = call(
        pick_kernel, jax.ShapeDtypeStruct((listed, width), BF16), 2, 2 * listed * mesh_rows * width
    )(halo_send.reshape(listed, 1), mid_all)
    received = lax.all_to_all(outgoing.reshape(lat_count, halo_cap, width), "lat", 0, 0, tiled=True).reshape(listed, width)

    local_edges = mesh_edge.shape[0]
    sender_col = mesh_sender.reshape(local_edges, 1)
    receiver_col = mesh_receiver.reshape(local_edges, 1)
    near = call(
        near_kernel,
        jax.ShapeDtypeStruct((local_edges, width), F32),
        10,
        2 * local_edges * width * (width + 2 * mesh_rows),
        [pltpu.VMEM((3 * width, width), BF16)],
        1,
    )(lon1, mesh_edge, mid_all, sender_col, receiver_col, proc_edge_bias, *edge_pieces)
    edge_update, incoming = call(
        far_kernel,
        [jax.ShapeDtypeStruct((local_edges, width), BF16), jax.ShapeDtypeStruct((mesh_rows, width), BF16)],
        11,
        2 * local_edges * width * (width + listed + mesh_rows),
        [pltpu.VMEM((mesh_rows, width), F32), pltpu.VMEM((width, width), BF16), pltpu.VMEM((width, width), BF16)],
        n_out=2,
    )(near, mesh_edge, received, sender_col, mesh_receiver[None, :], proc_edge_bias, proc_edge_gain[None, :], *edge_pieces)

    incoming = incoming.reshape(2, 2, node_rows, width)
    came = hop(take(incoming, 1 - core, 1), "lon", 1)
    mine = take(incoming, core, 1)
    got = hop(plus(take(mine, 1 - side, 0), take(came, 1 - side, 0)), "lon", 2)
    parts = jnp.stack([take(mine, side, 0), take(came, side, 0), got], 0)
    new = node_network(lon1, (mid,), parts, proc_node_bias, proc_node_gain, last_pieces)
    spread_out = jnp.stack([new[:, m * quarter : (m + 1) * quarter] for m in range(4)], 0)
    mesh_update = lax.all_to_all(spread_out, "lon", 0, 0, tiled=True).reshape(mesh_rows, quarter)
    return (mesh_update, edge_update)


def solution(mesh):
    both = ("lat", "lon")
    placed = (
        P(both, None),
        P(None, both),
        P(both),
        P(both, None),
        P(both),
        P("lat", "lon"),
        P(both, None),
        P("lat", None),
        P(both),
        P(both),
        P(None, "lon"),
        P(),
        P(None, "lon"),
        P(),
        P(),
        P(None, "lon"),
        P("lon", None),
        P(),
        P(),
        P(None, "lon"),
        P(None, "lon"),
        P(),
        P(),
        P(None, "lon"),
        P("lon", None),
        P(),
        P(),
    )
    return jax.shard_map(
        local,
        mesh=mesh,
        in_specs=placed,
        out_specs=(P("lat", "lon"), P(both, None)),
        check_vma=False,
    )
```

time: 418 us -> 153 us (0.37)
  waiting for transfers between devices: 196 us -> 31.5 us
  Pallas kernels: 0 us -> 55 us
  local copies, waits for them, and re-layouts: 66.1 us -> 18.7 us
  other arithmetic: 50.8 us -> 4.16 us
  matrix products: 33.5 us -> 0 us
  blocking collectives: 32.3 us -> 15.3 us
  between operations: 14.2 us -> 1.14 us
    psum x4 -> x0, waiting for transfers between devices: 124 us -> none  [the longest x2 63 us: node_network(): lax.psum(jnp.dot(hidden, weight_out, preferred_element_type=jnp.float32)....]
    all_to_all x4 -> x2, waiting for transfers between devices: 70.7 us -> 7.49 us  [the longest x1 4.33 us: local(): lax.all_to_all(summed, 'lat', 0, 0, axis_index_groups=groups, tiled=True)]
    pallas_call x0 -> x9, Pallas kernels: none -> 55 us  [the longest x2 13.9 us: node_sums(): pl.pallas_call(functools.partial(sums_kernel, mesh_rows, edges), out_shap...]
    scatter x3 -> x0, local copies, waits for them, and re-layouts: 36.1 us -> none  [the longest x1 21.3 us: local(): row_buffer = jnp.zeros((slot_total, feature_width), jnp.bfloat16).at[slot...]
    dot_general x8 -> x0, matrix products: 33.5 us -> none  [the longest x1 8.92 us: encoder_edges(): lax.dot_general(hidden, piece_out, (((1,), (1,)), ((), ())), preferred_el...]
    scatter-add x1 -> x0, other arithmetic: 27.6 us -> none  [local(): jax.ops.segment_sum(arrived, segment_ids, num_segments=mesh_rows + 1)]
    ppermute x0 -> x22, waiting for transfers between devices: none -> 24 us  [hop(): return lax.ppermute(values, axis, [(i, i ^ flip) for i in range(size)])]
    all_gather x4 -> x1, blocking collectives: 32.3 us -> 8.3 us  [local(): mid_all = lax.all_gather(mid, 'lon', axis=0, tiled=True)]
  transfers between devices with their start and end apart: 9 -> 24, of which waited for: 6 -> 9; matrix products, arithmetic and copies ran while one was open for 13% -> 7% of each run, Pallas kernels for 0% -> 21%
where the time goes in v1:
time: 153 us; the launch traced here: 152 us
  Pallas kernels  55 us (36%)
  waiting for transfers between devices  31.5 us (21%)
  starting transfers between devices  26.4 us (17%)
  local copies, waits for them, and re-layouts  18.7 us (12%)
  blocking collectives  15.3 us (10%)
  other arithmetic  4.16 us (3%)
    ppermute x22, waiting for transfers between devices, hop(): return lax.ppermute(values, axis, [(i, i ^ flip) for i in range(size)])  24 us
    ppermute x22, starting transfers between devices, hop(): return lax.ppermute(values, axis, [(i, i ^ flip) for i in range(size)])  17.1 us
    pallas_call x2, Pallas kernels, node_sums(): pl.pallas_call(functools.partial(sums_kernel, mesh_rows, edges), out_shap...  13.9 us
    pallas_call x1, Pallas kernels, local(): call(functools.partial(message_kernel, grid_feat.shape[0]), jax.ShapeDtyp...  11.9 us
    pallas_call x1, Pallas kernels, local(): call(far_kernel, [jax.ShapeDtypeStruct((local_edges, width), BF16), jax.S...  8.79 us
    all_gather x1, blocking collectives, local(): mid_all = lax.all_gather(mid, 'lon', axis=0, tiled=True)  8.3 us
    unnamed x79, local copies, waits for them, and re-layouts  8.22 us
    pallas_call x1, Pallas kernels, local(): call(near_kernel, jax.ShapeDtypeStruct((local_edges, width), F32), 10, 2...  7.13 us
  transfers between devices with their start and end apart: 24, of which 9 were waited for; matrix products, arithmetic and copies ran while one was open for 7% of the time, Pallas kernels for 21%

profile of v1, /device:TPU:0, one launch (start us, length us, event | category | flops | bytes accessed | tf_op | source)
XLA Modules:
  0.0 152.2 jit_solution(9814989888749171317)
XLA Ops:
  2.5 3.0 %collective-permute-start.4 = (bf16[1024,128]{1,0:T(8,128)(2,1)S(1)}, bf16[1024,128]{1,0:T(8,128)(2,1)S(1)}, u32[]{:S(2)}, u32[]{:S(2)}) collective-permute-start(bf16[1024,128]{1,0:T(8,128)(2,1)S(1)} %constant_dynamic-update-slice_fusion.w0), channel_id=1, source_target_pairs={{0,2},{1,3},{2,0},{3,1},{4,6},{5,7},{6,4},{7,5},{8,10},{9,11},{10,... | collective-permute-start | bytes 786440 | tf_op jit(solution)/shard_map/ppermute | solution.py:308
  5.6 4.7 %shard_map.266 = (s32[1,2048]{1,0:T(1,128)}, s32[1,2048]{1,0:T(1,128)}, bf16[16,2048]{1,0:T(8,128)(2,1)}, s32[8,128]{1,0:T(8,128)}) custom-call(s32[1,2048]{1,0:T(1,128)} %bitcast.80, s32[1,2048]{1,0:T(1,128)} %bitcast.81, s32[1,2048]{1,0:T(1,128)} %bitcast.82, bf16[4,2048]{1,0:T(4,128)(2,1)} %feat_ref.1), custom_call_target="tpu_custom_call" | custom-call | flops 1073741824 | bytes 4194304 | tf_op jit(solution)/shard_map/pallas_call | solution.py:328
  10.3 1.6 %collective-permute-done.4.w2 = bf16[1024,128]{1,0:T(8,128)(2,1)S(1)} collective-permute-done((bf16[1024,128]{1,0:T(8,128)(2,1)S(1)}, bf16[1024,128]{1,0:T(8,128)(2,1)S(1)}, u32[]{:S(2)}, u32[]{:S(2)}) %collective-permute-start.4) | collective-permute-done | bytes 262176 | tf_op jit(solution)/shard_map/ppermute | solution.py:308
  14.2 11.9 %shard_map.267.msg_ref = bf16[8,512,256]{2,1,0:T(8,128)(2,1)} custom-call(s32[1]{0:T(128)} %bitcast.lon_ref, bf16[512,512]{1,0:T(8,128)(2,1)} %rows_ref.1, s32[1,2048]{1,0:T(1,128)} %get-tuple-element.10.send_ref, bf16[16,2048]{1,0:T(8,128)(2,1)} %get-tuple-element.11.feats_ref, bf16[4,512]{1,0:T(4,128)(2,1)} %proj_ref.1, f32[2,512]{1,0:T(2,128)} %bias_ref.3, ...), custom_call_target="tpu_custom_call" | custom-call | flops 2147483648 | bytes 4194304 | tf_op jit(solution)/shard_map/pallas_call | solution.py:345
  26.1 1.6 %copy-done = bf16[8,512,256]{2,1,0:T(8,128)(2,1)S(1)} copy-done((bf16[8,512,256]{2,1,0:T(8,128)(2,1)S(1)}, bf16[8,512,256]{2,1,0:T(8,128)(2,1)}, u32[]{:S(2)}) %copy-start) | copy-done | bytes 2097176
  27.7 7.5 %shard_map.269 = bf16[8,2,128,512]{3,2,1,0:T(8,128)(2,1)} custom-call(s32[8]{0:T(128)S(1)} %slice_reduce_fusion.start_ref, s32[1]{0:T(128)} %bitcast.8.core_ref, s32[8,1,256]{2,1,0:T(1,128)S(1)} %bitcast.64, bf16[8,512,256]{2,1,0:T(8,128)(2,1)S(1)} %copy-done), custom_call_target="tpu_custom_call" | custom-call | flops 1073741824 | bytes 8388608 | tf_op jit(solution)/shard_map/pallas_call | solution.py:145
  35.6 6.3 %shard_map.268 = bf16[8,2,128,512]{3,2,1,0:T(8,128)(2,1)S(1)} custom-call(s32[8]{0:T(128)S(1)} %slice_reduce_fusion.start_ref, s32[1]{0:T(128)} %bitcast.4.core_ref, s32[8,1,256]{2,1,0:T(1,128)S(1)} %bitcast.65, bf16[8,512,256]{2,1,0:T(8,128)(2,1)S(1)} %copy-done.1), custom_call_target="tpu_custom_call" | custom-call | flops 1073741824 | bytes 8388608 | tf_op jit(solution)/shard_map/pallas_call | solution.py:145
  42.1 1.7 %fusion.10 = (bf16[4,2,2,64,512]{4,3,2,1,0:T(8,128)(2,1)S(1)}, bf16[4,2,2,64,512]{4,3,2,1,0:T(8,128)(2,1)S(1)}) fusion(bf16[4,2,2,128,512]{4,3,2,1,0:T(8,128)(2,1)} %bitcast.9), kind=kLoop, calls=%fused_computation.59 | loop fusion | bytes 4194304 | tf_op jit(solution)/shard_map/slice | solution.py:364
  44.2 1.6 %collective-permute-start.7 = (bf16[4,2,64,512]{3,2,0,1:T(8,128)(2,1)S(1)}, bf16[4,2,64,512]{3,2,0,1:T(8,128)(2,1)S(1)}, u32[]{:S(2)}, u32[]{:S(2)}) collective-permute-start(bf16[4,2,64,512]{3,2,0,1:T(8,128)(2,1)S(1)} %fusion.3), channel_id=1, source_target_pairs={{0,2},{1,3},{2,0},{3,1},{4,6},{5,7},{6,4},{7,5},{8,10},{9,11},{10,... | collective-permute-start | bytes 1572872 | tf_op jit(solution)/shard_map/ppermute | solution.py:308
  46.1 1.8 %collective-permute-start.9 = (bf16[4,2,64,512]{3,2,0,1:T(8,128)(2,1)S(1)}, bf16[4,2,64,512]{3,2,0,1:T(8,128)(2,1)S(1)}, u32[]{:S(2)}, u32[]{:S(2)}) collective-permute-start(bf16[4,2,64,512]{3,2,0,1:T(8,128)(2,1)S(1)} %fusion.5), channel_id=1, source_target_pairs={{0,4},{4,0},{8,12},{12,8},{16,20},{20,16},{24,28},{28,24},{1,5},{5... | collective-permute-start | bytes 1572872 | tf_op jit(solution)/shard_map/ppermute | solution.py:308
  48.0 10.3 %collective-permute-done.7 = bf16[4,2,64,512]{3,2,0,1:T(8,128)(2,1)S(1)} collective-permute-done((bf16[4,2,64,512]{3,2,0,1:T(8,128)(2,1)S(1)}, bf16[4,2,64,512]{3,2,0,1:T(8,128)(2,1)S(1)}, u32[]{:S(2)}, u32[]{:S(2)}) %collective-permute-start.7) | collective-permute-done | bytes 524320 | tf_op jit(solution)/shard_map/ppermute | solution.py:308
  58.6 1.6 %collective-permute-start.8 = (bf16[4,64,512]{2,1,0:T(8,128)(2,1)S(1)}, bf16[4,64,512]{2,1,0:T(8,128)(2,1)S(1)}, u32[]{:S(2)}, u32[]{:S(2)}) collective-permute-start(bf16[4,64,512]{2,1,0:T(8,128)(2,1)S(1)} %dynamic-slice_bitcast_fusion.2), channel_id=1, source_target_pairs={{0,4},{4,0},{8,12},{12,8},{16,20},{20,16},{24,28},{28,24},{1,5},{5... | collective-permute-start | bytes 786440 | tf_op jit(solution)/shard_map/ppermute | solution.py:308
  60.5 1.6 %collective-permute-start.10 = (bf16[4,64,512]{2,1,0:T(8,128)(2,1)S(1)}, bf16[4,64,512]{2,1,0:T(8,128)(2,1)S(1)}, u32[]{:S(2)}, u32[]{:S(2)}) collective-permute-start(bf16[4,64,512]{2,1,0:T(8,128)(2,1)S(1)} %dynamic-slice_bitcast_fusion.1), channel_id=1, source_target_pairs={{0,2},{1,3},{2,0},{3,1},{4,6},{5,7},{6,4},{7,5},{8,10},{9,11},{10,... | collective-permute-start | bytes 786440 | tf_op jit(solution)/shard_map/ppermute | solution.py:308
  62.6 3.6 %collective-permute-done.8 = bf16[4,64,512]{2,1,0:T(8,128)(2,1)S(1)} collective-permute-done((bf16[4,64,512]{2,1,0:T(8,128)(2,1)S(1)}, bf16[4,64,512]{2,1,0:T(8,128)(2,1)S(1)}, u32[]{:S(2)}, u32[]{:S(2)}) %collective-permute-start.8) | collective-permute-done | bytes 262176 | tf_op jit(solution)/shard_map/ppermute | solution.py:308
  66.3 3.4 %collective-permute-done.10 = bf16[4,64,512]{2,1,0:T(8,128)(2,1)S(1)} collective-permute-done((bf16[4,64,512]{2,1,0:T(8,128)(2,1)S(1)}, bf16[4,64,512]{2,1,0:T(8,128)(2,1)S(1)}, u32[]{:S(2)}, u32[]{:S(2)}) %collective-permute-start.10) | collective-permute-done | bytes 262176 | tf_op jit(solution)/shard_map/ppermute | solution.py:308
  70.6 4.9 %all-to-all-start = ((bf16[4,128,512]{2,1,0:T(8,128)(2,1)}), bf16[4,128,512]{2,1,0:T(8,128)(2,1)S(1)}, u32[]{:S(2)}, u32[]{:S(2)}) async-start(bf16[4,128,512]{2,1,0:T(8,128)(2,1)} %pad_maximum_fusion), calls=%async_computation | async-start | bytes 1048576 | tf_op jit(solution)/shard_map/all_to_all | solution.py:378
  76.6 1.5 collective-permute-start.1
  78.9 1.6 %collective-permute-start.15 = (bf16[2048,128]{1,0:T(8,128)(2,1)S(1)}, bf16[2048,128]{1,0:T(8,128)(2,1)S(1)}, u32[]{:S(2)}, u32[]{:S(2)}) collective-permute-start(bf16[2048,128]{1,0:T(8,128)(2,1)S(1)} %constant_dynamic-update-slice_fusion.3.w0), channel_id=1, source_target_pairs={{0,2},{1,3},{2,0},{3,1},{4,6},{5,7},{6,4},{7,5},{8,10},{9,11},{10,... | collective-permute-start | bytes 1572872 | tf_op jit(solution)/shard_map/ppermute | solution.py:308
  81.7 4.3 %all-to-all-done.refs_4_ = bf16[4,128,512]{2,1,0:T(8,128)(2,1)S(1)} async-done(((bf16[4,128,512]{2,1,0:T(8,128)(2,1)}), bf16[4,128,512]{2,1,0:T(8,128)(2,1)S(1)}, u32[]{:S(2)}, u32[]{:S(2)}) %all-to-all-start) | async-done | bytes 524320 | tf_op jit(solution)/shard_map/all_to_all | solution.py:378
  86.9 3.2 %shard_map.270.refs_0_ = bf16[128,512]{1,0:T(8,128)(2,1)} custom-call(s32[1]{0:T(128)} %bitcast.lon_ref, bf16[128,128]{1,0:T(8,128)(2,1)} %get-tuple-element.32.refs_0_, bf16[128,128]{1,0:T(8,128)(2,1)} %copy-done.23, bf16[128,128]{1,0:T(8,128)(2,1)} %copy-done.24, bf16[128,128]{1,0:T(8,128)(2,1)} %copy-done.25, bf16[4,128,512]{2,1,0:T(8,128)(2,1)} %copy-done.8, ...), custom_call_target="tpu_custom_call" | custom-call | flops 201326592 | bytes 4194304 | tf_op jit(solution)/shard_map/pallas_call | solution.py:189
  90.0 8.3 %all_gather.3.mid_ref.table_ref = bf16[512,512]{1,0:T(8,128)(2,1)} all-gather(bf16[128,512]{1,0:T(8,128)(2,1)} %shard_map.270.refs_0_), channel_id=1, replica_groups=mesh['lat'=8,'lon'=4] {'lon'}, dimensions={0}, use_global_device_ids=true | all-gather | bytes 655360 | tf_op jit(solution)/shard_map/all_gather | solution.py:381
  98.3 2.4 %shard_map.272 = bf16[512,512]{1,0:T(8,128)(2,1)} custom-call(s32[512,1]{1,0:T(8,128)} %reshape.85.index_ref, bf16[512,512]{1,0:T(8,128)(2,1)} %all_gather.3.mid_ref.table_ref), custom_call_target="tpu_custom_call" | custom-call | flops 268435456 | bytes 4194304 | tf_op jit(solution)/shard_map/pallas_call | solution.py:385
  100.7 4.4 %all-to-all-start.1 = ((bf16[8,64,512]{2,1,0:T(8,128)(2,1)}), bf16[8,64,512]{2,1,0:T(8,128)(2,1)S(1)}, u32[]{:S(2)}, u32[]{:S(2)}) async-start(bf16[8,64,512]{2,1,0:T(8,128)(2,1)} %bitcast.67), calls=%async_computation.1 | async-start | bytes 1048576 | tf_op jit(solution)/shard_map/all_to_all | solution.py:388
  106.2 1.0 copy.36.sender_ref
  107.3 1.0 copy.37.receiver_ref
  109.9 7.1 %shard_map.271.pre_ref = f32[1024,512]{1,0:T(8,128)} custom-call(s32[1]{0:T(128)} %bitcast.lon_ref, bf16[1024,512]{1,0:T(8,128)(2,1)} %edge_ref.3, bf16[512,512]{1,0:T(8,128)(2,1)} %all_gather.3.mid_ref.table_ref, s32[1024,1]{1,0:T(8,128)} %copy.36.sender_ref, s32[1024,1]{1,0:T(8,128)} %copy.37.receiver_ref, f32[2,512]{1,0:T(2,128)} %bias_ref.5, ...), custom_call_target="tpu_custom_call" | custom-call | flops 1610612736 | bytes 4194304 | tf_op jit(solution)/shard_map/pallas_call | solution.py:393
  117.0 3.2 %all-to-all-done.1 = bf16[8,64,512]{2,1,0:T(8,128)(2,1)S(1)} async-done(((bf16[8,64,512]{2,1,0:T(8,128)(2,1)}), bf16[8,64,512]{2,1,0:T(8,128)(2,1)S(1)}, u32[]{:S(2)}, u32[]{:S(2)}) %all-to-all-start.1) | async-done | bytes 524320 | tf_op jit(solution)/shard_map/all_to_all | solution.py:388
  121.0 8.8 %shard_map.273 = (bf16[1024,512]{1,0:T(8,128)(2,1)}, bf16[512,512]{1,0:T(8,128)(2,1)}) custom-call(f32[1024,512]{1,0:T(8,128)} %shard_map.271.pre_ref, bf16[1024,512]{1,0:T(8,128)(2,1)} %edge_ref.3, bf16[512,512]{1,0:T(8,128)(2,1)} %bitcast.66, s32[1024,1]{1,0:T(8,128)} %copy.36.sender_ref, s32[1,1024]{1,0:T(1,128)} %bitcast.73, f32[2,512]{1,0:T(2,128)} %bias_ref.5, ...), custom_call_target="tpu_custom_call" | custom-call | flops 1610612736 | bytes 4194304 | tf_op jit(solution)/shard_map/pallas_call | solution.py:401
  129.8 1.0 dynamic-slice_bitcast_fusion
  135.0 3.9 %collective-permute-done.18 = bf16[128,512]{1,0:T(8,128)(2,1)S(1)} collective-permute-done((bf16[128,512]{1,0:T(8,128)(2,1)S(1)}, bf16[128,512]{1,0:T(8,128)(2,1)S(1)}, u32[]{:S(2)}, u32[]{:S(2)}) %collective-permute-start.18) | collective-permute-done | bytes 131104 | tf_op jit(solution)/shard_map/ppermute | solution.py:308
  140.6 3.1 %shard_map.274 = bf16[128,512]{1,0:T(8,128)(2,1)} custom-call(s32[1]{0:T(128)} %bitcast.lon_ref, bf16[128,512]{1,0:T(8,128)(2,1)} %shard_map.270.refs_0_, bf16[3,128,512]{2,1,0:T(8,128)(2,1)} %pad_maximum_fusion.1.refs_1_, f32[2,512]{1,0:T(2,128)} %refs_2_.1, f32[1,512]{1,0:T(1,128)} %bitcast.79, bf16[1536,128]{1,0:T(8,128)(2,1)} %copy-done.9, ...), custom_call_target="tpu_custom_call" | custom-call | flops 201326592 | bytes 4194304 | tf_op jit(solution)/shard_map/pallas_call | solution.py:189
  144.5 7.0 %all_to_all.15 = bf16[4,128,128]{2,1,0:T(8,128)(2,1)S(1)} all-to-all(bf16[4,128,128]{2,1,0:T(8,128)(2,1)S(1)} %pad_maximum_fusion.2), channel_id=1, replica_groups=mesh['lat'=8,'lon'=4] {'lon'}, dimensions={0} | all-to-all | bytes 262144 | tf_op jit(solution)/shard_map/all_to_all | solution.py:417
  (139 shorter events, 22.2 us)
Async XLA Ops:
  2.5 9.3 %collective-permute-start.4 = (bf16[1024,128]{1,0:T(8,128)(2,1)S(1)}, bf16[1024,128]{1,0:T(8,128)(2,1)S(1)}, u32[]{:S(2)}, u32[]{:S(2)}) collective-permute-start(bf16[1024,128]{1,0:T(8,128)(2,1)S(1)} %constant_dynamic-update-slice_fusion.w0), channel_id=1, source_target_pairs={{0,2},{1,3},{2,0},{3,1},{4,6},{5,7},{6,4},{7,5},{8,10},{9,11},{10,... | collective-permute-start | bytes 786440 | tf_op jit(solution)/shard_map/ppermute | solution.py:308
  5.5 7.9 %collective-permute-start.3 = (bf16[1024,128]{1,0:T(8,128)(2,1)S(1)}, bf16[1024,128]{1,0:T(8,128)(2,1)S(1)}, u32[]{:S(2)}, u32[]{:S(2)}) collective-permute-start(bf16[1024,128]{1,0:T(8,128)(2,1)S(1)} %constant_dynamic-update-slice_fusion.w0), channel_id=1, source_target_pairs={{0,1},{1,0},{2,3},{3,2},{4,5},{5,4},{6,7},{7,6},{8,9},{9,8},{10,11... | collective-permute-start | bytes 786440 | tf_op jit(solution)/shard_map/ppermute | solution.py:308
  11.9 1.6 %collective-permute-start.5 = (bf16[1024,128]{1,0:T(8,128)(2,1)S(1)}, bf16[1024,128]{1,0:T(8,128)(2,1)S(1)}, u32[]{:S(2)}, u32[]{:S(2)}) collective-permute-start(bf16[1024,128]{1,0:T(8,128)(2,1)S(1)} %collective-permute-done.4.w2), channel_id=1, source_target_pairs={{0,1},{1,0},{2,3},{3,2},{4,5},{5,4},{6,7},{7,6},{8,9},{9,8},{10,11... | collective-permute-start | bytes 786440 | tf_op jit(solution)/shard_map/ppermute | solution.py:308
  35.2 6.9 %collective-permute-start.6 = (bf16[8,2,128,512]{3,2,1,0:T(8,128)(2,1)}, bf16[8,2,128,512]{3,2,1,0:T(8,128)(2,1)}, u32[]{:S(2)}, u32[]{:S(2)}) collective-permute-start(bf16[8,2,128,512]{3,2,1,0:T(8,128)(2,1)} %shard_map.269), channel_id=1, source_target_pairs={{0,1},{1,0},{2,3},{3,2},{4,5},{5,4},{6,7},{7,6},{8,9},{9,8},{10,11... | collective-permute-start | bytes 6291464 | tf_op jit(solution)/shard_map/ppermute | solution.py:308
  44.2 14.1 %collective-permute-start.7 = (bf16[4,2,64,512]{3,2,0,1:T(8,128)(2,1)S(1)}, bf16[4,2,64,512]{3,2,0,1:T(8,128)(2,1)S(1)}, u32[]{:S(2)}, u32[]{:S(2)}) collective-permute-start(bf16[4,2,64,512]{3,2,0,1:T(8,128)(2,1)S(1)} %fusion.3), channel_id=1, source_target_pairs={{0,2},{1,3},{2,0},{3,1},{4,6},{5,7},{6,4},{7,5},{8,10},{9,11},{10,... | collective-permute-start | bytes 1572872 | tf_op jit(solution)/shard_map/ppermute | solution.py:308
  46.1 14.0 %collective-permute-start.9 = (bf16[4,2,64,512]{3,2,0,1:T(8,128)(2,1)S(1)}, bf16[4,2,64,512]{3,2,0,1:T(8,128)(2,1)S(1)}, u32[]{:S(2)}, u32[]{:S(2)}) collective-permute-start(bf16[4,2,64,512]{3,2,0,1:T(8,128)(2,1)S(1)} %fusion.5), channel_id=1, source_target_pairs={{0,4},{4,0},{8,12},{12,8},{16,20},{20,16},{24,28},{28,24},{1,5},{5... | collective-permute-start | bytes 1572872 | tf_op jit(solution)/shard_map/ppermute | solution.py:308
  58.6 7.7 %collective-permute-start.8 = (bf16[4,64,512]{2,1,0:T(8,128)(2,1)S(1)}, bf16[4,64,512]{2,1,0:T(8,128)(2,1)S(1)}, u32[]{:S(2)}, u32[]{:S(2)}) collective-permute-start(bf16[4,64,512]{2,1,0:T(8,128)(2,1)S(1)} %dynamic-slice_bitcast_fusion.2), channel_id=1, source_target_pairs={{0,4},{4,0},{8,12},{12,8},{16,20},{20,16},{24,28},{28,24},{1,5},{5... | collective-permute-start | bytes 786440 | tf_op jit(solution)/shard_map/ppermute | solution.py:308
  60.4 15.1 %copy-start.19 = (bf16[512,128]{1,0:T(8,128)(2,1)S(1)}, bf16[512,128]{1,0:T(8,128)(2,1)}, u32[]{:S(2)}) copy-start(bf16[512,128]{1,0:T(8,128)(2,1)} %param.32) | copy-start | bytes 393220
  60.4 18.3 %copy-start.11 = (bf16[1536,128]{1,0:T(8,128)(2,1)S(1)}, bf16[1536,128]{1,0:T(8,128)(2,1)}, u32[]{:S(2)}) copy-start(bf16[1536,128]{1,0:T(8,128)(2,1)} %param.46) | copy-start | bytes 1179652
  60.5 9.2 %collective-permute-start.10 = (bf16[4,64,512]{2,1,0:T(8,128)(2,1)S(1)}, bf16[4,64,512]{2,1,0:T(8,128)(2,1)S(1)}, u32[]{:S(2)}, u32[]{:S(2)}) collective-permute-start(bf16[4,64,512]{2,1,0:T(8,128)(2,1)S(1)} %dynamic-slice_bitcast_fusion.1), channel_id=1, source_target_pairs={{0,2},{1,3},{2,0},{3,1},{4,6},{5,7},{6,4},{7,5},{8,10},{9,11},{10,... | collective-permute-start | bytes 786440 | tf_op jit(solution)/shard_map/ppermute | solution.py:308
  62.0 16.8 %copy-start.10 = (bf16[1536,128]{1,0:T(8,128)(2,1)}, bf16[1536,128]{1,0:T(8,128)(2,1)S(1)}, u32[]{:S(2)}) copy-start(bf16[1536,128]{1,0:T(8,128)(2,1)S(1)} %slice_dynamic-update-slice_fusion.4.refs_7_) | copy-start | bytes 1179652
  62.0 16.1 %collective-permute-start.12 = (bf16[1536,128]{1,0:T(8,128)(2,1)S(1)}, bf16[1536,128]{1,0:T(8,128)(2,1)S(1)}, u32[]{:S(2)}, u32[]{:S(2)}) collective-permute-start(bf16[1536,128]{1,0:T(8,128)(2,1)S(1)} %slice_dynamic-update-slice_fusion.4.refs_7_), channel_id=1, source_target_pairs={{0,2},{1,3},{2,0},{3,1},{4,6},{5,7},{6,4},{7,5},{8,10},{9,11},{10,... | collective-permute-start | bytes 1179656 | tf_op jit(solution)/shard_map/ppermute | solution.py:308
  70.6 15.4 %all-to-all-start = ((bf16[4,128,512]{2,1,0:T(8,128)(2,1)}), bf16[4,128,512]{2,1,0:T(8,128)(2,1)S(1)}, u32[]{:S(2)}, u32[]{:S(2)}) async-start(bf16[4,128,512]{2,1,0:T(8,128)(2,1)} %pad_maximum_fusion), calls=%async_computation | async-start | bytes 1048576 | tf_op jit(solution)/shard_map/all_to_all | solution.py:378
  75.5 6.2 %collective-permute-start.11 = (bf16[1536,128]{1,0:T(8,128)(2,1)S(1)}, bf16[1536,128]{1,0:T(8,128)(2,1)}, u32[]{:S(2)}, u32[]{:S(2)}) collective-permute-start(bf16[1536,128]{1,0:T(8,128)(2,1)S(1)} %slice_dynamic-update-slice_fusion.4.refs_7_), channel_id=1, source_target_pairs={{0,1},{1,0},{2,3},{3,2},{4,5},{5,4},{6,7},{7,6},{8,9},{9,8},{10,11... | collective-permute-start | bytes 1179656 | tf_op jit(solution)/shard_map/ppermute | solution.py:308
  76.1 2.7 %collective-permute-start = (bf16[128,128]{1,0:T(8,128)(2,1)S(1)}, bf16[128,128]{1,0:T(8,128)(2,1)S(1)}, u32[]{:S(2)}, u32[]{:S(2)}) collective-permute-start(bf16[128,128]{1,0:T(8,128)(2,1)S(1)} %get-tuple-element.31), channel_id=1, source_target_pairs={{0,1},{1,0},{2,3},{3,2},{4,5},{5,4},{6,7},{7,6},{8,9},{9,8},{10,11... | collective-permute-start | bytes 98312 | tf_op jit(solution)/shard_map/ppermute | solution.py:308
  76.6 4.8 %collective-permute-start.1 = (bf16[128,128]{1,0:T(8,128)(2,1)S(1)}, bf16[128,128]{1,0:T(8,128)(2,1)S(1)}, u32[]{:S(2)}, u32[]{:S(2)}) collective-permute-start(bf16[128,128]{1,0:T(8,128)(2,1)S(1)} %get-tuple-element.33), channel_id=1, source_target_pairs={{0,2},{1,3},{2,0},{3,1},{4,6},{5,7},{6,4},{7,5},{8,10},{9,11},{10,... | collective-permute-start | bytes 98312 | tf_op jit(solution)/shard_map/ppermute | solution.py:308
  78.1 3.6 %collective-permute-start.2 = (bf16[128,128]{1,0:T(8,128)(2,1)S(1)}, bf16[128,128]{1,0:T(8,128)(2,1)S(1)}, u32[]{:S(2)}, u32[]{:S(2)}) collective-permute-start(bf16[128,128]{1,0:T(8,128)(2,1)S(1)} %get-tuple-element.30), channel_id=1, source_target_pairs={{0,3},{1,2},{2,1},{3,0},{4,7},{5,6},{6,5},{7,4},{8,11},{9,10},{10,... | collective-permute-start | bytes 98312 | tf_op jit(solution)/shard_map/ppermute | solution.py:308
  78.1 3.6 %collective-permute-start.13 = (bf16[1536,128]{1,0:T(8,128)(2,1)S(1)}, bf16[1536,128]{1,0:T(8,128)(2,1)}, u32[]{:S(2)}, u32[]{:S(2)}) collective-permute-start(bf16[1536,128]{1,0:T(8,128)(2,1)S(1)} %collective-permute-done.12.refs_9_), channel_id=1, source_target_pairs={{0,1},{1,0},{2,3},{3,2},{4,5},{5,4},{6,7},{7,6},{8,9},{9,8},{10,11... | collective-permute-start | bytes 1179656 | tf_op jit(solution)/shard_map/ppermute | solution.py:308
  78.8 21.9 %copy-start.3 = (bf16[2048,128]{1,0:T(8,128)(2,1)}, bf16[2048,128]{1,0:T(8,128)(2,1)S(1)}, u32[]{:S(2)}) copy-start(bf16[2048,128]{1,0:T(8,128)(2,1)S(1)} %constant_dynamic-update-slice_fusion.3.w0) | copy-start | bytes 1572868
  78.9 26.3 %collective-permute-start.15 = (bf16[2048,128]{1,0:T(8,128)(2,1)S(1)}, bf16[2048,128]{1,0:T(8,128)(2,1)S(1)}, u32[]{:S(2)}, u32[]{:S(2)}) collective-permute-start(bf16[2048,128]{1,0:T(8,128)(2,1)S(1)} %constant_dynamic-update-slice_fusion.3.w0), channel_id=1, source_target_pairs={{0,2},{1,3},{2,0},{3,1},{4,6},{5,7},{6,4},{7,5},{8,10},{9,11},{10,... | collective-permute-start | bytes 1572872 | tf_op jit(solution)/shard_map/ppermute | solution.py:308
  81.4 26.9 %collective-permute-start.14 = (bf16[2048,128]{1,0:T(8,128)(2,1)S(1)}, bf16[2048,128]{1,0:T(8,128)(2,1)S(1)}, u32[]{:S(2)}, u32[]{:S(2)}) collective-permute-start(bf16[2048,128]{1,0:T(8,128)(2,1)S(1)} %constant_dynamic-update-slice_fusion.3.w0), channel_id=1, source_target_pairs={{0,1},{1,0},{2,3},{3,2},{4,5},{5,4},{6,7},{7,6},{8,9},{9,8},{10,11... | collective-permute-start | bytes 1572872 | tf_op jit(solution)/shard_map/ppermute | solution.py:308
  90.0 15.2 %copy-start.21 = (bf16[128,512]{1,0:T(8,128)(2,1)S(1)}, bf16[128,512]{1,0:T(8,128)(2,1)}, u32[]{:S(2)}) copy-start(bf16[128,512]{1,0:T(8,128)(2,1)} %param.51) | copy-start | bytes 393220
  90.0 16.2 %copy-start.28 = (s32[1024]{0:T(1024)S(1)}, s32[1024]{0:T(1024)}, u32[]{:S(2)}) copy-start(s32[1024]{0:T(1024)} %param.35) | copy-start | bytes 12292
  90.0 17.2 %copy-start.26 = (s32[1024]{0:T(1024)S(1)}, s32[1024]{0:T(1024)}, u32[]{:S(2)}) copy-start(s32[1024]{0:T(1024)} %param.36) | copy-start | bytes 12292
  100.7 19.4 %all-to-all-start.1 = ((bf16[8,64,512]{2,1,0:T(8,128)(2,1)}), bf16[8,64,512]{2,1,0:T(8,128)(2,1)S(1)}, u32[]{:S(2)}, u32[]{:S(2)}) async-start(bf16[8,64,512]{2,1,0:T(8,128)(2,1)} %bitcast.67), calls=%async_computation.1 | async-start | bytes 1048576 | tf_op jit(solution)/shard_map/all_to_all | solution.py:388
  105.2 3.1 %collective-permute-start.16 = (bf16[2048,128]{1,0:T(8,128)(2,1)S(1)}, bf16[2048,128]{1,0:T(8,128)(2,1)S(1)}, u32[]{:S(2)}, u32[]{:S(2)}) collective-permute-start(bf16[2048,128]{1,0:T(8,128)(2,1)S(1)} %collective-permute-done.15.w2), channel_id=1, source_target_pairs={{0,1},{1,0},{2,3},{3,2},{4,5},{5,4},{6,7},{7,6},{8,9},{9,8},{10,11... | collective-permute-start | bytes 1572872 | tf_op jit(solution)/shard_map/ppermute | solution.py:308
  105.4 25.4 %copy-start.9 = (bf16[1536,128]{1,0:T(8,128)(2,1)}, bf16[1536,128]{1,0:T(8,128)(2,1)S(1)}, u32[]{:S(2)}) copy-start(bf16[1536,128]{1,0:T(8,128)(2,1)S(1)} %slice_dynamic-update-slice_fusion.refs_4_) | copy-start | bytes 1179652
  105.4 25.9 %collective-permute-start.20 = (bf16[1536,128]{1,0:T(8,128)(2,1)S(1)}, bf16[1536,128]{1,0:T(8,128)(2,1)S(1)}, u32[]{:S(2)}, u32[]{:S(2)}) collective-permute-start(bf16[1536,128]{1,0:T(8,128)(2,1)S(1)} %slice_dynamic-update-slice_fusion.refs_4_), channel_id=1, source_target_pairs={{0,2},{1,3},{2,0},{3,1},{4,6},{5,7},{6,4},{7,5},{8,10},{9,11},{10,... | collective-permute-start | bytes 1179656 | tf_op jit(solution)/shard_map/ppermute | solution.py:308
  130.7 1.6 %collective-permute-start.17 = (bf16[2,128,512]{2,1,0:T(8,128)(2,1)S(1)}, bf16[2,128,512]{2,1,0:T(8,128)(2,1)S(1)}, u32[]{:S(2)}, u32[]{:S(2)}) collective-permute-start(bf16[2,128,512]{2,1,0:T(8,128)(2,1)S(1)} %dynamic-slice_bitcast_fusion), channel_id=1, source_target_pairs={{0,1},{1,0},{2,3},{3,2},{4,5},{5,4},{6,7},{7,6},{8,9},{9,8},{10,11... | collective-permute-start | bytes 786440 | tf_op jit(solution)/shard_map/ppermute | solution.py:308
  130.8 8.9 %collective-permute-start.19 = (bf16[1536,128]{1,0:T(8,128)(2,1)S(1)}, bf16[1536,128]{1,0:T(8,128)(2,1)S(1)}, u32[]{:S(2)}, u32[]{:S(2)}) collective-permute-start(bf16[1536,128]{1,0:T(8,128)(2,1)S(1)} %slice_dynamic-update-slice_fusion.refs_4_), channel_id=1, source_target_pairs={{0,1},{1,0},{2,3},{3,2},{4,5},{5,4},{6,7},{7,6},{8,9},{9,8},{10,11... | collective-permute-start | bytes 1179656 | tf_op jit(solution)/shard_map/ppermute | solution.py:308
  131.3 8.4 %collective-permute-start.21 = (bf16[1536,128]{1,0:T(8,128)(2,1)S(1)}, bf16[1536,128]{1,0:T(8,128)(2,1)S(1)}, u32[]{:S(2)}, u32[]{:S(2)}) collective-permute-start(bf16[1536,128]{1,0:T(8,128)(2,1)S(1)} %collective-permute-done.20.refs_6_), channel_id=1, source_target_pairs={{0,1},{1,0},{2,3},{3,2},{4,5},{5,4},{6,7},{7,6},{8,9},{9,8},{10,11... | collective-permute-start | bytes 1179656 | tf_op jit(solution)/shard_map/ppermute | solution.py:308
  133.3 5.6 %collective-permute-start.18 = (bf16[128,512]{1,0:T(8,128)(2,1)S(1)}, bf16[128,512]{1,0:T(8,128)(2,1)S(1)}, u32[]{:S(2)}, u32[]{:S(2)}) collective-permute-start(bf16[128,512]{1,0:T(8,128)(2,1)S(1)} %fusion.8), channel_id=1, source_target_pairs={{0,2},{1,3},{2,0},{3,1},{4,6},{5,7},{6,4},{7,5},{8,10},{9,11},{10,... | collective-permute-start | bytes 393224 | tf_op jit(solution)/shard_map/ppermute | solution.py:308
  (26 other events, 151.2 us)

commit v2 on v1

v2 whole, which is shorter than its diff:
```python
import functools
import jax
import jax.numpy as jnp
from jax import lax
from jax.experimental import pallas as pl
from jax.experimental.pallas import tpu as pltpu
from jax.sharding import PartitionSpec as P


F32 = jnp.float32
BF16 = jnp.bfloat16
I32 = jnp.int32
SPLIT = 32
CHUNK = 256
LANES = 128
WINDOW = 4
GRANT = 16 << 20
FULL = 59 << 20
META = 16

VMEM = pl.BlockSpec(memory_space=pltpu.VMEM)
SMEM = pl.BlockSpec(memory_space=pltpu.SMEM)
HBM = pl.BlockSpec(memory_space=pltpu.HBM)


def dot(a, b, ca=1, cb=0):
    return lax.dot_general(a, b, (((ca,), (cb,)), ((), ())), preferred_element_type=F32)


def cost(flops, nbytes):
    return pl.CostEstimate(flops=int(flops), bytes_accessed=int(nbytes), transcendentals=0)


def call(kernel, out_shape, specs, flops, scratch=(), grant=GRANT):
    many = isinstance(out_shape, list)
    return pl.pallas_call(
        kernel,
        out_shape=out_shape,
        in_specs=specs,
        out_specs=[VMEM] * len(out_shape) if many else VMEM,
        scratch_shapes=list(scratch),
        cost_estimate=cost(flops, 4 << 20),
        compiler_params=pltpu.CompilerParams(vmem_limit_bytes=grant),
    )


def silu(t):
    return 0.5 * t * (1.0 + jnp.tanh(0.5 * t))


def normed(raw, gain, offset, axis):
    width = raw.shape[axis]
    average = jnp.sum(raw, axis=axis, keepdims=True) * (1.0 / width)
    centred = raw - average
    spread = jnp.sum(centred * centred, axis=axis, keepdims=True) * (1.0 / width)
    return centred * lax.rsqrt(spread + 1e-05) * gain + offset


def columns_of(rows):
    height, width = rows.shape
    rows = rows.astype(F32)
    if height % 8:
        rows = jnp.concatenate([rows, jnp.zeros((8 - height % 8, width), F32)], 0)
    if width % LANES:
        rows = jnp.concatenate([rows, jnp.zeros((rows.shape[0], LANES - width % LANES), F32)], 1)
    return jnp.transpose(rows)


def open_kernel(
    lat_count,
    mesh_rows,
    owner_hbm,
    sender_hbm,
    node_hbm,
    feat_hbm,
    halo_hbm,
    from_hbm,
    to_hbm,
    latent,
    node_in,
    node_out,
    edge_in,
    edge_out,
    last_in,
    last_out,
    table_ref,
    meta_ref,
    ends_ref,
    asked_ref,
    base0,
    base1,
    base2,
    base3,
    node_pack,
    edge_pack,
    last_pack,
    owner_ref,
    sender_ref,
    node_ref,
    feat_ref,
    halo_ref,
    from_ref,
    to_ref,
    first_sem,
    sem,
):
    lon = lax.axis_index("lon")
    quarter = base0.shape[1]
    rows = base0.shape[0]
    inputs = (owner_hbm, sender_hbm, node_hbm, feat_hbm, halo_hbm, from_hbm, to_hbm)
    held = (owner_ref, sender_ref, node_ref, feat_ref, halo_ref, from_ref, to_ref)
    early = [pltpu.make_async_copy(a, b, first_sem.at[k]) for k, (a, b) in enumerate(zip(inputs, held))]
    late = []

    def bring(source, target):
        late.append(pltpu.make_async_copy(source, target, sem.at[len(late)]))

    for j, base in enumerate((base0, base1, base2, base3)):
        bring(latent.at[pl.ds(pl.multiple_of((lon ^ j) * rows, rows), rows), :], base)
    for w_in, w_out, pack in ((node_in, node_out, node_pack), (last_in, last_out, last_pack)):
        depth = w_in.shape[0]
        bring(w_in, pack.at[pl.ds(0, depth), :])
        for m in range(w_out.shape[1] // quarter):
            bring(w_out.at[:, pl.ds(m * quarter, quarter)], pack.at[pl.ds(depth + m * quarter, quarter), :])
    bring(edge_in, edge_pack.at[pl.ds(0, edge_in.shape[0]), :])
    bring(edge_out, edge_pack.at[pl.ds(edge_in.shape[0], edge_out.shape[0]), :])
    for copy in early + late:
        copy.start()
    for copy in early:
        copy.wait()
    ends_ref[...] = columns_of(jnp.concatenate([from_ref[...].astype(F32), to_ref[...].astype(F32)], 0)).astype(I32)
    asked = columns_of(halo_ref[...]).astype(I32)
    cap = halo_ref.shape[1]
    for p in range(lat_count):
        asked_ref[p * cap : (p + 1) * cap, :] = asked[0:cap, p : p + 1]
    edges = owner_ref.shape[1]
    owner = owner_ref[...]
    parts = lax.broadcasted_iota(I32, (lat_count, edges), 0)
    hits = jnp.where(parts == owner, 1.0, 0.0)
    lane = lax.broadcasted_iota(I32, (lat_count, edges), 1)
    count = hits
    step = 1
    while step < edges:
        count = count + jnp.where(lane >= step, pltpu.roll(count, step, 1), 0.0)
        step *= 2
    first = jnp.sum(jnp.where(owner < parts, 1.0, 0.0), axis=1, keepdims=True)
    place = jnp.sum(hits * (first + count - hits), axis=0, keepdims=True).astype(I32)
    key_rows = edges // LANES
    table_ref[key_rows:, :] = jnp.broadcast_to(first, (lat_count, LANES)).astype(I32)
    sender = sender_ref[...]
    node = node_ref[...]
    digits = [sender // SPLIT, sender % SPLIT, node // SPLIT, node % SPLIT, owner]
    rows = [d.astype(F32) for d in digits] + [feat_ref[...].astype(F32)]
    used = len(digits) + feat_ref.shape[0]
    meta = jnp.concatenate(rows + [jnp.ones((META - used, edges), F32)], 0).astype(BF16)
    for i in range(edges // CHUNK):
        spot = lax.broadcasted_iota(I32, (CHUNK, edges), 0) + i * CHUNK
        perm = jnp.where(spot == place, 1.0, 0.0).astype(BF16)
        moved = dot(meta, perm, 1, 1)
        meta_ref[i * CHUNK : (i + 1) * CHUNK, :] = jnp.transpose(moved).astype(BF16)
        key = moved[4:5] * float(mesh_rows) + moved[2:3] * float(SPLIT) + moved[3:4]
        for k in range(CHUNK // LANES):
            row = i * (CHUNK // LANES) + k
            table_ref[row : row + 1, :] = key[:, k * LANES : (k + 1) * LANES].astype(I32)
    for copy in late:
        copy.wait()


def message_kernel(n_feat, rows_ref, meta_ref, proj_ref, bias_ref, gain_ref, w0, w1, w2, w3, v0, v1, v2, v3, out_ref, win, wout, proj):
    quarter = w0.shape[1]
    lon = lax.axis_index("lon")
    for j, (w, v) in enumerate(((w0, v0), (w1, v1), (w2, v2), (w3, v3))):
        win[:, j * quarter : (j + 1) * quarter] = w[...]
        wout[:, j * quarter : (j + 1) * quarter] = v[...]
        at = pl.ds(pl.multiple_of((lon ^ j) * quarter, quarter), quarter)
        bias = bias_ref[0:1, at]
        high = bias.astype(BF16).astype(F32)
        mid = (bias - high).astype(BF16).astype(F32)
        low = bias - high - mid
        used = META - 5 - n_feat
        proj[:, j * quarter : (j + 1) * quarter] = jnp.concatenate(
            [jnp.zeros((5, quarter), F32), proj_ref[:, at].astype(F32), high, mid, low, jnp.zeros((used - 3, quarter), F32)], 0
        ).astype(BF16)
    rows = rows_ref[...]
    table = dot(rows, win[...]).astype(BF16)
    edges = meta_ref.shape[0]
    block = CHUNK
    for i in range(edges // block):
        at = slice(i * block, (i + 1) * block)
        meta = meta_ref[at, :]
        places = meta[:, 0:2].astype(F32)
        sender = (places[:, 0:1] * float(SPLIT) + places[:, 1:2]).astype(I32)
        source = lax.broadcasted_iota(I32, (block, rows.shape[0]), 1)
        pick = jnp.where(source == sender, 1.0, 0.0).astype(BF16)
        pre = dot(pick, table) + dot(meta, proj[...])
        raw = dot(silu(pre).astype(BF16), wout[...], 1, 1)
        out_ref[at, :] = normed(raw, gain_ref[...], bias_ref[1:2, :], 1).astype(BF16)


def sums_kernel(mesh_rows, keep, start_a, start_b, table_a, table_b, msg_a, msg_b, x_ref, y_ref):
    edges, _ = msg_a.shape
    key_rows = edges // LANES
    tall = y_ref.shape[1]
    parts = 2 * tall
    quarter = mesh_rows // 4
    half = quarter // 2
    lat = lax.axis_index("lat")
    low, high = lax.rem(lat, 2), lat // 2
    lon = lax.axis_index("lon")
    mine = lon * quarter
    other = (lon ^ 2) * quarter
    ready = min(key_rows, WINDOW)
    sets = ((start_a, table_a, msg_a), (start_b, table_b, msg_b))

    def sums(part, bases):
        rows = half * len(bases)
        row = lax.broadcasted_iota(I32, (rows, LANES), 0)
        node = row + (bases[0] + part * mesh_rows)
        for k in range(1, len(bases)):
            node = jnp.where(row >= k * half, row + (bases[k] - k * half + part * mesh_rows), node)

        def term(at, count, table, msg):
            pick = jnp.concatenate(
                [jnp.where(node == table[pl.ds(at + k, 1), :], 1.0, 0.0).astype(BF16) for k in range(count)], 1
            )
            return dot(pick, msg[pl.ds(pl.multiple_of(at * LANES, LANES), count * LANES), :])

        total = None
        later = []
        for start, table, msg in sets:
            begin = start[key_rows + part, 0]
            following = jnp.minimum(part + 1, parts - 1)
            end = jnp.where(part + 1 < parts, start[key_rows + following, 0], edges)
            at = jnp.minimum(begin // LANES, key_rows - ready)
            now = term(at, ready, table, msg)
            total = now if total is None else total + now
            later.append((at + ready, (end + LANES - 1) // LANES, table, msg))
        for at, end, table, msg in later:
            total = lax.fori_loop(at, end, lambda i, t, table=table, msg=msg: t + term(i, 1, table, msg), total)
        return total.astype(BF16)

    near_low = low if keep else 1 - low
    base = mine if keep else other

    @pl.loop(0, tall)
    def _(i):
        both = sums(2 * i + near_low, (base, mine + half, other + half))
        one = sums(2 * i + 1 - near_low, (base,))
        to = i ^ high
        x_ref[0 if keep else 1, to] = both[:half]
        x_ref[1 if keep else 0, to] = one
        y_ref[0, to] = both[half : 2 * half]
        y_ref[1, to] = both[2 * half :]


def node_sums(keep, tables, messages, lat_count, mesh_rows):
    tall = lat_count // 2
    edges, width = messages[0].shape
    out = jax.ShapeDtypeStruct((2, tall, mesh_rows // 8, width), BF16)
    return call(
        functools.partial(sums_kernel, mesh_rows, keep), [out, out], [SMEM] * 2 + [VMEM] * 4, 2 * edges * mesh_rows * width
    )(*tables, *tables, *messages)


def join_kernel(keep_x, got_x, got_xy, keep_y, got_y, got_yx, *outs):
    half = keep_x.shape[2]
    for j, out in enumerate(outs):
        out[:half] = (keep_x[0, j].astype(F32) + got_x[0, j].astype(F32) + got_xy[j].astype(F32)).astype(BF16)
        out[half:] = (keep_y[0, j].astype(F32) + got_y[0, j].astype(F32) + got_yx[j].astype(F32)).astype(BF16)


def node_kernel(n_base, n_agg, n_out, *refs):
    bases, refs = refs[:n_base], refs[n_base:]
    aggs, refs = refs[:n_agg], refs[n_agg:]
    bias_ref, gain_ref, w0, w1, w2, w3 = refs[:6]
    outs = refs[6 : 6 + n_out]
    base, win, wout = refs[6 + n_out :]
    width = base.shape[1]
    quarter = w0.shape[1]
    lon = lax.axis_index("lon")
    biases = []
    for j, w in enumerate((w0, w1, w2, w3)):
        win[:, j * quarter : (j + 1) * quarter] = w[0 : 2 * width, :]
        for m in range(width // quarter):
            wout[j * quarter : (j + 1) * quarter, m * quarter : (m + 1) * quarter] = w[
                2 * width + m * quarter : 2 * width + (m + 1) * quarter, :
            ]
        at = pl.ds(pl.multiple_of((lon ^ j) * quarter, quarter), quarter)
        biases.append(bias_ref[0:1, at])
        if n_base > 1:
            base[:, at] = bases[j][...]
    if n_base == 1:
        base[...] = bases[0][...]
    total = None
    for ref in aggs:
        term = ref[...] if len(ref.shape) == 2 else ref[0]
        total = term.astype(F32) if total is None else total + term.astype(F32)
    own = base[...]
    pre = dot(own, win[0:width, :]) + dot(total.astype(BF16), win[width:, :]) + jnp.concatenate(biases, 1)
    raw = dot(silu(pre).astype(BF16), wout[...])
    new = (own.astype(F32) + normed(raw, gain_ref[...], bias_ref[1:2, :], 1)).astype(BF16)
    if n_out == 1:
        outs[0][...] = new
    else:
        base[...] = new
        for j in range(n_out):
            outs[j][...] = base[:, pl.ds(pl.multiple_of((lon ^ j) * quarter, quarter), quarter)]


def node_network(bases, aggregates, biases, gain, pieces, n_out):
    rows, width = bases[0].shape[0], gain.shape[0]
    quarter = pieces[0].shape[1]
    kernel = functools.partial(node_kernel, len(bases), len(aggregates), n_out)
    scratch = [pltpu.VMEM((rows, width), BF16), pltpu.VMEM((2 * width, width), BF16), pltpu.VMEM((width, width), BF16)]
    out = jax.ShapeDtypeStruct((rows, width if n_out == 1 else quarter), BF16)
    operands = (*bases, *aggregates, biases, gain[None, :], *pieces)
    return call(
        kernel, out if n_out == 1 else [out] * n_out, [VMEM] * len(operands), 6 * rows * width * width, scratch
    )(*operands)


def lay_kernel(*refs):
    pieces, out_ref = refs[:4], refs[4]
    rows = pieces[0].shape[0]
    for j in range(4):
        out_ref[pl.ds(pl.multiple_of((lax.axis_index("lon") ^ j) * rows, rows), rows), :] = pieces[j][...]


def pick_kernel(index_ref, table_ref, *refs):
    outs, held = refs[:-1], refs[-1]
    lane = lax.broadcasted_iota(I32, (index_ref.shape[0], table_ref.shape[0]), 1)
    pick = jnp.where(lane == index_ref[...], 1.0, 0.0).astype(BF16)
    held[...] = dot(pick, table_ref[...])
    half = outs[0].shape[0]
    core = lax.rem(lax.axis_index("lon"), 2)
    for j, out in enumerate(outs):
        at = (lax.axis_index("lat") ^ j) * (2 * half)
        rows = held[pl.ds(pl.multiple_of(at, 2 * half), 2 * half), :]
        out[...] = jnp.where(core == 0, rows[:half], rows[half:]).astype(BF16)


def pack_kernel(*refs):
    out_ref = refs[-1]
    out_ref[...] = jnp.concatenate([ref[...].astype(F32) for ref in refs[:-1]], 0).astype(BF16)


def near_kernel(edge_hbm, mid_ref, ends_ref, bias_ref, w0, w1, w2, w3, out_ref, win, edge_ref, sem):
    block = CHUNK
    edges, width = edge_ref.shape
    loads = []
    for i in range(edges // block):
        at = pl.ds(i * block, block)
        loads.append(pltpu.make_async_copy(edge_hbm.at[at, :], edge_ref.at[at, :], sem.at[i]))
        loads[-1].start()
    quarter = w0.shape[1]
    lon = lax.axis_index("lon")
    biases = []
    for j, w in enumerate((w0, w1, w2, w3)):
        win[:, j * quarter : (j + 1) * quarter] = w[0 : 3 * width, :]
        at = pl.ds(pl.multiple_of((lon ^ j) * quarter, quarter), quarter)
        biases.append(bias_ref[0:1, at])
    bias = jnp.concatenate(biases, 1)
    rows = mid_ref.shape[0]
    sent = dot(mid_ref[...], win[width : 2 * width, :]).astype(BF16)
    got = dot(mid_ref[...], win[2 * width :, :]).astype(BF16)
    for i in range(edges // block):
        at = slice(i * block, (i + 1) * block)
        lane = lax.broadcasted_iota(I32, (block, rows), 1)
        pick_s = jnp.where(lane == ends_ref[at, 0:1], 1.0, 0.0).astype(BF16)
        pick_r = jnp.where(lane == ends_ref[at, 1:2], 1.0, 0.0).astype(BF16)
        pre = dot(pick_s, sent) + dot(pick_r, got) + bias
        loads[i].wait()
        out_ref[at, :] = pre + dot(edge_ref[at, :], win[0:width, :])


def far_kernel(halo_cap, edge_hbm, pre_ref, halo_a, halo_b, ends_ref, receiver_ref, bias_ref, gain_ref, w0, w1, w2, w3, new_ref, away_ref, keep_ref, pass_ref, total, win, wout, edge_ref, sem):
    load = pltpu.make_async_copy(edge_hbm, edge_ref, sem)
    load.start()
    width = halo_a.shape[1]
    quarter = w0.shape[1]
    lon = lax.axis_index("lon")
    for j, w in enumerate((w0, w1, w2, w3)):
        win[:, j * quarter : (j + 1) * quarter] = w[width : 2 * width, :]
        wout[:, j * quarter : (j + 1) * quarter] = w[3 * width : 4 * width, :]
    rows = halo_a.shape[0]
    mesh_rows = total.shape[0]
    sent = [dot(h[...], win[...]).astype(BF16) for h in (halo_a, halo_b)]
    half = halo_cap // 2
    lane = lax.broadcasted_iota(I32, (1, rows), 1)
    core = lax.rem(lon, 2)
    source = (lane // half) ^ lax.axis_index("lat")
    names = [mesh_rows + source * halo_cap + lane % half + c * half for c in (core, 1 - core)]
    edges = edge_ref.shape[0]
    block = 256
    for i in range(edges // block):
        at = slice(i * block, (i + 1) * block)
        pre = pre_ref[at, :]
        for name, rows_in in zip(names, sent):
            pick = jnp.where(name == ends_ref[at, 0:1], 1.0, 0.0).astype(BF16)
            pre = pre + dot(pick, rows_in)
        if i == 0:
            load.wait()
        raw = dot(silu(pre).astype(BF16), wout[...], 1, 1)
        new_ref[at, :] = (edge_ref[at, :].astype(F32) + normed(raw, gain_ref[...], bias_ref[1:2, :], 1)).astype(BF16)
    node = lax.broadcasted_iota(I32, (mesh_rows, edges), 0)
    onto = jnp.where(node == receiver_ref[...], 1.0, 0.0).astype(BF16)
    total[...] = dot(onto, new_ref[...]).astype(BF16)
    rows = keep_ref.shape[0]

    def part(flip):
        return total[pl.ds(pl.multiple_of((lon ^ flip) * rows, rows), rows), :]

    away_ref[0] = part(1)
    away_ref[1] = part(3)
    keep_ref[...] = part(0)
    pass_ref[...] = part(2)


def plus(*values):
    total = values[0].astype(F32)
    for v in values[1:]:
        total = total + v.astype(F32)
    return total.astype(BF16)


def local(
    grid_latent,
    grid_feat,
    grid_sender,
    grid_owner,
    grid_node,
    mesh_latent,
    mesh_edge,
    halo_send,
    mesh_sender,
    mesh_receiver,
    enc_edge_in,
    enc_feat_proj,
    enc_edge_out,
    enc_edge_bias,
    enc_edge_gain,
    enc_node_in,
    enc_node_out,
    enc_node_bias,
    enc_node_gain,
    proc_edge_in,
    proc_edge_out,
    proc_edge_bias,
    proc_edge_gain,
    proc_node_in,
    proc_node_out,
    proc_node_bias,
    proc_node_gain,
):
    lat_count = lax.axis_size("lat")
    width = grid_latent.shape[1]
    quarter = mesh_latent.shape[1]
    mesh_rows = mesh_latent.shape[0]
    node_rows = mesh_rows // 4
    edges = grid_sender.shape[0]
    local_edges = mesh_edge.shape[0]
    halo_cap = halo_send.shape[1]
    listed = halo_send.size

    def like(rows, columns, kind=BF16):
        return jax.ShapeDtypeStruct((rows, columns), kind)

    def hop(values, axis, flip):
        size = lax.axis_size(axis)
        return lax.ppermute(values, axis, [(i, i ^ flip) for i in range(size)])

    def spread(shard):
        across = hop(shard, "lon", 2)
        return (shard, hop(shard, "lon", 1), across, hop(across, "lon", 1))

    enc_in = spread(enc_edge_in)
    enc_out = spread(enc_edge_out)
    small = (grid_owner.reshape(1, edges), grid_sender[None, :], grid_node[None, :], grid_feat)
    small = small + (halo_send, mesh_sender[None, :], mesh_receiver[None, :])
    deep = 2 * width + 4 * enc_node_out.shape[0]
    copies = 4 + 2 * (1 + width // quarter) + 2
    table, meta, ends, asked, *rest = call(
        functools.partial(open_kernel, lat_count, mesh_rows),
        [
            like(edges // LANES + lat_count, LANES, I32),
            like(edges, META),
            like(local_edges, 8, I32),
            like(listed, 1, I32),
        ]
        + [like(node_rows, quarter)] * 4
        + [like(deep, quarter), like(4 * width, quarter), like(deep, quarter)],
        [HBM] * 14,
        2 * META * edges * edges * 8,
        [pltpu.VMEM(v.shape, v.dtype) for v in small]
        + [pltpu.SemaphoreType.DMA((len(small),)), pltpu.SemaphoreType.DMA((copies,))],
        FULL,
    )(*small, mesh_latent, enc_node_in, enc_node_out, proc_edge_in, proc_edge_out, proc_node_in, proc_node_out)
    bases = tuple(rest[j] if j == 0 else hop(rest[j], "lon", j) for j in range(4))
    node_pieces = spread(rest[4])
    edge_pieces = spread(rest[5])
    last_pieces = spread(rest[6])

    tables = (table, hop(table, "lon", 1))
    message = call(
        functools.partial(message_kernel, grid_feat.shape[0]),
        like(edges, width),
        [VMEM] * 13,
        4 * edges * width * width,
        [pltpu.VMEM((width, width), BF16), pltpu.VMEM((width, width), BF16), pltpu.VMEM((META, width), BF16)],
    )(grid_latent, meta, enc_feat_proj, enc_edge_bias, enc_edge_gain[None, :], *enc_in, *enc_out)
    messages = (message, hop(message, "lon", 1))

    tall = lat_count // 2
    send_x, send_y = node_sums(False, tables, messages, lat_count, mesh_rows)
    got_x = hop(send_x, "lon", 2)
    got_y = hop(send_y, "lat", 1)
    keep_x, keep_y = node_sums(True, tables, messages, lat_count, mesh_rows)
    got_xy = hop(plus(keep_x[1], got_x[1]), "lat", 1)
    got_yx = hop(plus(keep_y[1], got_y[1]), "lon", 2)
    joined = call(join_kernel, [like(node_rows, width)] * tall, [VMEM] * 6, 1 << 20)(
        keep_x, got_x, got_xy, keep_y, got_y, got_yx
    )
    partials = tuple(joined[j] if j == 0 else hop(joined[j], "lat", 2 * j) for j in range(tall))

    mid = node_network(bases, partials, enc_node_bias, enc_node_gain, node_pieces, 1)
    mid_all = lax.all_gather(mid, "lon", axis=0, tiled=True)

    half_cap = halo_cap // 2
    picked = call(
        pick_kernel,
        [like(half_cap, width)] * lat_count,
        [VMEM] * 2,
        2 * listed * mesh_rows * width,
        [pltpu.VMEM((listed, width), F32)],
    )(asked, mid_all)
    arrived = [picked[j] if j == 0 else hop(picked[j], "lat", j) for j in range(lat_count)]
    near = call(
        near_kernel,
        like(local_edges, width, F32),
        [HBM] + [VMEM] * 7,
        2 * local_edges * width * (width + 2 * mesh_rows),
        [
            pltpu.VMEM((3 * width, width), BF16),
            pltpu.VMEM((local_edges, width), BF16),
            pltpu.SemaphoreType.DMA((local_edges // CHUNK,)),
        ],
    )(mesh_edge, mid_all, ends, proc_edge_bias, *edge_pieces)
    packed = call(pack_kernel, like(listed // 2, width), [VMEM] * lat_count, 1 << 20)(*arrived)
    halves = (packed, hop(packed, "lon", 1))

    edge_update, away, kept, passed = call(
        functools.partial(far_kernel, halo_cap),
        [
            like(local_edges, width),
            jax.ShapeDtypeStruct((2, node_rows, width), BF16),
            like(node_rows, width),
            like(node_rows, width),
        ],
        [HBM] + [VMEM] * 11,
        2 * local_edges * width * (width + listed + mesh_rows),
        [
            pltpu.VMEM((mesh_rows, width), BF16),
            pltpu.VMEM((width, width), BF16),
            pltpu.VMEM((width, width), BF16),
            pltpu.VMEM((local_edges, width), BF16),
            pltpu.SemaphoreType.DMA,
        ],
    )(mesh_edge, near, *halves, ends, mesh_receiver[None, :], proc_edge_bias, proc_edge_gain[None, :], *edge_pieces)

    came = hop(away, "lon", 1)
    got = hop(plus(passed, came[1]), "lon", 2)
    new = node_network((mid,), (kept, came, got), proc_node_bias, proc_node_gain, last_pieces, 4)
    mesh_update = call(lay_kernel, like(mesh_rows, quarter), [VMEM] * 4, 1 << 20)(
        new[0], *[hop(new[j], "lon", j) for j in (1, 2, 3)]
    )
    return (mesh_update, edge_update)


def solution(mesh):
    both = ("lat", "lon")
    placed = (
        P(both, None),
        P(None, both),
        P(both),
        P(both, None),
        P(both),
        P("lat", "lon"),
        P(both, None),
        P("lat", None),
        P(both),
        P(both),
        P(None, "lon"),
        P(),
        P(None, "lon"),
        P(),
        P(),
        P(None, "lon"),
        P("lon", None),
        P(),
        P(),
        P(None, "lon"),
        P(None, "lon"),
        P(),
        P(),
        P(None, "lon"),
        P("lon", None),
        P(),
        P(),
    )

    return jax.shard_map(
        local,
        mesh=mesh,
        in_specs=placed,
        out_specs=(P("lat", "lon"), P(both, None)),
        check_vma=False,
    )
```

time: 153 us -> 140 us (0.915)
  waiting for transfers between devices: 31.5 us -> 63.7 us
  Pallas kernels: 55 us -> 29.2 us
  local copies, waits for them, and re-layouts: 18.7 us -> 1.15 us
  starting transfers between devices: 26.4 us -> 36.6 us
  blocking collectives: 15.3 us -> 7.66 us
  other arithmetic: 4.16 us -> 0.17 us
    ppermute x22 -> x40, waiting for transfers between devices: 24 us -> 63.7 us  [hop(): return lax.ppermute(values, axis, [(i, i ^ flip) for i in range(size)])]
    pallas_call x9 -> x12, Pallas kernels: 55 us -> 29.2 us  [the longest x2 8.54 us: node_sums(): call(functools.partial(sums_kernel, mesh_rows, keep), [out, out], [SMEM]...]
    ppermute x22 -> x40, starting transfers between devices: 17.1 us -> 36.6 us  [hop(): return lax.ppermute(values, axis, [(i, i ^ flip) for i in range(size)])]
    all_to_all x2 -> x0, starting transfers between devices: 9.31 us -> none  [the longest x1 4.87 us: local(): lax.all_to_all(summed, 'lat', 0, 0, axis_index_groups=groups, tiled=True)]
    all_to_all x2 -> x0, waiting for transfers between devices: 7.49 us -> none  [the longest x1 4.33 us: local(): lax.all_to_all(summed, 'lat', 0, 0, axis_index_groups=groups, tiled=True)]
    unnamed x79 -> x50, local copies, waits for them, and re-layouts: 8.22 us -> 1.15 us
    all_to_all x1 -> x0, blocking collectives: 6.99 us -> none  [local(): lax.all_to_all(spread_out, 'lon', 0, 0, tiled=True)]
    reshape x3 -> x0, local copies, waits for them, and re-layouts: 2.96 us -> none  [the longest x1 1.03 us: local(): sender_col = mesh_sender.reshape(local_edges, 1)]
  transfers between devices with their start and end apart: 24 -> 40, of which waited for: 9 -> 18; matrix products, arithmetic and copies ran while one was open for 7% -> 0% of each run, Pallas kernels for 21% -> 13%
where the time goes in v2:
time: 140 us
  waiting for transfers between devices  63.7 us (46%)
  starting transfers between devices  36.6 us (26%)
  Pallas kernels  29.2 us (21%)
  blocking collectives  7.66 us (5%)
    ppermute x40, waiting for transfers between devices, hop(): return lax.ppermute(values, axis, [(i, i ^ flip) for i in range(size)])  63.7 us
    ppermute x40, starting transfers between devices, hop(): return lax.ppermute(values, axis, [(i, i ^ flip) for i in range(size)])  36.6 us
    pallas_call x2, Pallas kernels, node_sums(): call(functools.partial(sums_kernel, mesh_rows, keep), [out, out], [SMEM]...  8.54 us
    all_gather x1, blocking collectives, local(): mid_all = lax.all_gather(mid, 'lon', axis=0, tiled=True)  7.66 us
    pallas_call x1, Pallas kernels, local(): call(functools.partial(open_kernel, lat_count, mesh_rows), [like(edges //...  6.09 us
    pallas_call x1, Pallas kernels, local(): call(functools.partial(message_kernel, grid_feat.shape[0]), like(edges, w...  4.66 us
    pallas_call x1, Pallas kernels, local(): call(functools.partial(far_kernel, halo_cap), [like(local_edges, width),...  3.75 us
    pallas_call x1, Pallas kernels, local(): call(near_kernel, like(local_edges, width, F32), [HBM] + [VMEM] * 7, 2 *...  3.02 us
  transfers between devices with their start and end apart: 40, of which 18 were waited for; matrix products, arithmetic and copies ran while one was open for 0% of the time, Pallas kernels for 13%

profile of v2, /device:TPU:0, one launch (start us, length us, event | category | flops | bytes accessed | tf_op | source)
XLA Modules:
  0.0 139.6 jit_solution(7487591761427270528)
XLA Ops:
  0.7 3.0 %collective-permute-start.5 = (bf16[512,128]{1,0:T(8,128)(2,1)}, bf16[512,128]{1,0:T(8,128)(2,1)S(1)}, u32[]{:S(2)}, u32[]{:S(2)}) collective-permute-start(bf16[512,128]{1,0:T(8,128)(2,1)} %w0.1), channel_id=1, source_target_pairs={{0,2},{1,3},{2,0},{3,1},{4,6},{5,7},{6,4},{7,5},{8,10},{9,11},{10,... | collective-permute-start | bytes 393224 | tf_op jit(solution)/shard_map/ppermute | solution.py:470
  4.3 4.0 %collective-permute-done.5.w2 = bf16[512,128]{1,0:T(8,128)(2,1)S(1)} collective-permute-done((bf16[512,128]{1,0:T(8,128)(2,1)}, bf16[512,128]{1,0:T(8,128)(2,1)S(1)}, u32[]{:S(2)}, u32[]{:S(2)}) %collective-permute-start.5) | collective-permute-done | bytes 131104 | tf_op jit(solution)/shard_map/ppermute | solution.py:470
  8.3 2.0 %collective-permute-done.8.v2 = bf16[512,128]{1,0:T(8,128)(2,1)S(1)} collective-permute-done((bf16[512,128]{1,0:T(8,128)(2,1)}, bf16[512,128]{1,0:T(8,128)(2,1)S(1)}, u32[]{:S(2)}, u32[]{:S(2)}) %collective-permute-start.8) | collective-permute-done | bytes 131104 | tf_op jit(solution)/shard_map/ppermute | solution.py:470
  10.2 6.1 %shard_map.266 = (s32[24,128]{1,0:T(8,128)}, bf16[2048,16]{1,0:T(8,128)(2,1)}, s32[1024,8]{1,0:T(8,128)}, s32[512,1]{1,0:T(8,128)}, bf16[128,128]{1,0:T(8,128)(2...) custom-call(s32[1,2048]{1,0:T(1,128)} %bitcast.24, ...), custom_call_target="tpu_custom_call" | custom-call | flops 1073741824 | bytes 4194304 | tf_op jit(solution)/shard_map/pallas_call | solution.py:482
  17.5 4.7 %shard_map.267.msg_a = bf16[2048,512]{1,0:T(8,128)(2,1)S(1)} custom-call(bf16[512,512]{1,0:T(8,128)(2,1)S(1)} %copy-done.14, bf16[2048,16]{1,0:T(8,128)(2,1)S(1)} %copy-done.21, bf16[4,512]{1,0:T(4,128)(2,1)S(1)} %copy-done.17, f32[2,512]{1,0:T(2,128)S(1)} %copy-done.18, f32[1,512]{1,0:T(1,128)S(1)} %bitcast.23, bf16[512,128]{1,0:T(8,128)(2,1)S(1)} %copy-done.15, ...), custom_call_target="tpu_custom_call" | custom-call | flops 2147483648 | bytes 4194304 | tf_op jit(solution)/shard_map/pallas_call | solution.py:504
  22.8 3.7 %collective-permute-done.3.start_b.table_b = s32[24,128]{1,0:T(8,128)S(1)} collective-permute-done((s32[24,128]{1,0:T(8,128)S(1)}, s32[24,128]{1,0:T(8,128)S(1)}, u32[]{:S(2)}, u32[]{:S(2)}) %collective-permute-start.3) | collective-permute-done | bytes 12320 | tf_op jit(solution)/shard_map/ppermute | solution.py:470
  26.5 4.3 %shard_map.269 = (bf16[2,4,64,512]{3,2,1,0:T(8,128)(2,1)S(1)}, bf16[2,4,64,512]{3,2,1,0:T(8,128)(2,1)S(1)}) custom-call(s32[24,128]{1,0:T(8,128)S(1)} %copy-done.5, s32[24,128]{1,0:T(8,128)S(1)} %collective-permute-done.3.start_b.table_b, s32[24,128]{1,0:T(8,128)S(1)} %copy-done.5, s32[24,128]{1,0:T(8,128)S(1)} %collective-permute-done.3.start_b.table_b, ...), custom_call_target="tpu_custom_call" | custom-call | flops 1073741824 | bytes 4194304 | tf_op jit(solution)/shard_map/pallas_call | solution.py:260
  30.9 1.6 %collective-permute-start.13 = (bf16[2,4,64,512]{3,2,1,0:T(8,128)(2,1)S(1)}, bf16[2,4,64,512]{3,2,1,0:T(8,128)(2,1)S(1)}, u32[]{:S(2)}, u32[]{:S(2)}) collective-permute-start(bf16[2,4,64,512]{3,2,1,0:T(8,128)(2,1)S(1)} %get-tuple-element.46), channel_id=1, source_target_pairs={{0,4},{4,0},{8,12},{12,8},{16,20},{20,16},{24,28},{28,24},{1,5},{5... | collective-permute-start | bytes 1572872 | tf_op jit(solution)/shard_map/ppermute | solution.py:470
  32.4 1.5 %collective-permute-start.19 = (bf16[1536,128]{1,0:T(8,128)(2,1)S(1)}, bf16[1536,128]{1,0:T(8,128)(2,1)S(1)}, u32[]{:S(2)}, u32[]{:S(2)}) collective-permute-start(bf16[1536,128]{1,0:T(8,128)(2,1)S(1)} %copy-done.4), channel_id=1, source_target_pairs={{0,2},{1,3},{2,0},{3,1},{4,6},{5,7},{6,4},{7,5},{8,10},{9,11},{10,... | collective-permute-start | bytes 1179656 | tf_op jit(solution)/shard_map/ppermute | solution.py:470
  35.1 4.2 %shard_map.268 = (bf16[2,4,64,512]{3,2,1,0:T(8,128)(2,1)S(1)}, bf16[2,4,64,512]{3,2,1,0:T(8,128)(2,1)S(1)}) custom-call(s32[24,128]{1,0:T(8,128)S(1)} %copy-done.5, s32[24,128]{1,0:T(8,128)S(1)} %collective-permute-done.3.start_b.table_b, s32[24,128]{1,0:T(8,128)S(1)} %copy-done.5, s32[24,128]{1,0:T(8,128)S(1)} %collective-permute-done.3.start_b.table_b, ...), custom_call_target="tpu_custom_call" | custom-call | flops 1073741824 | bytes 4194304 | tf_op jit(solution)/shard_map/pallas_call | solution.py:260
  39.3 5.1 %collective-permute-done.19.refs_12_ = bf16[1536,128]{1,0:T(8,128)(2,1)S(1)} collective-permute-done((bf16[1536,128]{1,0:T(8,128)(2,1)S(1)}, bf16[1536,128]{1,0:T(8,128)(2,1)S(1)}, u32[]{:S(2)}, u32[]{:S(2)}) %collective-permute-start.19) | collective-permute-done | bytes 393248 | tf_op jit(solution)/shard_map/ppermute | solution.py:470
  44.4 1.5 %collective-permute-start.22 = (bf16[2048,128]{1,0:T(8,128)(2,1)S(1)}, bf16[2048,128]{1,0:T(8,128)(2,1)S(1)}, u32[]{:S(2)}, u32[]{:S(2)}) collective-permute-start(bf16[2048,128]{1,0:T(8,128)(2,1)S(1)} %copy-done.2), channel_id=1, source_target_pairs={{0,2},{1,3},{2,0},{3,1},{4,6},{5,7},{6,4},{7,5},{8,10},{9,11},{10,... | collective-permute-start | bytes 1572872 | tf_op jit(solution)/shard_map/ppermute | solution.py:470
  46.0 9.6 %collective-permute-done.11.got_x = bf16[2,4,64,512]{3,2,1,0:T(8,128)(2,1)S(1)} collective-permute-done((bf16[2,4,64,512]{3,2,1,0:T(8,128)(2,1)S(1)}, bf16[2,4,64,512]{3,2,1,0:T(8,128)(2,1)S(1)}, u32[]{:S(2)}, u32[]{:S(2)}) %collective-permute-start.11) | collective-permute-done | bytes 524320 | tf_op jit(solution)/shard_map/ppermute | solution.py:470
  55.7 1.5 %collective-permute-start.14 = (bf16[4,64,512]{2,1,0:T(8,128)(2,1)S(1)}, bf16[4,64,512]{2,1,0:T(8,128)(2,1)S(1)}, u32[]{:S(2)}, u32[]{:S(2)}) collective-permute-start(bf16[4,64,512]{2,1,0:T(8,128)(2,1)S(1)} %fusion.1), channel_id=1, source_target_pairs={{0,2},{1,3},{2,0},{3,1},{4,6},{5,7},{6,4},{7,5},{8,10},{9,11},{10,... | collective-permute-start | bytes 786440 | tf_op jit(solution)/shard_map/ppermute | solution.py:470
  57.8 13.8 %collective-permute-done.14.got_yx = bf16[4,64,512]{2,1,0:T(8,128)(2,1)S(1)} collective-permute-done((bf16[4,64,512]{2,1,0:T(8,128)(2,1)S(1)}, bf16[4,64,512]{2,1,0:T(8,128)(2,1)S(1)}, u32[]{:S(2)}, u32[]{:S(2)}) %collective-permute-start.14) | collective-permute-done | bytes 262176 | tf_op jit(solution)/shard_map/ppermute | solution.py:470
  71.6 1.5 %collective-permute-start.1 = (bf16[128,128]{1,0:T(8,128)(2,1)S(1)}, bf16[128,128]{1,0:T(8,128)(2,1)S(1)}, u32[]{:S(2)}, u32[]{:S(2)}) collective-permute-start(bf16[128,128]{1,0:T(8,128)(2,1)S(1)} %copy-done.23), channel_id=1, source_target_pairs={{0,2},{1,3},{2,0},{3,1},{4,6},{5,7},{6,4},{7,5},{8,10},{9,11},{10,... | collective-permute-start | bytes 98312 | tf_op jit(solution)/shard_map/ppermute | solution.py:470
  73.4 2.2 %collective-permute-done.1.refs_2_ = bf16[128,128]{1,0:T(8,128)(2,1)S(1)} collective-permute-done((bf16[128,128]{1,0:T(8,128)(2,1)S(1)}, bf16[128,128]{1,0:T(8,128)(2,1)S(1)}, u32[]{:S(2)}, u32[]{:S(2)}) %collective-permute-start.1) | collective-permute-done | bytes 32800 | tf_op jit(solution)/shard_map/ppermute | solution.py:470
  75.6 1.7 %collective-permute-start.15 = (bf16[128,512]{1,0:T(8,128)(2,1)S(1)}, bf16[128,512]{1,0:T(8,128)(2,1)S(1)}, u32[]{:S(2)}, u32[]{:S(2)}) collective-permute-start(bf16[128,512]{1,0:T(8,128)(2,1)S(1)} %get-tuple-element.48), channel_id=1, source_target_pairs={{0,8},{4,12},{8,0},{12,4},{16,24},{20,28},{24,16},{28,20},{1,9},{5... | collective-permute-start | bytes 393224 | tf_op jit(solution)/shard_map/ppermute | solution.py:470
  77.3 2.4 %collective-permute-start.16 = (bf16[128,512]{1,0:T(8,128)(2,1)S(1)}, bf16[128,512]{1,0:T(8,128)(2,1)S(1)}, u32[]{:S(2)}, u32[]{:S(2)}) collective-permute-start(bf16[128,512]{1,0:T(8,128)(2,1)S(1)} %get-tuple-element.49), channel_id=1, source_target_pairs={{0,16},{4,20},{8,24},{12,28},{16,0},{20,4},{24,8},{28,12},{1,17},{... | collective-permute-start | bytes 393224 | tf_op jit(solution)/shard_map/ppermute | solution.py:470
  82.0 7.1 %collective-permute-done.16.refs_6_ = bf16[128,512]{1,0:T(8,128)(2,1)S(1)} collective-permute-done((bf16[128,512]{1,0:T(8,128)(2,1)S(1)}, bf16[128,512]{1,0:T(8,128)(2,1)S(1)}, u32[]{:S(2)}, u32[]{:S(2)}) %collective-permute-start.16) | collective-permute-done | bytes 131104 | tf_op jit(solution)/shard_map/ppermute | solution.py:470
  90.1 7.7 %all_gather.3.mid_ref.table_ref = bf16[512,512]{1,0:T(8,128)(2,1)S(1)} all-gather(bf16[128,512]{1,0:T(8,128)(2,1)S(1)} %shard_map.271.refs_0_), channel_id=1, replica_groups=mesh['lat'=8,'lon'=4] {'lon'}, dimensions={0}, use_global_device_ids=true | all-gather | bytes 655360 | tf_op jit(solution)/shard_map/all_gather | solution.py:526
  98.7 2.2 %collective-permute-start.25 = (bf16[32,512]{1,0:T(8,128)(2,1)S(1)}, bf16[32,512]{1,0:T(8,128)(2,1)S(1)}, u32[]{:S(2)}, u32[]{:S(2)}) collective-permute-start(bf16[32,512]{1,0:T(8,128)(2,1)S(1)} %get-tuple-element.57), channel_id=1, source_target_pairs={{0,8},{4,12},{8,0},{12,4},{16,24},{20,28},{24,16},{28,20},{1,9},{5... | collective-permute-start | bytes 98312 | tf_op jit(solution)/shard_map/ppermute | solution.py:470
  102.2 4.0 %collective-permute-start.27 = (bf16[32,512]{1,0:T(8,128)(2,1)S(1)}, bf16[32,512]{1,0:T(8,128)(2,1)S(1)}, u32[]{:S(2)}, u32[]{:S(2)}) collective-permute-start(bf16[32,512]{1,0:T(8,128)(2,1)S(1)} %get-tuple-element.59), channel_id=1, source_target_pairs={{0,16},{4,20},{8,24},{12,28},{16,0},{20,4},{24,8},{28,12},{1,17},{... | collective-permute-start | bytes 98312 | tf_op jit(solution)/shard_map/ppermute | solution.py:470
  106.2 1.6 %collective-permute-start.28 = (bf16[32,512]{1,0:T(8,128)(2,1)S(1)}, bf16[32,512]{1,0:T(8,128)(2,1)S(1)}, u32[]{:S(2)}, u32[]{:S(2)}) collective-permute-start(bf16[32,512]{1,0:T(8,128)(2,1)S(1)} %get-tuple-element.60), channel_id=1, source_target_pairs={{0,20},{4,16},{8,28},{12,24},{16,4},{20,0},{24,12},{28,8},{1,21},{... | collective-permute-start | bytes 98312 | tf_op jit(solution)/shard_map/ppermute | solution.py:470
  109.3 2.6 %collective-permute-start.30 = (bf16[32,512]{1,0:T(8,128)(2,1)S(1)}, bf16[32,512]{1,0:T(8,128)(2,1)S(1)}, u32[]{:S(2)}, u32[]{:S(2)}) collective-permute-start(bf16[32,512]{1,0:T(8,128)(2,1)S(1)} %get-tuple-element.62), channel_id=1, source_target_pairs={{0,28},{4,24},{8,20},{12,16},{16,12},{20,8},{24,4},{28,0},{1,29},{... | collective-permute-start | bytes 98312 | tf_op jit(solution)/shard_map/ppermute | solution.py:470
  112.1 1.5 %collective-permute-done.29.refs_6_ = bf16[32,512]{1,0:T(8,128)(2,1)S(1)} collective-permute-done((bf16[32,512]{1,0:T(8,128)(2,1)S(1)}, bf16[32,512]{1,0:T(8,128)(2,1)S(1)}, u32[]{:S(2)}, u32[]{:S(2)}) %collective-permute-start.29) | collective-permute-done | bytes 32800 | tf_op jit(solution)/shard_map/ppermute | solution.py:470
  113.6 2.3 %collective-permute-done.30.refs_7_ = bf16[32,512]{1,0:T(8,128)(2,1)S(1)} collective-permute-done((bf16[32,512]{1,0:T(8,128)(2,1)S(1)}, bf16[32,512]{1,0:T(8,128)(2,1)S(1)}, u32[]{:S(2)}, u32[]{:S(2)}) %collective-permute-start.30) | collective-permute-done | bytes 32800 | tf_op jit(solution)/shard_map/ppermute | solution.py:470
  116.9 3.0 %shard_map.272.pre_ref = f32[1024,512]{1,0:T(8,128)S(1)} custom-call(bf16[1024,512]{1,0:T(8,128)(2,1)S(1)} %copy-done, bf16[512,512]{1,0:T(8,128)(2,1)S(1)} %all_gather.3.mid_ref.table_ref, s32[1024,8]{1,0:T(8,128)S(1)} %copy-done.1, f32[2,512]{1,0:T(2,128)S(1)} %copy-done.7, bf16[2048,128]{1,0:T(8,128)(2,1)S(1)} %copy-done.2, ...), custom_call_target="tpu_custom_call" | custom-call | flops 1610612736 | bytes 4194304 | tf_op jit(solution)/shard_map/pallas_call | solution.py:537
  120.0 3.8 %shard_map.275 = (bf16[1024,512]{1,0:T(8,128)(2,1)}, bf16[2,128,512]{2,1,0:T(8,128)(2,1)S(1)}, bf16[128,512]{1,0:T(8,128)(2,1)S(1)}, bf16[128,512]{1,0:T(8,128)(2,1)S(1)}) custom-call(bf16[1024,512]{1,0:T(8,128)(2,1)S(1)} %copy-done, f32[1024,512]{1,0:T(8,128)S(1)} %shard_map.272.pre_ref, bf16[256,512]{1,0:T(8,128)(2,1)S(1)} %shard_map.274.halo_a, ...), custom_call_target="tpu_custom_call" | custom-call | flops 1610612736 | bytes 4194304 | tf_op jit(solution)/shard_map/pallas_call | solution.py:551
  124.3 3.2 %collective-permute-done.35.refs_8_ = bf16[1536,128]{1,0:T(8,128)(2,1)S(1)} collective-permute-done((bf16[1536,128]{1,0:T(8,128)(2,1)S(1)}, bf16[1536,128]{1,0:T(8,128)(2,1)S(1)}, u32[]{:S(2)}, u32[]{:S(2)}) %collective-permute-start.35) | collective-permute-done | bytes 393248 | tf_op jit(solution)/shard_map/ppermute | solution.py:470
  129.2 4.3 %collective-permute-done.33.refs_3_ = bf16[128,512]{1,0:T(8,128)(2,1)S(1)} collective-permute-done((bf16[128,512]{1,0:T(8,128)(2,1)S(1)}, bf16[128,512]{1,0:T(8,128)(2,1)S(1)}, u32[]{:S(2)}, u32[]{:S(2)}) %collective-permute-start.33) | collective-permute-done | bytes 131104 | tf_op jit(solution)/shard_map/ppermute | solution.py:470
  136.4 2.2 %collective-permute-done.38.refs_2_ = bf16[128,128]{1,0:T(8,128)(2,1)S(1)} collective-permute-done((bf16[128,128]{1,0:T(8,128)(2,1)S(1)}, bf16[128,128]{1,0:T(8,128)(2,1)S(1)}, u32[]{:S(2)}, u32[]{:S(2)}) %collective-permute-start.38) | collective-permute-done | bytes 32800 | tf_op jit(solution)/shard_map/ppermute | solution.py:470
  (114 shorter events, 18.6 us)
Async XLA Ops:
  0.7 7.6 %collective-permute-start.5 = (bf16[512,128]{1,0:T(8,128)(2,1)}, bf16[512,128]{1,0:T(8,128)(2,1)S(1)}, u32[]{:S(2)}, u32[]{:S(2)}) collective-permute-start(bf16[512,128]{1,0:T(8,128)(2,1)} %w0.1), channel_id=1, source_target_pairs={{0,2},{1,3},{2,0},{3,1},{4,6},{5,7},{6,4},{7,5},{8,10},{9,11},{10,... | collective-permute-start | bytes 393224 | tf_op jit(solution)/shard_map/ppermute | solution.py:470
  3.7 6.5 %collective-permute-start.8 = (bf16[512,128]{1,0:T(8,128)(2,1)}, bf16[512,128]{1,0:T(8,128)(2,1)S(1)}, u32[]{:S(2)}, u32[]{:S(2)}) collective-permute-start(bf16[512,128]{1,0:T(8,128)(2,1)} %v0.1), channel_id=1, source_target_pairs={{0,2},{1,3},{2,0},{3,1},{4,6},{5,7},{6,4},{7,5},{8,10},{9,11},{10,... | collective-permute-start | bytes 393224 | tf_op jit(solution)/shard_map/ppermute | solution.py:470
  3.8 12.5 %collective-permute-start.4 = (bf16[512,128]{1,0:T(8,128)(2,1)}, bf16[512,128]{1,0:T(8,128)(2,1)S(1)}, u32[]{:S(2)}, u32[]{:S(2)}) collective-permute-start(bf16[512,128]{1,0:T(8,128)(2,1)} %w0.1), channel_id=1, source_target_pairs={{0,1},{1,0},{2,3},{3,2},{4,5},{5,4},{6,7},{7,6},{8,9},{9,8},{10,11... | collective-permute-start | bytes 393224 | tf_op jit(solution)/shard_map/ppermute | solution.py:470
  3.8 12.5 %collective-permute-start.7 = (bf16[512,128]{1,0:T(8,128)(2,1)}, bf16[512,128]{1,0:T(8,128)(2,1)S(1)}, u32[]{:S(2)}, u32[]{:S(2)}) collective-permute-start(bf16[512,128]{1,0:T(8,128)(2,1)} %v0.1), channel_id=1, source_target_pairs={{0,1},{1,0},{2,3},{3,2},{4,5},{5,4},{6,7},{7,6},{8,9},{9,8},{10,11... | collective-permute-start | bytes 393224 | tf_op jit(solution)/shard_map/ppermute | solution.py:470
  8.3 8.1 %collective-permute-start.6 = (bf16[512,128]{1,0:T(8,128)(2,1)S(1)}, bf16[512,128]{1,0:T(8,128)(2,1)S(1)}, u32[]{:S(2)}, u32[]{:S(2)}) collective-permute-start(bf16[512,128]{1,0:T(8,128)(2,1)S(1)} %collective-permute-done.5.w2), channel_id=1, source_target_pairs={{0,1},{1,0},{2,3},{3,2},{4,5},{5,4},{6,7},{7,6},{8,9},{9,8},{10,11... | collective-permute-start | bytes 393224 | tf_op jit(solution)/shard_map/ppermute | solution.py:470
  10.2 6.1 %collective-permute-start.9 = (bf16[512,128]{1,0:T(8,128)(2,1)S(1)}, bf16[512,128]{1,0:T(8,128)(2,1)S(1)}, u32[]{:S(2)}, u32[]{:S(2)}) collective-permute-start(bf16[512,128]{1,0:T(8,128)(2,1)S(1)} %collective-permute-done.8.v2), channel_id=1, source_target_pairs={{0,1},{1,0},{2,3},{3,2},{4,5},{5,4},{6,7},{7,6},{8,9},{9,8},{10,11... | collective-permute-start | bytes 393224 | tf_op jit(solution)/shard_map/ppermute | solution.py:470
  22.2 4.4 %collective-permute-start.10 = (bf16[2048,512]{1,0:T(8,128)(2,1)S(1)}, bf16[2048,512]{1,0:T(8,128)(2,1)S(1)}, u32[]{:S(2)}, u32[]{:S(2)}) collective-permute-start(bf16[2048,512]{1,0:T(8,128)(2,1)S(1)} %shard_map.267.msg_a), channel_id=1, source_target_pairs={{0,1},{1,0},{2,3},{3,2},{4,5},{5,4},{6,7},{7,6},{8,9},{9,8},{10,11... | collective-permute-start | bytes 6291464 | tf_op jit(solution)/shard_map/ppermute | solution.py:470
  30.9 15.1 %collective-permute-start.13 = (bf16[2,4,64,512]{3,2,1,0:T(8,128)(2,1)S(1)}, bf16[2,4,64,512]{3,2,1,0:T(8,128)(2,1)S(1)}, u32[]{:S(2)}, u32[]{:S(2)}) collective-permute-start(bf16[2,4,64,512]{3,2,1,0:T(8,128)(2,1)S(1)} %get-tuple-element.46), channel_id=1, source_target_pairs={{0,4},{4,0},{8,12},{12,8},{16,20},{20,16},{24,28},{28,24},{1,5},{5... | collective-permute-start | bytes 1572872 | tf_op jit(solution)/shard_map/ppermute | solution.py:470
  32.4 12.0 %collective-permute-start.19 = (bf16[1536,128]{1,0:T(8,128)(2,1)S(1)}, bf16[1536,128]{1,0:T(8,128)(2,1)S(1)}, u32[]{:S(2)}, u32[]{:S(2)}) collective-permute-start(bf16[1536,128]{1,0:T(8,128)(2,1)S(1)} %copy-done.4), channel_id=1, source_target_pairs={{0,2},{1,3},{2,0},{3,1},{4,6},{5,7},{6,4},{7,5},{8,10},{9,11},{10,... | collective-permute-start | bytes 1179656 | tf_op jit(solution)/shard_map/ppermute | solution.py:470
  33.9 21.7 %collective-permute-start.11 = (bf16[2,4,64,512]{3,2,1,0:T(8,128)(2,1)S(1)}, bf16[2,4,64,512]{3,2,1,0:T(8,128)(2,1)S(1)}, u32[]{:S(2)}, u32[]{:S(2)}) collective-permute-start(bf16[2,4,64,512]{3,2,1,0:T(8,128)(2,1)S(1)} %get-tuple-element.44), channel_id=1, source_target_pairs={{0,2},{1,3},{2,0},{3,1},{4,6},{5,7},{6,4},{7,5},{8,10},{9,11},{10,... | collective-permute-start | bytes 1572872 | tf_op jit(solution)/shard_map/ppermute | solution.py:470
  34.5 45.3 %collective-permute-start.18 = (bf16[1536,128]{1,0:T(8,128)(2,1)S(1)}, bf16[1536,128]{1,0:T(8,128)(2,1)S(1)}, u32[]{:S(2)}, u32[]{:S(2)}) collective-permute-start(bf16[1536,128]{1,0:T(8,128)(2,1)S(1)} %copy-done.4), channel_id=1, source_target_pairs={{0,1},{1,0},{2,3},{3,2},{4,5},{5,4},{6,7},{7,6},{8,9},{9,8},{10,11... | collective-permute-start | bytes 1179656 | tf_op jit(solution)/shard_map/ppermute | solution.py:470
  34.5 22.7 %collective-permute-start = (bf16[128,128]{1,0:T(8,128)(2,1)S(1)}, bf16[128,128]{1,0:T(8,128)(2,1)S(1)}, u32[]{:S(2)}, u32[]{:S(2)}) collective-permute-start(bf16[128,128]{1,0:T(8,128)(2,1)S(1)} %copy-done.24), channel_id=1, source_target_pairs={{0,1},{1,0},{2,3},{3,2},{4,5},{5,4},{6,7},{7,6},{8,9},{9,8},{10,11... | collective-permute-start | bytes 98312 | tf_op jit(solution)/shard_map/ppermute | solution.py:470
  44.4 36.1 %collective-permute-start.22 = (bf16[2048,128]{1,0:T(8,128)(2,1)S(1)}, bf16[2048,128]{1,0:T(8,128)(2,1)S(1)}, u32[]{:S(2)}, u32[]{:S(2)}) collective-permute-start(bf16[2048,128]{1,0:T(8,128)(2,1)S(1)} %copy-done.2), channel_id=1, source_target_pairs={{0,2},{1,3},{2,0},{3,1},{4,6},{5,7},{6,4},{7,5},{8,10},{9,11},{10,... | collective-permute-start | bytes 1572872 | tf_op jit(solution)/shard_map/ppermute | solution.py:470
  45.9 34.7 %collective-permute-start.20 = (bf16[1536,128]{1,0:T(8,128)(2,1)S(1)}, bf16[1536,128]{1,0:T(8,128)(2,1)S(1)}, u32[]{:S(2)}, u32[]{:S(2)}) collective-permute-start(bf16[1536,128]{1,0:T(8,128)(2,1)S(1)} %collective-permute-done.19.refs_12_), channel_id=1, source_target_pairs={{0,1},{1,0},{2,3},{3,2},{4,5},{5,4},{6,7},{7,6},{8,9},{9,8},{10,11... | collective-permute-start | bytes 1179656 | tf_op jit(solution)/shard_map/ppermute | solution.py:470
  55.7 16.0 %collective-permute-start.14 = (bf16[4,64,512]{2,1,0:T(8,128)(2,1)S(1)}, bf16[4,64,512]{2,1,0:T(8,128)(2,1)S(1)}, u32[]{:S(2)}, u32[]{:S(2)}) collective-permute-start(bf16[4,64,512]{2,1,0:T(8,128)(2,1)S(1)} %fusion.1), channel_id=1, source_target_pairs={{0,2},{1,3},{2,0},{3,1},{4,6},{5,7},{6,4},{7,5},{8,10},{9,11},{10,... | collective-permute-start | bytes 786440 | tf_op jit(solution)/shard_map/ppermute | solution.py:470
  57.2 15.9 %collective-permute-start.12 = (bf16[4,64,512]{2,1,0:T(8,128)(2,1)S(1)}, bf16[4,64,512]{2,1,0:T(8,128)(2,1)S(1)}, u32[]{:S(2)}, u32[]{:S(2)}) collective-permute-start(bf16[4,64,512]{2,1,0:T(8,128)(2,1)S(1)} %fusion), channel_id=1, source_target_pairs={{0,4},{4,0},{8,12},{12,8},{16,20},{20,16},{24,28},{28,24},{1,5},{5... | collective-permute-start | bytes 786440 | tf_op jit(solution)/shard_map/ppermute | solution.py:470
  73.1 4.2 %collective-permute-start.2 = (bf16[128,128]{1,0:T(8,128)(2,1)S(1)}, bf16[128,128]{1,0:T(8,128)(2,1)S(1)}, u32[]{:S(2)}, u32[]{:S(2)}) collective-permute-start(bf16[128,128]{1,0:T(8,128)(2,1)S(1)} %copy-done.22), channel_id=1, source_target_pairs={{0,3},{1,2},{2,1},{3,0},{4,7},{5,6},{6,5},{7,4},{8,11},{9,10},{10,... | collective-permute-start | bytes 98312 | tf_op jit(solution)/shard_map/ppermute | solution.py:470
  75.6 6.4 %collective-permute-start.15 = (bf16[128,512]{1,0:T(8,128)(2,1)S(1)}, bf16[128,512]{1,0:T(8,128)(2,1)S(1)}, u32[]{:S(2)}, u32[]{:S(2)}) collective-permute-start(bf16[128,512]{1,0:T(8,128)(2,1)S(1)} %get-tuple-element.48), channel_id=1, source_target_pairs={{0,8},{4,12},{8,0},{12,4},{16,24},{20,28},{24,16},{28,20},{1,9},{5... | collective-permute-start | bytes 393224 | tf_op jit(solution)/shard_map/ppermute | solution.py:470
  77.3 11.8 %collective-permute-start.16 = (bf16[128,512]{1,0:T(8,128)(2,1)S(1)}, bf16[128,512]{1,0:T(8,128)(2,1)S(1)}, u32[]{:S(2)}, u32[]{:S(2)}) collective-permute-start(bf16[128,512]{1,0:T(8,128)(2,1)S(1)} %get-tuple-element.49), channel_id=1, source_target_pairs={{0,16},{4,20},{8,24},{12,28},{16,0},{20,4},{24,8},{28,12},{1,17},{... | collective-permute-start | bytes 393224 | tf_op jit(solution)/shard_map/ppermute | solution.py:470
  79.7 9.4 %collective-permute-start.17 = (bf16[128,512]{1,0:T(8,128)(2,1)S(1)}, bf16[128,512]{1,0:T(8,128)(2,1)S(1)}, u32[]{:S(2)}, u32[]{:S(2)}) collective-permute-start(bf16[128,512]{1,0:T(8,128)(2,1)S(1)} %get-tuple-element.50), channel_id=1, source_target_pairs={{0,24},{4,28},{8,16},{12,20},{16,8},{20,12},{24,0},{28,4},{1,25},{... | collective-permute-start | bytes 393224 | tf_op jit(solution)/shard_map/ppermute | solution.py:470
  80.6 36.3 %collective-permute-start.21 = (bf16[2048,128]{1,0:T(8,128)(2,1)S(1)}, bf16[2048,128]{1,0:T(8,128)(2,1)S(1)}, u32[]{:S(2)}, u32[]{:S(2)}) collective-permute-start(bf16[2048,128]{1,0:T(8,128)(2,1)S(1)} %copy-done.2), channel_id=1, source_target_pairs={{0,1},{1,0},{2,3},{3,2},{4,5},{5,4},{6,7},{7,6},{8,9},{9,8},{10,11... | collective-permute-start | bytes 1572872 | tf_op jit(solution)/shard_map/ppermute | solution.py:470
  80.6 36.3 %collective-permute-start.23 = (bf16[2048,128]{1,0:T(8,128)(2,1)S(1)}, bf16[2048,128]{1,0:T(8,128)(2,1)S(1)}, u32[]{:S(2)}, u32[]{:S(2)}) collective-permute-start(bf16[2048,128]{1,0:T(8,128)(2,1)S(1)} %collective-permute-done.22.w2), channel_id=1, source_target_pairs={{0,1},{1,0},{2,3},{3,2},{4,5},{5,4},{6,7},{7,6},{8,9},{9,8},{10,11... | collective-permute-start | bytes 1572872 | tf_op jit(solution)/shard_map/ppermute | solution.py:470
  98.7 7.5 %collective-permute-start.25 = (bf16[32,512]{1,0:T(8,128)(2,1)S(1)}, bf16[32,512]{1,0:T(8,128)(2,1)S(1)}, u32[]{:S(2)}, u32[]{:S(2)}) collective-permute-start(bf16[32,512]{1,0:T(8,128)(2,1)S(1)} %get-tuple-element.57), channel_id=1, source_target_pairs={{0,8},{4,12},{8,0},{12,4},{16,24},{20,28},{24,16},{28,20},{1,9},{5... | collective-permute-start | bytes 98312 | tf_op jit(solution)/shard_map/ppermute | solution.py:470
  101.0 6.9 %collective-permute-start.26 = (bf16[32,512]{1,0:T(8,128)(2,1)S(1)}, bf16[32,512]{1,0:T(8,128)(2,1)S(1)}, u32[]{:S(2)}, u32[]{:S(2)}) collective-permute-start(bf16[32,512]{1,0:T(8,128)(2,1)S(1)} %get-tuple-element.58), channel_id=1, source_target_pairs={{0,12},{4,8},{8,4},{12,0},{16,28},{20,24},{24,20},{28,16},{1,13},{... | collective-permute-start | bytes 98312 | tf_op jit(solution)/shard_map/ppermute | solution.py:470
  102.2 7.0 %collective-permute-start.27 = (bf16[32,512]{1,0:T(8,128)(2,1)S(1)}, bf16[32,512]{1,0:T(8,128)(2,1)S(1)}, u32[]{:S(2)}, u32[]{:S(2)}) collective-permute-start(bf16[32,512]{1,0:T(8,128)(2,1)S(1)} %get-tuple-element.59), channel_id=1, source_target_pairs={{0,16},{4,20},{8,24},{12,28},{16,0},{20,4},{24,8},{28,12},{1,17},{... | collective-permute-start | bytes 98312 | tf_op jit(solution)/shard_map/ppermute | solution.py:470
  106.2 5.8 %collective-permute-start.28 = (bf16[32,512]{1,0:T(8,128)(2,1)S(1)}, bf16[32,512]{1,0:T(8,128)(2,1)S(1)}, u32[]{:S(2)}, u32[]{:S(2)}) collective-permute-start(bf16[32,512]{1,0:T(8,128)(2,1)S(1)} %get-tuple-element.60), channel_id=1, source_target_pairs={{0,20},{4,16},{8,28},{12,24},{16,4},{20,0},{24,12},{28,8},{1,21},{... | collective-permute-start | bytes 98312 | tf_op jit(solution)/shard_map/ppermute | solution.py:470
  107.9 5.7 %collective-permute-start.29 = (bf16[32,512]{1,0:T(8,128)(2,1)S(1)}, bf16[32,512]{1,0:T(8,128)(2,1)S(1)}, u32[]{:S(2)}, u32[]{:S(2)}) collective-permute-start(bf16[32,512]{1,0:T(8,128)(2,1)S(1)} %get-tuple-element.61), channel_id=1, source_target_pairs={{0,24},{4,28},{8,16},{12,20},{16,8},{20,12},{24,0},{28,4},{1,25},{... | collective-permute-start | bytes 98312 | tf_op jit(solution)/shard_map/ppermute | solution.py:470
  109.3 6.6 %collective-permute-start.30 = (bf16[32,512]{1,0:T(8,128)(2,1)S(1)}, bf16[32,512]{1,0:T(8,128)(2,1)S(1)}, u32[]{:S(2)}, u32[]{:S(2)}) collective-permute-start(bf16[32,512]{1,0:T(8,128)(2,1)S(1)} %get-tuple-element.62), channel_id=1, source_target_pairs={{0,28},{4,24},{8,20},{12,16},{16,12},{20,8},{24,4},{28,0},{1,29},{... | collective-permute-start | bytes 98312 | tf_op jit(solution)/shard_map/ppermute | solution.py:470
  116.0 11.5 %collective-permute-start.35 = (bf16[1536,128]{1,0:T(8,128)(2,1)S(1)}, bf16[1536,128]{1,0:T(8,128)(2,1)S(1)}, u32[]{:S(2)}, u32[]{:S(2)}) collective-permute-start(bf16[1536,128]{1,0:T(8,128)(2,1)S(1)} %copy-done.3), channel_id=1, source_target_pairs={{0,2},{1,3},{2,0},{3,1},{4,6},{5,7},{6,4},{7,5},{8,10},{9,11},{10,... | collective-permute-start | bytes 1179656 | tf_op jit(solution)/shard_map/ppermute | solution.py:470
  124.0 4.4 %collective-permute-start.34 = (bf16[1536,128]{1,0:T(8,128)(2,1)S(1)}, bf16[1536,128]{1,0:T(8,128)(2,1)S(1)}, u32[]{:S(2)}, u32[]{:S(2)}) collective-permute-start(bf16[1536,128]{1,0:T(8,128)(2,1)S(1)} %copy-done.3), channel_id=1, source_target_pairs={{0,1},{1,0},{2,3},{3,2},{4,5},{5,4},{6,7},{7,6},{8,9},{9,8},{10,11... | collective-permute-start | bytes 1179656 | tf_op jit(solution)/shard_map/ppermute | solution.py:470
  127.5 6.0 %collective-permute-start.33 = (bf16[128,512]{1,0:T(8,128)(2,1)S(1)}, bf16[128,512]{1,0:T(8,128)(2,1)S(1)}, u32[]{:S(2)}, u32[]{:S(2)}) collective-permute-start(bf16[128,512]{1,0:T(8,128)(2,1)S(1)} %fusion.2), channel_id=1, source_target_pairs={{0,2},{1,3},{2,0},{3,1},{4,6},{5,7},{6,4},{7,5},{8,10},{9,11},{10,... | collective-permute-start | bytes 393224 | tf_op jit(solution)/shard_map/ppermute | solution.py:470
  134.5 4.1 %collective-permute-start.38 = (bf16[128,128]{1,0:T(8,128)(2,1)S(1)}, bf16[128,128]{1,0:T(8,128)(2,1)S(1)}, u32[]{:S(2)}, u32[]{:S(2)}) collective-permute-start(bf16[128,128]{1,0:T(8,128)(2,1)S(1)} %get-tuple-element.69), channel_id=1, source_target_pairs={{0,2},{1,3},{2,0},{3,1},{4,6},{5,7},{6,4},{7,5},{8,10},{9,11},{10,... | collective-permute-start | bytes 98312 | tf_op jit(solution)/shard_map/ppermute | solution.py:470
  (33 other events, 531.9 us)

commit v3 on v2

--- a/solution.py
+++ b/solution.py
@@ -13,7 +13,6 @@
 SPLIT = 32
 CHUNK = 256
 LANES = 128
-WINDOW = 4
 GRANT = 16 << 20
 FULL = 59 << 20
 META = 16
@@ -25,6 +24,12 @@
 
 def dot(a, b, ca=1, cb=0):
     return lax.dot_general(a, b, (((ca,), (cb,)), ((), ())), preferred_element_type=F32)
+
+
+def turns(count):
+    flips = sorted(range(count), key=lambda f: (-(f % 2 + f // 2), -f))
+    shares = [f for k, f in enumerate(flips) if k % 4 in (0, 3)], [f for k, f in enumerate(flips) if k % 4 in (1, 2)]
+    return list(zip(*sorted(shares, key=lambda share: share[-1])))
 
 
 def cost(flops, nbytes):
@@ -77,12 +82,6 @@
     from_hbm,
     to_hbm,
     latent,
-    node_in,
-    node_out,
-    edge_in,
-    edge_out,
-    last_in,
-    last_out,
     table_ref,
     meta_ref,
     ends_ref,
@@ -91,9 +90,6 @@
     base1,
     base2,
     base3,
-    node_pack,
-    edge_pack,
-    last_pack,
     owner_ref,
     sender_ref,
     node_ref,
@@ -105,7 +101,6 @@
     sem,
 ):
     lon = lax.axis_index("lon")
-    quarter = base0.shape[1]
     rows = base0.shape[0]
     inputs = (owner_hbm, sender_hbm, node_hbm, feat_hbm, halo_hbm, from_hbm, to_hbm)
     held = (owner_ref, sender_ref, node_ref, feat_ref, halo_ref, from_ref, to_ref)
@@ -117,13 +112,6 @@
 
     for j, base in enumerate((base0, base1, base2, base3)):
         bring(latent.at[pl.ds(pl.multiple_of((lon ^ j) * rows, rows), rows), :], base)
-    for w_in, w_out, pack in ((node_in, node_out, node_pack), (last_in, last_out, last_pack)):
-        depth = w_in.shape[0]
-        bring(w_in, pack.at[pl.ds(0, depth), :])
-        for m in range(w_out.shape[1] // quarter):
-            bring(w_out.at[:, pl.ds(m * quarter, quarter)], pack.at[pl.ds(depth + m * quarter, quarter), :])
-    bring(edge_in, edge_pack.at[pl.ds(0, edge_in.shape[0]), :])
-    bring(edge_out, edge_pack.at[pl.ds(edge_in.shape[0], edge_out.shape[0]), :])
     for copy in early + late:
         copy.start()
     for copy in early:
@@ -157,7 +145,7 @@
         spot = lax.broadcasted_iota(I32, (CHUNK, edges), 0) + i * CHUNK
         perm = jnp.where(spot == place, 1.0, 0.0).astype(BF16)
         moved = dot(meta, perm, 1, 1)
-        meta_ref[i * CHUNK : (i + 1) * CHUNK, :] = jnp.transpose(moved).astype(BF16)
+        meta_ref[:, i * CHUNK : (i + 1) * CHUNK] = moved.astype(BF16)
         key = moved[4:5] * float(mesh_rows) + moved[2:3] * float(SPLIT) + moved[3:4]
         for k in range(CHUNK // LANES):
             row = i * (CHUNK // LANES) + k
@@ -183,12 +171,12 @@
         ).astype(BF16)
     rows = rows_ref[...]
     table = dot(rows, win[...]).astype(BF16)
-    edges = meta_ref.shape[0]
+    edges = meta_ref.shape[1]
     block = CHUNK
     for i in range(edges // block):
         at = slice(i * block, (i + 1) * block)
-        meta = meta_ref[at, :]
-        places = meta[:, 0:2].astype(F32)
+        places = jnp.transpose(meta_ref[:, at].astype(F32))
+        meta = places.astype(BF16)
         sender = (places[:, 0:1] * float(SPLIT) + places[:, 1:2]).astype(I32)
         source = lax.broadcasted_iota(I32, (block, rows.shape[0]), 1)
         pick = jnp.where(source == sender, 1.0, 0.0).astype(BF16)
@@ -197,11 +185,10 @@
         out_ref[at, :] = normed(raw, gain_ref[...], bias_ref[1:2, :], 1).astype(BF16)
 
 
-def sums_kernel(mesh_rows, keep, start_a, start_b, table_a, table_b, msg_a, msg_b, x_ref, y_ref):
+def sums_kernel(mesh_rows, cap, keep, start_a, start_b, table_a, table_b, msg_a, msg_b, x_ref, y_ref):
     edges, _ = msg_a.shape
     key_rows = edges // LANES
     tall = y_ref.shape[1]
-    parts = 2 * tall
     quarter = mesh_rows // 4
     half = quarter // 2
     lat = lax.axis_index("lat")
@@ -209,7 +196,7 @@
     lon = lax.axis_index("lon")
     mine = lon * quarter
     other = (lon ^ 2) * quarter
-    ready = min(key_rows, WINDOW)
+    ready = min(key_rows, (cap + 2 * LANES - 2) // LANES)
     sets = ((start_a, table_a, msg_a), (start_b, table_b, msg_b))
 
     def sums(part, bases):
@@ -219,30 +206,20 @@
         for k in range(1, len(bases)):
             node = jnp.where(row >= k * half, row + (bases[k] - k * half + part * mesh_rows), node)
 
-        def term(at, count, table, msg):
+        total = None
+        for start, table, msg in sets:
+            at = jnp.minimum(start[key_rows + part, 0] // LANES, key_rows - ready)
             pick = jnp.concatenate(
-                [jnp.where(node == table[pl.ds(at + k, 1), :], 1.0, 0.0).astype(BF16) for k in range(count)], 1
+                [jnp.where(node == table[pl.ds(at + k, 1), :], 1.0, 0.0).astype(BF16) for k in range(ready)], 1
             )
-            return dot(pick, msg[pl.ds(pl.multiple_of(at * LANES, LANES), count * LANES), :])
-
-        total = None
-        later = []
-        for start, table, msg in sets:
-            begin = start[key_rows + part, 0]
-            following = jnp.minimum(part + 1, parts - 1)
-            end = jnp.where(part + 1 < parts, start[key_rows + following, 0], edges)
-            at = jnp.minimum(begin // LANES, key_rows - ready)
-            now = term(at, ready, table, msg)
-            total = now if total is None else total + now
-            later.append((at + ready, (end + LANES - 1) // LANES, table, msg))
-        for at, end, table, msg in later:
-            total = lax.fori_loop(at, end, lambda i, t, table=table, msg=msg: t + term(i, 1, table, msg), total)
+            term = dot(pick, msg[pl.ds(pl.multiple_of(at * LANES, LANES), ready * LANES), :])
+            total = term if total is None else total + term
         return total.astype(BF16)
 
     near_low = low if keep else 1 - low
     base = mine if keep else other
 
-    @pl.loop(0, tall)
+    @pl.loop(0, tall, unroll=2)
     def _(i):
         both = sums(2 * i + near_low, (base, mine + half, other + half))
         one = sums(2 * i + 1 - near_low, (base,))
@@ -258,7 +235,7 @@
     edges, width = messages[0].shape
     out = jax.ShapeDtypeStruct((2, tall, mesh_rows // 8, width), BF16)
     return call(
-        functools.partial(sums_kernel, mesh_rows, keep), [out, out], [SMEM] * 2 + [VMEM] * 4, 2 * edges * mesh_rows * width
+        functools.partial(sums_kernel, mesh_rows, 2 * edges // lat_count, keep), [out, out], [SMEM] * 2 + [VMEM] * 4, 2 * edges * mesh_rows * width
     )(*tables, *tables, *messages)
 
 
@@ -272,19 +249,17 @@
 def node_kernel(n_base, n_agg, n_out, *refs):
     bases, refs = refs[:n_base], refs[n_base:]
     aggs, refs = refs[:n_agg], refs[n_agg:]
-    bias_ref, gain_ref, w0, w1, w2, w3 = refs[:6]
-    outs = refs[6 : 6 + n_out]
-    base, win, wout = refs[6 + n_out :]
+    bias_ref, gain_ref = refs[:2]
+    weights = refs[2:10]
+    outs = refs[10 : 10 + n_out]
+    base, win, wout = refs[10 + n_out :]
     width = base.shape[1]
-    quarter = w0.shape[1]
+    quarter = weights[0].shape[1]
     lon = lax.axis_index("lon")
     biases = []
-    for j, w in enumerate((w0, w1, w2, w3)):
-        win[:, j * quarter : (j + 1) * quarter] = w[0 : 2 * width, :]
-        for m in range(width // quarter):
-            wout[j * quarter : (j + 1) * quarter, m * quarter : (m + 1) * quarter] = w[
-                2 * width + m * quarter : 2 * width + (m + 1) * quarter, :
-            ]
+    for j in range(4):
+        win[:, j * quarter : (j + 1) * quarter] = weights[j][...]
+        wout[j * quarter : (j + 1) * quarter, :] = weights[4 + j][...]
         at = pl.ds(pl.multiple_of((lon ^ j) * quarter, quarter), quarter)
         biases.append(bias_ref[0:1, at])
         if n_base > 1:
@@ -331,17 +306,18 @@
     lane = lax.broadcasted_iota(I32, (index_ref.shape[0], table_ref.shape[0]), 1)
     pick = jnp.where(lane == index_ref[...], 1.0, 0.0).astype(BF16)
     held[...] = dot(pick, table_ref[...])
-    half = outs[0].shape[0]
+    cap = outs[0].shape[0]
     core = lax.rem(lax.axis_index("lon"), 2)
-    for j, out in enumerate(outs):
-        at = (lax.axis_index("lat") ^ j) * (2 * half)
-        rows = held[pl.ds(pl.multiple_of(at, 2 * half), 2 * half), :]
-        out[...] = jnp.where(core == 0, rows[:half], rows[half:]).astype(BF16)
-
-
-def pack_kernel(*refs):
+    for out, (flip0, flip1) in zip(outs, turns(2 * len(outs))):
+        at = (lax.axis_index("lat") ^ jnp.where(core == 0, flip0, flip1)) * cap
+        out[...] = held[pl.ds(pl.multiple_of(at, cap), cap), :].astype(BF16)
+
+
+def pack_kernel(own_ref, *refs):
     out_ref = refs[-1]
-    out_ref[...] = jnp.concatenate([ref[...].astype(F32) for ref in refs[:-1]], 0).astype(BF16)
+    core = lax.rem(lax.axis_index("lon"), 2)
+    last = jnp.where(core == 0, own_ref[...].astype(F32), refs[-2][...].astype(F32))
+    out_ref[...] = jnp.concatenate([ref[...].astype(F32) for ref in refs[:-2]] + [last], 0).astype(BF16)
 
 
 def near_kernel(edge_hbm, mid_ref, ends_ref, bias_ref, w0, w1, w2, w3, out_ref, win, edge_ref, sem):
@@ -356,7 +332,7 @@
     lon = lax.axis_index("lon")
     biases = []
     for j, w in enumerate((w0, w1, w2, w3)):
-        win[:, j * quarter : (j + 1) * quarter] = w[0 : 3 * width, :]
+        win[:, j * quarter : (j + 1) * quarter] = w[...]
         at = pl.ds(pl.multiple_of((lon ^ j) * quarter, quarter), quarter)
         biases.append(bias_ref[0:1, at])
     bias = jnp.concatenate(biases, 1)
@@ -373,23 +349,26 @@
         out_ref[at, :] = pre + dot(edge_ref[at, :], win[0:width, :])
 
 
-def far_kernel(halo_cap, edge_hbm, pre_ref, halo_a, halo_b, ends_ref, receiver_ref, bias_ref, gain_ref, w0, w1, w2, w3, new_ref, away_ref, keep_ref, pass_ref, total, win, wout, edge_ref, sem):
+def far_kernel(halo_cap, edge_hbm, pre_ref, halo_a, halo_b, ends_ref, receiver_ref, bias_ref, gain_ref, w0, w1, w2, w3, v0, v1, v2, v3, new_ref, away_ref, keep_ref, pass_ref, total, win, wout, edge_ref, sem):
     load = pltpu.make_async_copy(edge_hbm, edge_ref, sem)
     load.start()
     width = halo_a.shape[1]
     quarter = w0.shape[1]
     lon = lax.axis_index("lon")
-    for j, w in enumerate((w0, w1, w2, w3)):
+    for j, (w, v) in enumerate(((w0, v0), (w1, v1), (w2, v2), (w3, v3))):
         win[:, j * quarter : (j + 1) * quarter] = w[width : 2 * width, :]
-        wout[:, j * quarter : (j + 1) * quarter] = w[3 * width : 4 * width, :]
+        wout[:, j * quarter : (j + 1) * quarter] = v[...]
     rows = halo_a.shape[0]
     mesh_rows = total.shape[0]
     sent = [dot(h[...], win[...]).astype(BF16) for h in (halo_a, halo_b)]
-    half = halo_cap // 2
     lane = lax.broadcasted_iota(I32, (1, rows), 1)
     core = lax.rem(lon, 2)
-    source = (lane // half) ^ lax.axis_index("lat")
-    names = [mesh_rows + source * halo_cap + lane % half + c * half for c in (core, 1 - core)]
+    lat = lax.axis_index("lat")
+    flips = [jnp.zeros_like(lane), jnp.zeros_like(lane)]
+    for j, pair in enumerate(turns(2 * (rows // halo_cap))):
+        flips = [jnp.where(lane // halo_cap == j, flip, before) for flip, before in zip(pair, flips)]
+    flips = [jnp.where(core == 0, a, b) for a, b in (flips, flips[::-1])]
+    names = [mesh_rows + (lat ^ flip) * halo_cap + lane % halo_cap for flip in flips]
     edges = edge_ref.shape[0]
     block = 256
     for i in range(edges // block):
@@ -477,28 +456,26 @@
     enc_out = spread(enc_edge_out)
     small = (grid_owner.reshape(1, edges), grid_sender[None, :], grid_node[None, :], grid_feat)
     small = small + (halo_send, mesh_sender[None, :], mesh_receiver[None, :])
-    deep = 2 * width + 4 * enc_node_out.shape[0]
-    copies = 4 + 2 * (1 + width // quarter) + 2
     table, meta, ends, asked, *rest = call(
         functools.partial(open_kernel, lat_count, mesh_rows),
         [
             like(edges // LANES + lat_count, LANES, I32),
-            like(edges, META),
+            like(META, edges),
             like(local_edges, 8, I32),
             like(listed, 1, I32),
         ]
-        + [like(node_rows, quarter)] * 4
-        + [like(deep, quarter), like(4 * width, quarter), like(deep, quarter)],
-        [HBM] * 14,
+        + [like(node_rows, quarter)] * 4,
+        [HBM] * 8,
         2 * META * edges * edges * 8,
         [pltpu.VMEM(v.shape, v.dtype) for v in small]
-        + [pltpu.SemaphoreType.DMA((len(small),)), pltpu.SemaphoreType.DMA((copies,))],
+        + [pltpu.SemaphoreType.DMA((len(small),)), pltpu.SemaphoreType.DMA((4,))],
         FULL,
-    )(*small, mesh_latent, enc_node_in, enc_node_out, proc_edge_in, proc_edge_out, proc_node_in, proc_node_out)
+    )(*small, mesh_latent)
     bases = tuple(rest[j] if j == 0 else hop(rest[j], "lon", j) for j in range(4))
-    node_pieces = spread(rest[4])
-    edge_pieces = spread(rest[5])
-    last_pieces = spread(rest[6])
+    node_pieces = spread(enc_node_in) + spread(enc_node_out)
+    edge_in = spread(proc_edge_in)
+    edge_out = spread(proc_edge_out)
+    last_pieces = spread(proc_node_in) + spread(proc_node_out)
 
     tables = (table, hop(table, "lon", 1))
     message = call(
@@ -520,20 +497,30 @@
     joined = call(join_kernel, [like(node_rows, width)] * tall, [VMEM] * 6, 1 << 20)(
         keep_x, got_x, got_xy, keep_y, got_y, got_yx
     )
-    partials = tuple(joined[j] if j == 0 else hop(joined[j], "lat", 2 * j) for j in range(tall))
+    far_first = sorted(range(1, tall), key=lambda j: (j < tall // 2, j))
+    partials = (joined[0], *[hop(joined[j], "lat", 2 * j) for j in far_first])
 
     mid = node_network(bases, partials, enc_node_bias, enc_node_gain, node_pieces, 1)
     mid_all = lax.all_gather(mid, "lon", axis=0, tiled=True)
 
-    half_cap = halo_cap // 2
     picked = call(
         pick_kernel,
-        [like(half_cap, width)] * lat_count,
+        [like(halo_cap, width)] * tall,
         [VMEM] * 2,
         2 * listed * mesh_rows * width,
         [pltpu.VMEM((listed, width), F32)],
     )(asked, mid_all)
-    arrived = [picked[j] if j == 0 else hop(picked[j], "lat", j) for j in range(lat_count)]
+
+    def halo_hop(j, flips):
+        pairs = []
+        for i in range(lat_count):
+            for l in range(4):
+                to = i ^ flips[l % 2]
+                if to != i:
+                    pairs.append((i * 4 + l, to * 4 + l))
+        return lax.ppermute(picked[j], ("lat", "lon"), pairs)
+
+    arrived = [halo_hop(j, flips) for j, flips in enumerate(turns(lat_count))]
     near = call(
         near_kernel,
         like(local_edges, width, F32),
@@ -544,8 +531,8 @@
             pltpu.VMEM((local_edges, width), BF16),
             pltpu.SemaphoreType.DMA((local_edges // CHUNK,)),
         ],
-    )(mesh_edge, mid_all, ends, proc_edge_bias, *edge_pieces)
-    packed = call(pack_kernel, like(listed // 2, width), [VMEM] * lat_count, 1 << 20)(*arrived)
+    )(mesh_edge, mid_all, ends, proc_edge_bias, *edge_in)
+    packed = call(pack_kernel, like(listed // 2, width), [VMEM] * (tall + 1), 1 << 20)(picked[-1], *arrived)
     halves = (packed, hop(packed, "lon", 1))
 
     edge_update, away, kept, passed = call(
@@ -556,7 +543,7 @@
             like(node_rows, width),
             like(node_rows, width),
         ],
-        [HBM] + [VMEM] * 11,
+        [HBM] + [VMEM] * 15,
         2 * local_edges * width * (width + listed + mesh_rows),
         [
             pltpu.VMEM((mesh_rows, width), BF16),
@@ -565,7 +552,7 @@
             pltpu.VMEM((local_edges, width), BF16),
             pltpu.SemaphoreType.DMA,
         ],
-    )(mesh_edge, near, *halves, ends, mesh_receiver[None, :], proc_edge_bias, proc_edge_gain[None, :], *edge_pieces)
+    )(mesh_edge, near, *halves, ends, mesh_receiver[None, :], proc_edge_bias, proc_edge_gain[None, :], *edge_in, *edge_out)
 
     came = hop(away, "lon", 1)
     got = hop(plus(passed, came[1]), "lon", 2)

time: 140 us -> 130 us (0.929)
  waiting for transfers between devices: 63.7 us -> 58.9 us
  Pallas kernels: 29.2 us -> 26.4 us
    ppermute x40 -> x42, waiting for transfers between devices: 63.7 us -> 55.3 us  [hop(): return lax.ppermute(values, axis, [(i, i ^ flip) for i in range(size)])]
    ppermute x40 -> x42, starting transfers between devices: 36.6 us -> 28.6 us  [hop(): return lax.ppermute(values, axis, [(i, i ^ flip) for i in range(size)])]
    ppermute x0 -> x4, starting transfers between devices: none -> 6.75 us  [halo_hop(): return lax.ppermute(picked[j], ('lat', 'lon'), pairs)]
    ppermute x0 -> x4, waiting for transfers between devices: none -> 3.67 us  [halo_hop(): return lax.ppermute(picked[j], ('lat', 'lon'), pairs)]
    pallas_call x4, Pallas kernels: 9.09 us -> 7.34 us  [the longest x2 6.8 us: node_sums(): call(functools.partial(sums_kernel, mesh_rows, 2 * edges // lat_count, ke...]
  transfers between devices with their start and end apart: 40 -> 46, of which waited for: 18 -> 20; matrix products, arithmetic and copies ran while one was open for 0% -> 0% of each run, Pallas kernels for 13% -> 13%
where the time goes in v3:
time: 130 us; the launch traced here: 129 us
  waiting for transfers between devices  58.9 us (45%)
  starting transfers between devices  35.3 us (27%)
  Pallas kernels  26.4 us (20%)
  blocking collectives  6.53 us (5%)
    ppermute x42, waiting for transfers between devices, hop(): return lax.ppermute(values, axis, [(i, i ^ flip) for i in range(size)])  55.3 us
    ppermute x42, starting transfers between devices, hop(): return lax.ppermute(values, axis, [(i, i ^ flip) for i in range(size)])  28.6 us
    pallas_call x2, Pallas kernels, node_sums(): call(functools.partial(sums_kernel, mesh_rows, 2 * edges // lat_count, ke...  6.8 us
    ppermute x4, starting transfers between devices, halo_hop(): return lax.ppermute(picked[j], ('lat', 'lon'), pairs)  6.75 us
    all_gather x1, blocking collectives, local(): mid_all = lax.all_gather(mid, 'lon', axis=0, tiled=True)  6.53 us
    pallas_call x1, Pallas kernels, local(): call(functools.partial(open_kernel, lat_count, mesh_rows), [like(edges //...  4.9 us
    pallas_call x1, Pallas kernels, local(): call(functools.partial(message_kernel, grid_feat.shape[0]), like(edges, w...  4.76 us
    pallas_call x1, Pallas kernels, local(): call(functools.partial(far_kernel, halo_cap), [like(local_edges, width),...  3.75 us
  transfers between devices with their start and end apart: 46, of which 20 were waited for; matrix products, arithmetic and copies ran while one was open for 0% of the time, Pallas kernels for 13%

profile of v3, /device:TPU:0, one launch (start us, length us, event | category | flops | bytes accessed | tf_op | source)
XLA Modules:
  0.0 129.4 jit_solution(12881581161184145283)
XLA Ops:
  0.7 3.0 %collective-permute-start.5 = (bf16[512,128]{1,0:T(8,128)(2,1)}, bf16[512,128]{1,0:T(8,128)(2,1)S(1)}, u32[]{:S(2)}, u32[]{:S(2)}) collective-permute-start(bf16[512,128]{1,0:T(8,128)(2,1)} %w0.3), channel_id=1, source_target_pairs={{0,2},{1,3},{2,0},{3,1},{4,6},{5,7},{6,4},{7,5},{8,10},{9,11},{10,... | collective-permute-start | bytes 393224 | tf_op jit(solution)/shard_map/ppermute | solution.py:449
  4.3 4.0 %collective-permute-done.5.w2 = bf16[512,128]{1,0:T(8,128)(2,1)S(1)} collective-permute-done((bf16[512,128]{1,0:T(8,128)(2,1)}, bf16[512,128]{1,0:T(8,128)(2,1)S(1)}, u32[]{:S(2)}, u32[]{:S(2)}) %collective-permute-start.5) | collective-permute-done | bytes 131104 | tf_op jit(solution)/shard_map/ppermute | solution.py:449
  8.3 2.0 %collective-permute-done.8.v2 = bf16[512,128]{1,0:T(8,128)(2,1)S(1)} collective-permute-done((bf16[512,128]{1,0:T(8,128)(2,1)}, bf16[512,128]{1,0:T(8,128)(2,1)S(1)}, u32[]{:S(2)}, u32[]{:S(2)}) %collective-permute-start.8) | collective-permute-done | bytes 131104 | tf_op jit(solution)/shard_map/ppermute | solution.py:449
  10.2 4.9 %shard_map.266 = (s32[24,128]{1,0:T(8,128)}, bf16[16,2048]{1,0:T(8,128)(2,1)}, s32[1024,8]{1,0:T(8,128)}, s32[512,1]{1,0:T(8,128)}, bf16[128,128]{1,0:T(8,128)(2...) custom-call(s32[1,2048]{1,0:T(1,128)} %bitcast.24, s32[1,2048]{1,0:T(1,128)} %bitcast.25, ...), custom_call_target="tpu_custom_call" | custom-call | flops 1073741824 | bytes 4194304 | tf_op jit(solution)/shard_map/pallas_call | solution.py:459
  16.1 4.8 %shard_map.267.msg_a = bf16[2048,512]{1,0:T(8,128)(2,1)S(1)} custom-call(bf16[512,512]{1,0:T(8,128)(2,1)S(1)} %copy-done.17, bf16[16,2048]{1,0:T(8,128)(2,1)S(1)} %copy-done.24, bf16[4,512]{1,0:T(4,128)(2,1)S(1)} %copy-done.20, f32[2,512]{1,0:T(2,128)S(1)} %copy-done.21, f32[1,512]{1,0:T(1,128)S(1)} %bitcast.23, bf16[512,128]{1,0:T(8,128)(2,1)S(1)} %copy-done.18, ...), custom_call_target="tpu_custom_call" | custom-call | flops 2147483648 | bytes 4194304 | tf_op jit(solution)/shard_map/pallas_call | solution.py:481
  21.5 3.7 %collective-permute-done.3.start_b.table_b = s32[24,128]{1,0:T(8,128)S(1)} collective-permute-done((s32[24,128]{1,0:T(8,128)S(1)}, s32[24,128]{1,0:T(8,128)S(1)}, u32[]{:S(2)}, u32[]{:S(2)}) %collective-permute-start.3) | collective-permute-done | bytes 12320 | tf_op jit(solution)/shard_map/ppermute | solution.py:449
  25.2 3.4 %shard_map.269 = (bf16[2,4,64,512]{3,2,1,0:T(8,128)(2,1)S(1)}, bf16[2,4,64,512]{3,2,1,0:T(8,128)(2,1)S(1)}) custom-call(s32[24,128]{1,0:T(8,128)S(1)} %copy-done.5, s32[24,128]{1,0:T(8,128)S(1)} %collective-permute-done.3.start_b.table_b, s32[24,128]{1,0:T(8,128)S(1)} %copy-done.5, s32[24,128]{1,0:T(8,128)S(1)} %collective-permute-done.3.start_b.table_b, ...), custom_call_target="tpu_custom_call" | custom-call | flops 1073741824 | bytes 4194304 | tf_op jit(solution)/shard_map/pallas_call | solution.py:237
  28.6 1.9 %collective-permute-start.13 = (bf16[2,4,64,512]{3,2,1,0:T(8,128)(2,1)S(1)}, bf16[2,4,64,512]{3,2,1,0:T(8,128)(2,1)S(1)}, u32[]{:S(2)}, u32[]{:S(2)}) collective-permute-start(bf16[2,4,64,512]{3,2,1,0:T(8,128)(2,1)S(1)} %get-tuple-element.39), channel_id=1, source_target_pairs={{0,4},{4,0},{8,12},{12,8},{16,20},{20,16},{24,28},{28,24},{1,5},{5... | collective-permute-start | bytes 1572872 | tf_op jit(solution)/shard_map/ppermute | solution.py:449
  30.5 1.5 %collective-permute-start.11 = (bf16[2,4,64,512]{3,2,1,0:T(8,128)(2,1)S(1)}, bf16[2,4,64,512]{3,2,1,0:T(8,128)(2,1)S(1)}, u32[]{:S(2)}, u32[]{:S(2)}) collective-permute-start(bf16[2,4,64,512]{3,2,1,0:T(8,128)(2,1)S(1)} %get-tuple-element.37), channel_id=1, source_target_pairs={{0,2},{1,3},{2,0},{3,1},{4,6},{5,7},{6,4},{7,5},{8,10},{9,11},{10,... | collective-permute-start | bytes 1572872 | tf_op jit(solution)/shard_map/ppermute | solution.py:449
  32.6 3.4 %shard_map.268 = (bf16[2,4,64,512]{3,2,1,0:T(8,128)(2,1)S(1)}, bf16[2,4,64,512]{3,2,1,0:T(8,128)(2,1)S(1)}) custom-call(s32[24,128]{1,0:T(8,128)S(1)} %copy-done.5, s32[24,128]{1,0:T(8,128)S(1)} %collective-permute-done.3.start_b.table_b, s32[24,128]{1,0:T(8,128)S(1)} %copy-done.5, s32[24,128]{1,0:T(8,128)S(1)} %collective-permute-done.3.start_b.table_b, ...), custom_call_target="tpu_custom_call" | custom-call | flops 1073741824 | bytes 4194304 | tf_op jit(solution)/shard_map/pallas_call | solution.py:237
  36.0 6.9 %collective-permute-done.13.got_y = bf16[2,4,64,512]{3,2,1,0:T(8,128)(2,1)S(1)} collective-permute-done((bf16[2,4,64,512]{3,2,1,0:T(8,128)(2,1)S(1)}, bf16[2,4,64,512]{3,2,1,0:T(8,128)(2,1)S(1)}, u32[]{:S(2)}, u32[]{:S(2)}) %collective-permute-start.13) | collective-permute-done | bytes 524320 | tf_op jit(solution)/shard_map/ppermute | solution.py:449
  43.0 1.8 %collective-permute-start.14 = (bf16[4,64,512]{2,1,0:T(8,128)(2,1)S(1)}, bf16[4,64,512]{2,1,0:T(8,128)(2,1)S(1)}, u32[]{:S(2)}, u32[]{:S(2)}) collective-permute-start(bf16[4,64,512]{2,1,0:T(8,128)(2,1)S(1)} %fusion.1), channel_id=1, source_target_pairs={{0,2},{1,3},{2,0},{3,1},{4,6},{5,7},{6,4},{7,5},{8,10},{9,11},{10,... | collective-permute-start | bytes 786440 | tf_op jit(solution)/shard_map/ppermute | solution.py:449
  47.5 1.2 collective-permute-done.refs_1_
  49.7 9.5 %collective-permute-done.1.refs_2_ = bf16[128,128]{1,0:T(8,128)(2,1)S(1)} collective-permute-done((bf16[128,128]{1,0:T(8,128)(2,1)S(1)}, bf16[128,128]{1,0:T(8,128)(2,1)S(1)}, u32[]{:S(2)}, u32[]{:S(2)}) %collective-permute-start.1) | collective-permute-done | bytes 32800 | tf_op jit(solution)/shard_map/ppermute | solution.py:449
  59.6 3.3 %collective-permute-done.2.refs_3_ = bf16[128,128]{1,0:T(8,128)(2,1)S(1)} collective-permute-done((bf16[128,128]{1,0:T(8,128)(2,1)S(1)}, bf16[128,128]{1,0:T(8,128)(2,1)S(1)}, u32[]{:S(2)}, u32[]{:S(2)}) %collective-permute-start.2) | collective-permute-done | bytes 32800 | tf_op jit(solution)/shard_map/ppermute | solution.py:449
  62.9 1.2 collective-permute-start.25
  65.8 2.6 %collective-permute-start.15 = (bf16[128,512]{1,0:T(8,128)(2,1)S(1)}, bf16[128,512]{1,0:T(8,128)(2,1)S(1)}, u32[]{:S(2)}, u32[]{:S(2)}) collective-permute-start(bf16[128,512]{1,0:T(8,128)(2,1)S(1)} %get-tuple-element.41), channel_id=1, source_target_pairs={{0,16},{4,20},{8,24},{12,28},{16,0},{20,4},{24,8},{28,12},{1,17},{... | collective-permute-start | bytes 393224 | tf_op jit(solution)/shard_map/ppermute | solution.py:449
  68.4 1.3 %collective-permute-start.16 = (bf16[128,512]{1,0:T(8,128)(2,1)S(1)}, bf16[128,512]{1,0:T(8,128)(2,1)S(1)}, u32[]{:S(2)}, u32[]{:S(2)}) collective-permute-start(bf16[128,512]{1,0:T(8,128)(2,1)S(1)} %get-tuple-element.42), channel_id=1, source_target_pairs={{0,24},{4,28},{8,16},{12,20},{16,8},{20,12},{24,0},{28,4},{1,25},{... | collective-permute-start | bytes 393224 | tf_op jit(solution)/shard_map/ppermute | solution.py:449
  70.1 4.0 %collective-permute-done.25.w2 = bf16[1536,128]{1,0:T(8,128)(2,1)S(1)} collective-permute-done((bf16[1536,128]{1,0:T(8,128)(2,1)S(1)}, bf16[1536,128]{1,0:T(8,128)(2,1)S(1)}, u32[]{:S(2)}, u32[]{:S(2)}) %collective-permute-start.25) | collective-permute-done | bytes 393248 | tf_op jit(solution)/shard_map/ppermute | solution.py:449
  74.6 4.2 %collective-permute-done.15.refs_5_ = bf16[128,512]{1,0:T(8,128)(2,1)S(1)} collective-permute-done((bf16[128,512]{1,0:T(8,128)(2,1)S(1)}, bf16[128,512]{1,0:T(8,128)(2,1)S(1)}, u32[]{:S(2)}, u32[]{:S(2)}) %collective-permute-start.15) | collective-permute-done | bytes 131104 | tf_op jit(solution)/shard_map/ppermute | solution.py:449
  80.3 6.5 %all_gather.3.mid_ref.table_ref = bf16[512,512]{1,0:T(8,128)(2,1)S(1)} all-gather(bf16[128,512]{1,0:T(8,128)(2,1)S(1)} %shard_map.271.refs_0_), channel_id=1, replica_groups=mesh['lat'=8,'lon'=4] {'lon'}, dimensions={0}, use_global_device_ids=true | all-gather | bytes 655360 | tf_op jit(solution)/shard_map/all_gather | solution.py:504
  87.4 3.4 %collective-permute-start.27 = (bf16[64,512]{1,0:T(8,128)(2,1)S(1)}, bf16[64,512]{1,0:T(8,128)(2,1)S(1)}, u32[]{:S(2)}, u32[]{:S(2)}) collective-permute-start(bf16[64,512]{1,0:T(8,128)(2,1)S(1)} %get-tuple-element.47), channel_id=1, source_target_pairs={{0,28},{1,25},{2,30},{3,27},{4,24},{5,29},{6,26},{7,31},{8,20},{9,... | collective-permute-start | bytes 196616 | tf_op jit(solution)/shard_map/ppermute | solution.py:521
  90.7 1.2 collective-permute-start.28
  91.9 1.4 %collective-permute-start.29 = (bf16[64,512]{1,0:T(8,128)(2,1)S(1)}, bf16[64,512]{1,0:T(8,128)(2,1)S(1)}, u32[]{:S(2)}, u32[]{:S(2)}) collective-permute-start(bf16[64,512]{1,0:T(8,128)(2,1)S(1)} %get-tuple-element.49), channel_id=1, source_target_pairs={{0,12},{1,9},{2,14},{3,11},{4,8},{5,13},{6,10},{7,15},{8,4},{9,1},... | collective-permute-start | bytes 196616 | tf_op jit(solution)/shard_map/ppermute | solution.py:521
  95.3 2.5 %collective-permute-done.28.refs_1_ = bf16[64,512]{1,0:T(8,128)(2,1)S(1)} collective-permute-done((bf16[64,512]{1,0:T(8,128)(2,1)S(1)}, bf16[64,512]{1,0:T(8,128)(2,1)S(1)}, u32[]{:S(2)}, u32[]{:S(2)}) %collective-permute-start.28) | collective-permute-done | bytes 65568 | tf_op jit(solution)/shard_map/ppermute | solution.py:521
  97.8 1.2 collective-permute-start.33
  99.6 3.7 %collective-permute-done.33.v2 = bf16[512,128]{1,0:T(8,128)(2,1)S(1)} collective-permute-done((bf16[512,128]{1,0:T(8,128)(2,1)S(1)}, bf16[512,128]{1,0:T(8,128)(2,1)S(1)}, u32[]{:S(2)}, u32[]{:S(2)}) %collective-permute-start.33) | collective-permute-done | bytes 131104 | tf_op jit(solution)/shard_map/ppermute | solution.py:449
  104.4 3.0 %shard_map.272.pre_ref = f32[1024,512]{1,0:T(8,128)S(1)} custom-call(bf16[1024,512]{1,0:T(8,128)(2,1)S(1)} %copy-done, bf16[512,512]{1,0:T(8,128)(2,1)S(1)} %all_gather.3.mid_ref.table_ref, s32[1024,8]{1,0:T(8,128)S(1)} %copy-done.1, f32[2,512]{1,0:T(2,128)S(1)} %copy-done.13, bf16[1536,128]{1,0:T(8,128)(2,1)S(1)} %copy-done.2, ...), custom_call_target="tpu_custom_call" | custom-call | flops 1610612736 | bytes 4194304 | tf_op jit(solution)/shard_map/pallas_call | solution.py:524
  107.6 3.7 %shard_map.275 = (bf16[1024,512]{1,0:T(8,128)(2,1)}, bf16[2,128,512]{2,1,0:T(8,128)(2,1)S(1)}, bf16[128,512]{1,0:T(8,128)(2,1)S(1)}, bf16[128,512]{1,0:T(8,128)(2,1)S(1)}) custom-call(bf16[1024,512]{1,0:T(8,128)(2,1)S(1)} %copy-done, f32[1024,512]{1,0:T(8,128)S(1)} %shard_map.272.pre_ref, bf16[256,512]{1,0:T(8,128)(2,1)S(1)} %shard_map.274.halo_a, ...), custom_call_target="tpu_custom_call" | custom-call | flops 1610612736 | bytes 4194304 | tf_op jit(solution)/shard_map/pallas_call | solution.py:538
  113.3 4.1 %collective-permute-done.41.refs_12_ = bf16[128,512]{1,0:T(8,128)(2,1)S(1)} collective-permute-done((bf16[128,512]{1,0:T(8,128)(2,1)S(1)}, bf16[128,512]{1,0:T(8,128)(2,1)S(1)}, u32[]{:S(2)}, u32[]{:S(2)}) %collective-permute-start.41) | collective-permute-done | bytes 131104 | tf_op jit(solution)/shard_map/ppermute | solution.py:449
  119.1 4.3 %collective-permute-done.36.refs_3_ = bf16[128,512]{1,0:T(8,128)(2,1)S(1)} collective-permute-done((bf16[128,512]{1,0:T(8,128)(2,1)S(1)}, bf16[128,512]{1,0:T(8,128)(2,1)S(1)}, u32[]{:S(2)}, u32[]{:S(2)}) %collective-permute-start.36) | collective-permute-done | bytes 131104 | tf_op jit(solution)/shard_map/ppermute | solution.py:449
  126.2 2.1 %collective-permute-done.44.refs_2_ = bf16[128,128]{1,0:T(8,128)(2,1)S(1)} collective-permute-done((bf16[128,128]{1,0:T(8,128)(2,1)S(1)}, bf16[128,128]{1,0:T(8,128)(2,1)S(1)}, u32[]{:S(2)}, u32[]{:S(2)}) %collective-permute-start.44) | collective-permute-done | bytes 32800 | tf_op jit(solution)/shard_map/ppermute | solution.py:449
  (132 shorter events, 22.7 us)
Async XLA Ops:
  0.7 7.6 %collective-permute-start.5 = (bf16[512,128]{1,0:T(8,128)(2,1)}, bf16[512,128]{1,0:T(8,128)(2,1)S(1)}, u32[]{:S(2)}, u32[]{:S(2)}) collective-permute-start(bf16[512,128]{1,0:T(8,128)(2,1)} %w0.3), channel_id=1, source_target_pairs={{0,2},{1,3},{2,0},{3,1},{4,6},{5,7},{6,4},{7,5},{8,10},{9,11},{10,... | collective-permute-start | bytes 393224 | tf_op jit(solution)/shard_map/ppermute | solution.py:449
  3.7 6.5 %collective-permute-start.8 = (bf16[512,128]{1,0:T(8,128)(2,1)}, bf16[512,128]{1,0:T(8,128)(2,1)S(1)}, u32[]{:S(2)}, u32[]{:S(2)}) collective-permute-start(bf16[512,128]{1,0:T(8,128)(2,1)} %v0.2), channel_id=1, source_target_pairs={{0,2},{1,3},{2,0},{3,1},{4,6},{5,7},{6,4},{7,5},{8,10},{9,11},{10,... | collective-permute-start | bytes 393224 | tf_op jit(solution)/shard_map/ppermute | solution.py:449
  3.8 11.3 %collective-permute-start.4 = (bf16[512,128]{1,0:T(8,128)(2,1)}, bf16[512,128]{1,0:T(8,128)(2,1)S(1)}, u32[]{:S(2)}, u32[]{:S(2)}) collective-permute-start(bf16[512,128]{1,0:T(8,128)(2,1)} %w0.3), channel_id=1, source_target_pairs={{0,1},{1,0},{2,3},{3,2},{4,5},{5,4},{6,7},{7,6},{8,9},{9,8},{10,11... | collective-permute-start | bytes 393224 | tf_op jit(solution)/shard_map/ppermute | solution.py:449
  3.8 11.4 %collective-permute-start.7 = (bf16[512,128]{1,0:T(8,128)(2,1)}, bf16[512,128]{1,0:T(8,128)(2,1)S(1)}, u32[]{:S(2)}, u32[]{:S(2)}) collective-permute-start(bf16[512,128]{1,0:T(8,128)(2,1)} %v0.2), channel_id=1, source_target_pairs={{0,1},{1,0},{2,3},{3,2},{4,5},{5,4},{6,7},{7,6},{8,9},{9,8},{10,11... | collective-permute-start | bytes 393224 | tf_op jit(solution)/shard_map/ppermute | solution.py:449
  8.3 6.9 %collective-permute-start.6 = (bf16[512,128]{1,0:T(8,128)(2,1)S(1)}, bf16[512,128]{1,0:T(8,128)(2,1)S(1)}, u32[]{:S(2)}, u32[]{:S(2)}) collective-permute-start(bf16[512,128]{1,0:T(8,128)(2,1)S(1)} %collective-permute-done.5.w2), channel_id=1, source_target_pairs={{0,1},{1,0},{2,3},{3,2},{4,5},{5,4},{6,7},{7,6},{8,9},{9,8},{10,11... | collective-permute-start | bytes 393224 | tf_op jit(solution)/shard_map/ppermute | solution.py:449
  28.6 14.3 %collective-permute-start.13 = (bf16[2,4,64,512]{3,2,1,0:T(8,128)(2,1)S(1)}, bf16[2,4,64,512]{3,2,1,0:T(8,128)(2,1)S(1)}, u32[]{:S(2)}, u32[]{:S(2)}) collective-permute-start(bf16[2,4,64,512]{3,2,1,0:T(8,128)(2,1)S(1)} %get-tuple-element.39), channel_id=1, source_target_pairs={{0,4},{4,0},{8,12},{12,8},{16,20},{20,16},{24,28},{28,24},{1,5},{5... | collective-permute-start | bytes 1572872 | tf_op jit(solution)/shard_map/ppermute | solution.py:449
  30.5 14.9 %collective-permute-start.11 = (bf16[2,4,64,512]{3,2,1,0:T(8,128)(2,1)S(1)}, bf16[2,4,64,512]{3,2,1,0:T(8,128)(2,1)S(1)}, u32[]{:S(2)}, u32[]{:S(2)}) collective-permute-start(bf16[2,4,64,512]{3,2,1,0:T(8,128)(2,1)S(1)} %get-tuple-element.37), channel_id=1, source_target_pairs={{0,2},{1,3},{2,0},{3,1},{4,6},{5,7},{6,4},{7,5},{8,10},{9,11},{10,... | collective-permute-start | bytes 1572872 | tf_op jit(solution)/shard_map/ppermute | solution.py:449
  32.1 32.0 %collective-permute-start.19 = (bf16[1024,128]{1,0:T(8,128)(2,1)S(1)}, bf16[1024,128]{1,0:T(8,128)(2,1)S(1)}, u32[]{:S(2)}, u32[]{:S(2)}) collective-permute-start(bf16[1024,128]{1,0:T(8,128)(2,1)S(1)} %copy-done.4), channel_id=1, source_target_pairs={{0,2},{1,3},{2,0},{3,1},{4,6},{5,7},{6,4},{7,5},{8,10},{9,11},{10,... | collective-permute-start | bytes 786440 | tf_op jit(solution)/shard_map/ppermute | solution.py:449
  43.0 21.6 %collective-permute-start.14 = (bf16[4,64,512]{2,1,0:T(8,128)(2,1)S(1)}, bf16[4,64,512]{2,1,0:T(8,128)(2,1)S(1)}, u32[]{:S(2)}, u32[]{:S(2)}) collective-permute-start(bf16[4,64,512]{2,1,0:T(8,128)(2,1)S(1)} %fusion.1), channel_id=1, source_target_pairs={{0,2},{1,3},{2,0},{3,1},{4,6},{5,7},{6,4},{7,5},{8,10},{9,11},{10,... | collective-permute-start | bytes 786440 | tf_op jit(solution)/shard_map/ppermute | solution.py:449
  45.4 19.2 %collective-permute-start.12 = (bf16[4,64,512]{2,1,0:T(8,128)(2,1)S(1)}, bf16[4,64,512]{2,1,0:T(8,128)(2,1)S(1)}, u32[]{:S(2)}, u32[]{:S(2)}) collective-permute-start(bf16[4,64,512]{2,1,0:T(8,128)(2,1)S(1)} %fusion), channel_id=1, source_target_pairs={{0,4},{4,0},{8,12},{12,8},{16,20},{20,16},{24,28},{28,24},{1,5},{5... | collective-permute-start | bytes 786440 | tf_op jit(solution)/shard_map/ppermute | solution.py:449
  46.5 17.6 %collective-permute-start.22 = (bf16[128,512]{1,0:T(8,128)(2,1)S(1)}, bf16[128,512]{1,0:T(8,128)(2,1)S(1)}, u32[]{:S(2)}, u32[]{:S(2)}) collective-permute-start(bf16[128,512]{1,0:T(8,128)(2,1)S(1)} %copy-done.8), channel_id=1, source_target_pairs={{0,2},{1,3},{2,0},{3,1},{4,6},{5,7},{6,4},{7,5},{8,10},{9,11},{10,... | collective-permute-start | bytes 393224 | tf_op jit(solution)/shard_map/ppermute | solution.py:449
  48.7 10.5 %collective-permute-start.1 = (bf16[128,128]{1,0:T(8,128)(2,1)S(1)}, bf16[128,128]{1,0:T(8,128)(2,1)S(1)}, u32[]{:S(2)}, u32[]{:S(2)}) collective-permute-start(bf16[128,128]{1,0:T(8,128)(2,1)S(1)} %copy-done.26), channel_id=1, source_target_pairs={{0,2},{1,3},{2,0},{3,1},{4,6},{5,7},{6,4},{7,5},{8,10},{9,11},{10,... | collective-permute-start | bytes 98312 | tf_op jit(solution)/shard_map/ppermute | solution.py:449
  62.9 11.1 %collective-permute-start.25 = (bf16[1536,128]{1,0:T(8,128)(2,1)S(1)}, bf16[1536,128]{1,0:T(8,128)(2,1)S(1)}, u32[]{:S(2)}, u32[]{:S(2)}) collective-permute-start(bf16[1536,128]{1,0:T(8,128)(2,1)S(1)} %copy-done.2), channel_id=1, source_target_pairs={{0,2},{1,3},{2,0},{3,1},{4,6},{5,7},{6,4},{7,5},{8,10},{9,11},{10,... | collective-permute-start | bytes 1179656 | tf_op jit(solution)/shard_map/ppermute | solution.py:449
  64.1 5.7 %collective-permute-start.18 = (bf16[1024,128]{1,0:T(8,128)(2,1)S(1)}, bf16[1024,128]{1,0:T(8,128)(2,1)S(1)}, u32[]{:S(2)}, u32[]{:S(2)}) collective-permute-start(bf16[1024,128]{1,0:T(8,128)(2,1)S(1)} %copy-done.4), channel_id=1, source_target_pairs={{0,1},{1,0},{2,3},{3,2},{4,5},{5,4},{6,7},{7,6},{8,9},{9,8},{10,11... | collective-permute-start | bytes 786440 | tf_op jit(solution)/shard_map/ppermute | solution.py:449
  64.7 9.4 %collective-permute-start.20 = (bf16[1024,128]{1,0:T(8,128)(2,1)S(1)}, bf16[1024,128]{1,0:T(8,128)(2,1)S(1)}, u32[]{:S(2)}, u32[]{:S(2)}) collective-permute-start(bf16[1024,128]{1,0:T(8,128)(2,1)S(1)} %collective-permute-done.19.refs_12_), channel_id=1, source_target_pairs={{0,1},{1,0},{2,3},{3,2},{4,5},{5,4},{6,7},{7,6},{8,9},{9,8},{10,11... | collective-permute-start | bytes 786440 | tf_op jit(solution)/shard_map/ppermute | solution.py:449
  65.8 12.9 %collective-permute-start.15 = (bf16[128,512]{1,0:T(8,128)(2,1)S(1)}, bf16[128,512]{1,0:T(8,128)(2,1)S(1)}, u32[]{:S(2)}, u32[]{:S(2)}) collective-permute-start(bf16[128,512]{1,0:T(8,128)(2,1)S(1)} %get-tuple-element.41), channel_id=1, source_target_pairs={{0,16},{4,20},{8,24},{12,28},{16,0},{20,4},{24,8},{28,12},{1,17},{... | collective-permute-start | bytes 393224 | tf_op jit(solution)/shard_map/ppermute | solution.py:449
  68.4 10.3 %collective-permute-start.16 = (bf16[128,512]{1,0:T(8,128)(2,1)S(1)}, bf16[128,512]{1,0:T(8,128)(2,1)S(1)}, u32[]{:S(2)}, u32[]{:S(2)}) collective-permute-start(bf16[128,512]{1,0:T(8,128)(2,1)S(1)} %get-tuple-element.42), channel_id=1, source_target_pairs={{0,24},{4,28},{8,16},{12,20},{16,8},{20,12},{24,0},{28,4},{1,25},{... | collective-permute-start | bytes 393224 | tf_op jit(solution)/shard_map/ppermute | solution.py:449
  69.8 9.6 %collective-permute-start.17 = (bf16[128,512]{1,0:T(8,128)(2,1)S(1)}, bf16[128,512]{1,0:T(8,128)(2,1)S(1)}, u32[]{:S(2)}, u32[]{:S(2)}) collective-permute-start(bf16[128,512]{1,0:T(8,128)(2,1)S(1)} %get-tuple-element.43), channel_id=1, source_target_pairs={{0,8},{4,12},{8,0},{12,4},{16,24},{20,28},{24,16},{28,20},{1,9},{5... | collective-permute-start | bytes 393224 | tf_op jit(solution)/shard_map/ppermute | solution.py:449
  74.0 30.3 %collective-permute-start.24 = (bf16[1536,128]{1,0:T(8,128)(2,1)S(1)}, bf16[1536,128]{1,0:T(8,128)(2,1)S(1)}, u32[]{:S(2)}, u32[]{:S(2)}) collective-permute-start(bf16[1536,128]{1,0:T(8,128)(2,1)S(1)} %copy-done.2), channel_id=1, source_target_pairs={{0,1},{1,0},{2,3},{3,2},{4,5},{5,4},{6,7},{7,6},{8,9},{9,8},{10,11... | collective-permute-start | bytes 1179656 | tf_op jit(solution)/shard_map/ppermute | solution.py:449
  74.1 30.3 %collective-permute-start.26 = (bf16[1536,128]{1,0:T(8,128)(2,1)S(1)}, bf16[1536,128]{1,0:T(8,128)(2,1)S(1)}, u32[]{:S(2)}, u32[]{:S(2)}) collective-permute-start(bf16[1536,128]{1,0:T(8,128)(2,1)S(1)} %collective-permute-done.25.w2), channel_id=1, source_target_pairs={{0,1},{1,0},{2,3},{3,2},{4,5},{5,4},{6,7},{7,6},{8,9},{9,8},{10,11... | collective-permute-start | bytes 1179656 | tf_op jit(solution)/shard_map/ppermute | solution.py:449
  87.4 7.1 %collective-permute-start.27 = (bf16[64,512]{1,0:T(8,128)(2,1)S(1)}, bf16[64,512]{1,0:T(8,128)(2,1)S(1)}, u32[]{:S(2)}, u32[]{:S(2)}) collective-permute-start(bf16[64,512]{1,0:T(8,128)(2,1)S(1)} %get-tuple-element.47), channel_id=1, source_target_pairs={{0,28},{1,25},{2,30},{3,27},{4,24},{5,29},{6,26},{7,31},{8,20},{9,... | collective-permute-start | bytes 196616 | tf_op jit(solution)/shard_map/ppermute | solution.py:521
  90.7 7.1 %collective-permute-start.28 = (bf16[64,512]{1,0:T(8,128)(2,1)S(1)}, bf16[64,512]{1,0:T(8,128)(2,1)S(1)}, u32[]{:S(2)}, u32[]{:S(2)}) collective-permute-start(bf16[64,512]{1,0:T(8,128)(2,1)S(1)} %get-tuple-element.48), channel_id=1, source_target_pairs={{0,16},{1,21},{2,18},{3,23},{4,20},{5,17},{6,22},{7,19},{8,24},{9,... | collective-permute-start | bytes 196616 | tf_op jit(solution)/shard_map/ppermute | solution.py:521
  91.9 7.1 %collective-permute-start.29 = (bf16[64,512]{1,0:T(8,128)(2,1)S(1)}, bf16[64,512]{1,0:T(8,128)(2,1)S(1)}, u32[]{:S(2)}, u32[]{:S(2)}) collective-permute-start(bf16[64,512]{1,0:T(8,128)(2,1)S(1)} %get-tuple-element.49), channel_id=1, source_target_pairs={{0,12},{1,9},{2,14},{3,11},{4,8},{5,13},{6,10},{7,15},{8,4},{9,1},... | collective-permute-start | bytes 196616 | tf_op jit(solution)/shard_map/ppermute | solution.py:521
  97.8 5.5 %collective-permute-start.33 = (bf16[512,128]{1,0:T(8,128)(2,1)S(1)}, bf16[512,128]{1,0:T(8,128)(2,1)S(1)}, u32[]{:S(2)}, u32[]{:S(2)}) collective-permute-start(bf16[512,128]{1,0:T(8,128)(2,1)S(1)} %copy-done.6), channel_id=1, source_target_pairs={{0,2},{1,3},{2,0},{3,1},{4,6},{5,7},{6,4},{7,5},{8,10},{9,11},{10,... | collective-permute-start | bytes 393224 | tf_op jit(solution)/shard_map/ppermute | solution.py:449
  99.0 8.5 %collective-permute-start.31 = (bf16[256,512]{1,0:T(8,128)(2,1)S(1)}, bf16[256,512]{1,0:T(8,128)(2,1)S(1)}, u32[]{:S(2)}, u32[]{:S(2)}) collective-permute-start(bf16[256,512]{1,0:T(8,128)(2,1)S(1)} %shard_map.274.halo_a), channel_id=1, source_target_pairs={{0,1},{1,0},{2,3},{3,2},{4,5},{5,4},{6,7},{7,6},{8,9},{9,8},{10,11... | collective-permute-start | bytes 786440 | tf_op jit(solution)/shard_map/ppermute | solution.py:449
  99.1 8.4 %collective-permute-start.32 = (bf16[512,128]{1,0:T(8,128)(2,1)S(1)}, bf16[512,128]{1,0:T(8,128)(2,1)S(1)}, u32[]{:S(2)}, u32[]{:S(2)}) collective-permute-start(bf16[512,128]{1,0:T(8,128)(2,1)S(1)} %copy-done.6), channel_id=1, source_target_pairs={{0,1},{1,0},{2,3},{3,2},{4,5},{5,4},{6,7},{7,6},{8,9},{9,8},{10,11... | collective-permute-start | bytes 393224 | tf_op jit(solution)/shard_map/ppermute | solution.py:449
  103.2 14.1 %collective-permute-start.38 = (bf16[1024,128]{1,0:T(8,128)(2,1)S(1)}, bf16[1024,128]{1,0:T(8,128)(2,1)S(1)}, u32[]{:S(2)}, u32[]{:S(2)}) collective-permute-start(bf16[1024,128]{1,0:T(8,128)(2,1)S(1)} %copy-done.3), channel_id=1, source_target_pairs={{0,2},{1,3},{2,0},{3,1},{4,6},{5,7},{6,4},{7,5},{8,10},{9,11},{10,... | collective-permute-start | bytes 786440 | tf_op jit(solution)/shard_map/ppermute | solution.py:449
  111.3 6.6 %collective-permute-start.35 = (bf16[2,128,512]{2,1,0:T(8,128)(2,1)S(1)}, bf16[2,128,512]{2,1,0:T(8,128)(2,1)S(1)}, u32[]{:S(2)}, u32[]{:S(2)}) collective-permute-start(bf16[2,128,512]{2,1,0:T(8,128)(2,1)S(1)} %get-tuple-element.51), channel_id=1, source_target_pairs={{0,1},{1,0},{2,3},{3,2},{4,5},{5,4},{6,7},{7,6},{8,9},{9,8},{10,11... | collective-permute-start | bytes 786440 | tf_op jit(solution)/shard_map/ppermute | solution.py:449
  111.9 5.5 %collective-permute-start.41 = (bf16[128,512]{1,0:T(8,128)(2,1)S(1)}, bf16[128,512]{1,0:T(8,128)(2,1)S(1)}, u32[]{:S(2)}, u32[]{:S(2)}) collective-permute-start(bf16[128,512]{1,0:T(8,128)(2,1)S(1)} %copy-done.7), channel_id=1, source_target_pairs={{0,2},{1,3},{2,0},{3,1},{4,6},{5,7},{6,4},{7,5},{8,10},{9,11},{10,... | collective-permute-start | bytes 393224 | tf_op jit(solution)/shard_map/ppermute | solution.py:449
  112.8 6.1 %collective-permute-start.37 = (bf16[1024,128]{1,0:T(8,128)(2,1)S(1)}, bf16[1024,128]{1,0:T(8,128)(2,1)S(1)}, u32[]{:S(2)}, u32[]{:S(2)}) collective-permute-start(bf16[1024,128]{1,0:T(8,128)(2,1)S(1)} %copy-done.3), channel_id=1, source_target_pairs={{0,1},{1,0},{2,3},{3,2},{4,5},{5,4},{6,7},{7,6},{8,9},{9,8},{10,11... | collective-permute-start | bytes 786440 | tf_op jit(solution)/shard_map/ppermute | solution.py:449
  112.8 6.1 %collective-permute-start.40 = (bf16[128,512]{1,0:T(8,128)(2,1)S(1)}, bf16[128,512]{1,0:T(8,128)(2,1)S(1)}, u32[]{:S(2)}, u32[]{:S(2)}) collective-permute-start(bf16[128,512]{1,0:T(8,128)(2,1)S(1)} %copy-done.7), channel_id=1, source_target_pairs={{0,1},{1,0},{2,3},{3,2},{4,5},{5,4},{6,7},{7,6},{8,9},{9,8},{10,11... | collective-permute-start | bytes 393224 | tf_op jit(solution)/shard_map/ppermute | solution.py:449
  117.9 5.5 %collective-permute-start.36 = (bf16[128,512]{1,0:T(8,128)(2,1)S(1)}, bf16[128,512]{1,0:T(8,128)(2,1)S(1)}, u32[]{:S(2)}, u32[]{:S(2)}) collective-permute-start(bf16[128,512]{1,0:T(8,128)(2,1)S(1)} %fusion.2), channel_id=1, source_target_pairs={{0,2},{1,3},{2,0},{3,1},{4,6},{5,7},{6,4},{7,5},{8,10},{9,11},{10,... | collective-permute-start | bytes 393224 | tf_op jit(solution)/shard_map/ppermute | solution.py:449
  (42 other events, 564.5 us)

commit v4 on v3

--- a/solution.py
+++ b/solution.py
@@ -11,6 +11,7 @@
 BF16 = jnp.bfloat16
 I32 = jnp.int32
 SPLIT = 32
+LAT, LON = "lat", "lon"
 CHUNK = 256
 LANES = 128
 GRANT = 16 << 20
@@ -100,7 +101,7 @@
     first_sem,
     sem,
 ):
-    lon = lax.axis_index("lon")
+    lon = lax.axis_index(LON)
     rows = base0.shape[0]
     inputs = (owner_hbm, sender_hbm, node_hbm, feat_hbm, halo_hbm, from_hbm, to_hbm)
     held = (owner_ref, sender_ref, node_ref, feat_ref, halo_ref, from_ref, to_ref)
@@ -156,7 +157,7 @@
 
 def message_kernel(n_feat, rows_ref, meta_ref, proj_ref, bias_ref, gain_ref, w0, w1, w2, w3, v0, v1, v2, v3, out_ref, win, wout, proj):
     quarter = w0.shape[1]
-    lon = lax.axis_index("lon")
+    lon = lax.axis_index(LON)
     for j, (w, v) in enumerate(((w0, v0), (w1, v1), (w2, v2), (w3, v3))):
         win[:, j * quarter : (j + 1) * quarter] = w[...]
         wout[:, j * quarter : (j + 1) * quarter] = v[...]
@@ -191,9 +192,9 @@
     tall = y_ref.shape[1]
     quarter = mesh_rows // 4
     half = quarter // 2
-    lat = lax.axis_index("lat")
+    lat = lax.axis_index(LAT)
     low, high = lax.rem(lat, 2), lat // 2
-    lon = lax.axis_index("lon")
+    lon = lax.axis_index(LON)
     mine = lon * quarter
     other = (lon ^ 2) * quarter
     ready = min(key_rows, (cap + 2 * LANES - 2) // LANES)
@@ -219,7 +220,7 @@
     near_low = low if keep else 1 - low
     base = mine if keep else other
 
-    @pl.loop(0, tall, unroll=2)
+    @pl.loop(0, tall, unroll=4)
     def _(i):
         both = sums(2 * i + near_low, (base, mine + half, other + half))
         one = sums(2 * i + 1 - near_low, (base,))
@@ -255,7 +256,7 @@
     base, win, wout = refs[10 + n_out :]
     width = base.shape[1]
     quarter = weights[0].shape[1]
-    lon = lax.axis_index("lon")
+    lon = lax.axis_index(LON)
     biases = []
     for j in range(4):
         win[:, j * quarter : (j + 1) * quarter] = weights[j][...]
@@ -298,7 +299,7 @@
     pieces, out_ref = refs[:4], refs[4]
     rows = pieces[0].shape[0]
     for j in range(4):
-        out_ref[pl.ds(pl.multiple_of((lax.axis_index("lon") ^ j) * rows, rows), rows), :] = pieces[j][...]
+        out_ref[pl.ds(pl.multiple_of((lax.axis_index(LON) ^ j) * rows, rows), rows), :] = pieces[j][...]
 
 
 def pick_kernel(index_ref, table_ref, *refs):
@@ -307,15 +308,15 @@
     pick = jnp.where(lane == index_ref[...], 1.0, 0.0).astype(BF16)
     held[...] = dot(pick, table_ref[...])
     cap = outs[0].shape[0]
-    core = lax.rem(lax.axis_index("lon"), 2)
+    core = lax.rem(lax.axis_index(LON), 2)
     for out, (flip0, flip1) in zip(outs, turns(2 * len(outs))):
-        at = (lax.axis_index("lat") ^ jnp.where(core == 0, flip0, flip1)) * cap
+        at = (lax.axis_index(LAT) ^ jnp.where(core == 0, flip0, flip1)) * cap
         out[...] = held[pl.ds(pl.multiple_of(at, cap), cap), :].astype(BF16)
 
 
 def pack_kernel(own_ref, *refs):
     out_ref = refs[-1]
-    core = lax.rem(lax.axis_index("lon"), 2)
+    core = lax.rem(lax.axis_index(LON), 2)
     last = jnp.where(core == 0, own_ref[...].astype(F32), refs[-2][...].astype(F32))
     out_ref[...] = jnp.concatenate([ref[...].astype(F32) for ref in refs[:-2]] + [last], 0).astype(BF16)
 
@@ -329,7 +330,7 @@
         loads.append(pltpu.make_async_copy(edge_hbm.at[at, :], edge_ref.at[at, :], sem.at[i]))
         loads[-1].start()
     quarter = w0.shape[1]
-    lon = lax.axis_index("lon")
+    lon = lax.axis_index(LON)
     biases = []
     for j, w in enumerate((w0, w1, w2, w3)):
         win[:, j * quarter : (j + 1) * quarter] = w[...]
@@ -354,7 +355,7 @@
     load.start()
     width = halo_a.shape[1]
     quarter = w0.shape[1]
-    lon = lax.axis_index("lon")
+    lon = lax.axis_index(LON)
     for j, (w, v) in enumerate(((w0, v0), (w1, v1), (w2, v2), (w3, v3))):
         win[:, j * quarter : (j + 1) * quarter] = w[width : 2 * width, :]
         wout[:, j * quarter : (j + 1) * quarter] = v[...]
@@ -363,7 +364,7 @@
     sent = [dot(h[...], win[...]).astype(BF16) for h in (halo_a, halo_b)]
     lane = lax.broadcasted_iota(I32, (1, rows), 1)
     core = lax.rem(lon, 2)
-    lat = lax.axis_index("lat")
+    lat = lax.axis_index(LAT)
     flips = [jnp.zeros_like(lane), jnp.zeros_like(lane)]
     for j, pair in enumerate(turns(2 * (rows // halo_cap))):
         flips = [jnp.where(lane // halo_cap == j, flip, before) for flip, before in zip(pair, flips)]
@@ -431,7 +432,7 @@
     proc_node_bias,
     proc_node_gain,
 ):
-    lat_count = lax.axis_size("lat")
+    lat_count = lax.axis_size(LAT)
     width = grid_latent.shape[1]
     quarter = mesh_latent.shape[1]
     mesh_rows = mesh_latent.shape[0]
@@ -449,8 +450,8 @@
         return lax.ppermute(values, axis, [(i, i ^ flip) for i in range(size)])
 
     def spread(shard):
-        across = hop(shard, "lon", 2)
-        return (shard, hop(shard, "lon", 1), across, hop(across, "lon", 1))
+        across = hop(shard, LON, 2)
+        return (shard, hop(shard, LON, 1), across, hop(across, LON, 1))
 
     enc_in = spread(enc_edge_in)
     enc_out = spread(enc_edge_out)
@@ -471,13 +472,13 @@
         + [pltpu.SemaphoreType.DMA((len(small),)), pltpu.SemaphoreType.DMA((4,))],
         FULL,
     )(*small, mesh_latent)
-    bases = tuple(rest[j] if j == 0 else hop(rest[j], "lon", j) for j in range(4))
+    bases = tuple(rest[j] if j == 0 else hop(rest[j], LON, j) for j in range(4))
     node_pieces = spread(enc_node_in) + spread(enc_node_out)
     edge_in = spread(proc_edge_in)
     edge_out = spread(proc_edge_out)
     last_pieces = spread(proc_node_in) + spread(proc_node_out)
 
-    tables = (table, hop(table, "lon", 1))
+    tables = (table, hop(table, LON, 1))
     message = call(
         functools.partial(message_kernel, grid_feat.shape[0]),
         like(edges, width),
@@ -485,23 +486,23 @@
         4 * edges * width * width,
         [pltpu.VMEM((width, width), BF16), pltpu.VMEM((width, width), BF16), pltpu.VMEM((META, width), BF16)],
     )(grid_latent, meta, enc_feat_proj, enc_edge_bias, enc_edge_gain[None, :], *enc_in, *enc_out)
-    messages = (message, hop(message, "lon", 1))
+    messages = (message, hop(message, LON, 1))
 
     tall = lat_count // 2
     send_x, send_y = node_sums(False, tables, messages, lat_count, mesh_rows)
-    got_x = hop(send_x, "lon", 2)
-    got_y = hop(send_y, "lat", 1)
+    got_x = hop(send_x, LON, 2)
+    got_y = hop(send_y, LAT, 1)
     keep_x, keep_y = node_sums(True, tables, messages, lat_count, mesh_rows)
-    got_xy = hop(plus(keep_x[1], got_x[1]), "lat", 1)
-    got_yx = hop(plus(keep_y[1], got_y[1]), "lon", 2)
+    got_xy = hop(plus(keep_x[1], got_x[1]), LAT, 1)
+    got_yx = hop(plus(keep_y[1], got_y[1]), LON, 2)
     joined = call(join_kernel, [like(node_rows, width)] * tall, [VMEM] * 6, 1 << 20)(
         keep_x, got_x, got_xy, keep_y, got_y, got_yx
     )
     far_first = sorted(range(1, tall), key=lambda j: (j < tall // 2, j))
-    partials = (joined[0], *[hop(joined[j], "lat", 2 * j) for j in far_first])
+    partials = (joined[0], *[hop(joined[j], LAT, 2 * j) for j in far_first])
 
     mid = node_network(bases, partials, enc_node_bias, enc_node_gain, node_pieces, 1)
-    mid_all = lax.all_gather(mid, "lon", axis=0, tiled=True)
+    mid_all = lax.all_gather(mid, LON, axis=0, tiled=True)
 
     picked = call(
         pick_kernel,
@@ -518,7 +519,7 @@
                 to = i ^ flips[l % 2]
                 if to != i:
                     pairs.append((i * 4 + l, to * 4 + l))
-        return lax.ppermute(picked[j], ("lat", "lon"), pairs)
+        return lax.ppermute(picked[j], (LAT, LON), pairs)
 
     arrived = [halo_hop(j, flips) for j, flips in enumerate(turns(lat_count))]
     near = call(
@@ -533,7 +534,7 @@
         ],
     )(mesh_edge, mid_all, ends, proc_edge_bias, *edge_in)
     packed = call(pack_kernel, like(listed // 2, width), [VMEM] * (tall + 1), 1 << 20)(picked[-1], *arrived)
-    halves = (packed, hop(packed, "lon", 1))
+    halves = (packed, hop(packed, LON, 1))
 
     edge_update, away, kept, passed = call(
         functools.partial(far_kernel, halo_cap),
@@ -554,43 +555,43 @@
         ],
     )(mesh_edge, near, *halves, ends, mesh_receiver[None, :], proc_edge_bias, proc_edge_gain[None, :], *edge_in, *edge_out)
 
-    came = hop(away, "lon", 1)
-    got = hop(plus(passed, came[1]), "lon", 2)
+    came = hop(away, LON, 1)
+    got = hop(plus(passed, came[1]), LON, 2)
     new = node_network((mid,), (kept, came, got), proc_node_bias, proc_node_gain, last_pieces, 4)
     mesh_update = call(lay_kernel, like(mesh_rows, quarter), [VMEM] * 4, 1 << 20)(
-        new[0], *[hop(new[j], "lon", j) for j in (1, 2, 3)]
+        new[0], *[hop(new[j], LON, j) for j in (1, 2, 3)]
     )
     return (mesh_update, edge_update)
 
 
 def solution(mesh):
-    both = ("lat", "lon")
+    both = (LAT, LON)
     placed = (
         P(both, None),
         P(None, both),
         P(both),
         P(both, None),
         P(both),
-        P("lat", "lon"),
+        P(LAT, LON),
         P(both, None),
-        P("lat", None),
+        P(LAT, None),
         P(both),
         P(both),
-        P(None, "lon"),
-        P(),
-        P(None, "lon"),
-        P(),
-        P(),
-        P(None, "lon"),
-        P("lon", None),
-        P(),
-        P(),
-        P(None, "lon"),
-        P(None, "lon"),
-        P(),
-        P(),
-        P(None, "lon"),
-        P("lon", None),
+        P(None, LON),
+        P(),
+        P(None, LON),
+        P(),
+        P(),
+        P(None, LON),
+        P(LON, None),
+        P(),
+        P(),
+        P(None, LON),
+        P(None, LON),
+        P(),
+        P(),
+        P(None, LON),
+        P(LON, None),
         P(),
         P(),
     )
@@ -599,6 +600,6 @@
         local,
         mesh=mesh,
         in_specs=placed,
-        out_specs=(P("lat", "lon"), P(both, None)),
+        out_specs=(P(LAT, LON), P(both, None)),
         check_vma=False,
     )

time: 130 us -> 130 us (level)
  no operation moved by 1% of the time
where the time goes in v4:
time: 130 us; the launch traced here: 129 us
  waiting for transfers between devices  59.4 us (46%)
  starting transfers between devices  35 us (27%)
  Pallas kernels  26.3 us (20%)
  blocking collectives  6.59 us (5%)
    ppermute x42, waiting for transfers between devices, hop(): return lax.ppermute(values, axis, [(i, i ^ flip) for i in range(size)])  55.5 us
    ppermute x42, starting transfers between devices, hop(): return lax.ppermute(values, axis, [(i, i ^ flip) for i in range(size)])  28.5 us
    all_gather x1, blocking collectives, local(): mid_all = lax.all_gather(mid, LON, axis=0, tiled=True)  6.59 us
    ppermute x4, starting transfers between devices, halo_hop(): return lax.ppermute(picked[j], (LAT, LON), pairs)  6.54 us
    pallas_call x2, Pallas kernels, node_sums(): call(functools.partial(sums_kernel, mesh_rows, 2 * edges // lat_count, ke...  6.52 us
    pallas_call x1, Pallas kernels, local(): call(functools.partial(open_kernel, lat_count, mesh_rows), [like(edges //...  4.9 us
    pallas_call x1, Pallas kernels, local(): call(functools.partial(message_kernel, grid_feat.shape[0]), like(edges, w...  4.76 us
    ppermute x4, waiting for transfers between devices, halo_hop(): return lax.ppermute(picked[j], (LAT, LON), pairs)  3.88 us
  transfers between devices with their start and end apart: 46, of which 20 were waited for; matrix products, arithmetic and copies ran while one was open for 0% of the time, Pallas kernels for 13%

profile of v4, /device:TPU:0, one launch (start us, length us, event | category | flops | bytes accessed | tf_op | source)
XLA Modules:
  0.0 129.5 jit_solution(9848623331383955981)
XLA Ops:
  0.7 3.0 %collective-permute-start.5 = (bf16[512,128]{1,0:T(8,128)(2,1)}, bf16[512,128]{1,0:T(8,128)(2,1)S(1)}, u32[]{:S(2)}, u32[]{:S(2)}) collective-permute-start(bf16[512,128]{1,0:T(8,128)(2,1)} %w0.3), channel_id=1, source_target_pairs={{0,2},{1,3},{2,0},{3,1},{4,6},{5,7},{6,4},{7,5},{8,10},{9,11},{10,... | collective-permute-start | bytes 393224 | tf_op jit(solution)/shard_map/ppermute | solution.py:450
  4.3 4.0 %collective-permute-done.5.w2 = bf16[512,128]{1,0:T(8,128)(2,1)S(1)} collective-permute-done((bf16[512,128]{1,0:T(8,128)(2,1)}, bf16[512,128]{1,0:T(8,128)(2,1)S(1)}, u32[]{:S(2)}, u32[]{:S(2)}) %collective-permute-start.5) | collective-permute-done | bytes 131104 | tf_op jit(solution)/shard_map/ppermute | solution.py:450
  8.3 2.0 %collective-permute-done.8.v2 = bf16[512,128]{1,0:T(8,128)(2,1)S(1)} collective-permute-done((bf16[512,128]{1,0:T(8,128)(2,1)}, bf16[512,128]{1,0:T(8,128)(2,1)S(1)}, u32[]{:S(2)}, u32[]{:S(2)}) %collective-permute-start.8) | collective-permute-done | bytes 131104 | tf_op jit(solution)/shard_map/ppermute | solution.py:450
  10.2 4.9 %shard_map.266 = (s32[24,128]{1,0:T(8,128)}, bf16[16,2048]{1,0:T(8,128)(2,1)}, s32[1024,8]{1,0:T(8,128)}, s32[512,1]{1,0:T(8,128)}, bf16[128,128]{1,0:T(8,128)(2...) custom-call(s32[1,2048]{1,0:T(1,128)} %bitcast.24, s32[1,2048]{1,0:T(1,128)} %bitcast.25, ...), custom_call_target="tpu_custom_call" | custom-call | flops 1073741824 | bytes 4194304 | tf_op jit(solution)/shard_map/pallas_call | solution.py:460
  16.1 4.8 %shard_map.267.msg_a = bf16[2048,512]{1,0:T(8,128)(2,1)S(1)} custom-call(bf16[512,512]{1,0:T(8,128)(2,1)S(1)} %copy-done.17, bf16[16,2048]{1,0:T(8,128)(2,1)S(1)} %copy-done.24, bf16[4,512]{1,0:T(4,128)(2,1)S(1)} %copy-done.20, f32[2,512]{1,0:T(2,128)S(1)} %copy-done.21, f32[1,512]{1,0:T(1,128)S(1)} %bitcast.23, bf16[512,128]{1,0:T(8,128)(2,1)S(1)} %copy-done.18, ...), custom_call_target="tpu_custom_call" | custom-call | flops 2147483648 | bytes 4194304 | tf_op jit(solution)/shard_map/pallas_call | solution.py:482
  21.5 3.7 %collective-permute-done.3.start_b.table_b = s32[24,128]{1,0:T(8,128)S(1)} collective-permute-done((s32[24,128]{1,0:T(8,128)S(1)}, s32[24,128]{1,0:T(8,128)S(1)}, u32[]{:S(2)}, u32[]{:S(2)}) %collective-permute-start.3) | collective-permute-done | bytes 12320 | tf_op jit(solution)/shard_map/ppermute | solution.py:450
  25.2 3.3 %shard_map.269 = (bf16[2,4,64,512]{3,2,1,0:T(8,128)(2,1)S(1)}, bf16[2,4,64,512]{3,2,1,0:T(8,128)(2,1)S(1)}) custom-call(s32[24,128]{1,0:T(8,128)S(1)} %copy-done.5, s32[24,128]{1,0:T(8,128)S(1)} %collective-permute-done.3.start_b.table_b, s32[24,128]{1,0:T(8,128)S(1)} %copy-done.5, s32[24,128]{1,0:T(8,128)S(1)} %collective-permute-done.3.start_b.table_b, ...), custom_call_target="tpu_custom_call" | custom-call | flops 1073741824 | bytes 4194304 | tf_op jit(solution)/shard_map/pallas_call | solution.py:238
  28.5 1.8 %collective-permute-start.13 = (bf16[2,4,64,512]{3,2,1,0:T(8,128)(2,1)S(1)}, bf16[2,4,64,512]{3,2,1,0:T(8,128)(2,1)S(1)}, u32[]{:S(2)}, u32[]{:S(2)}) collective-permute-start(bf16[2,4,64,512]{3,2,1,0:T(8,128)(2,1)S(1)} %get-tuple-element.39), channel_id=1, source_target_pairs={{0,4},{4,0},{8,12},{12,8},{16,20},{20,16},{24,28},{28,24},{1,5},{5... | collective-permute-start | bytes 1572872 | tf_op jit(solution)/shard_map/ppermute | solution.py:450
  30.4 1.6 %collective-permute-start.11 = (bf16[2,4,64,512]{3,2,1,0:T(8,128)(2,1)S(1)}, bf16[2,4,64,512]{3,2,1,0:T(8,128)(2,1)S(1)}, u32[]{:S(2)}, u32[]{:S(2)}) collective-permute-start(bf16[2,4,64,512]{3,2,1,0:T(8,128)(2,1)S(1)} %get-tuple-element.37), channel_id=1, source_target_pairs={{0,2},{1,3},{2,0},{3,1},{4,6},{5,7},{6,4},{7,5},{8,10},{9,11},{10,... | collective-permute-start | bytes 1572872 | tf_op jit(solution)/shard_map/ppermute | solution.py:450
  32.5 3.3 %shard_map.268 = (bf16[2,4,64,512]{3,2,1,0:T(8,128)(2,1)S(1)}, bf16[2,4,64,512]{3,2,1,0:T(8,128)(2,1)S(1)}) custom-call(s32[24,128]{1,0:T(8,128)S(1)} %copy-done.5, s32[24,128]{1,0:T(8,128)S(1)} %collective-permute-done.3.start_b.table_b, s32[24,128]{1,0:T(8,128)S(1)} %copy-done.5, s32[24,128]{1,0:T(8,128)S(1)} %collective-permute-done.3.start_b.table_b, ...), custom_call_target="tpu_custom_call" | custom-call | flops 1073741824 | bytes 4194304 | tf_op jit(solution)/shard_map/pallas_call | solution.py:238
  35.7 7.1 %collective-permute-done.13.got_y = bf16[2,4,64,512]{3,2,1,0:T(8,128)(2,1)S(1)} collective-permute-done((bf16[2,4,64,512]{3,2,1,0:T(8,128)(2,1)S(1)}, bf16[2,4,64,512]{3,2,1,0:T(8,128)(2,1)S(1)}, u32[]{:S(2)}, u32[]{:S(2)}) %collective-permute-start.13) | collective-permute-done | bytes 524320 | tf_op jit(solution)/shard_map/ppermute | solution.py:450
  42.9 1.8 %collective-permute-start.14 = (bf16[4,64,512]{2,1,0:T(8,128)(2,1)S(1)}, bf16[4,64,512]{2,1,0:T(8,128)(2,1)S(1)}, u32[]{:S(2)}, u32[]{:S(2)}) collective-permute-start(bf16[4,64,512]{2,1,0:T(8,128)(2,1)S(1)} %fusion.1), channel_id=1, source_target_pairs={{0,2},{1,3},{2,0},{3,1},{4,6},{5,7},{6,4},{7,5},{8,10},{9,11},{10,... | collective-permute-start | bytes 786440 | tf_op jit(solution)/shard_map/ppermute | solution.py:450
  47.4 1.2 collective-permute-done.refs_1_
  49.5 9.6 %collective-permute-done.1.refs_2_ = bf16[128,128]{1,0:T(8,128)(2,1)S(1)} collective-permute-done((bf16[128,128]{1,0:T(8,128)(2,1)S(1)}, bf16[128,128]{1,0:T(8,128)(2,1)S(1)}, u32[]{:S(2)}, u32[]{:S(2)}) %collective-permute-start.1) | collective-permute-done | bytes 32800 | tf_op jit(solution)/shard_map/ppermute | solution.py:450
  59.4 3.4 %collective-permute-done.2.refs_3_ = bf16[128,128]{1,0:T(8,128)(2,1)S(1)} collective-permute-done((bf16[128,128]{1,0:T(8,128)(2,1)S(1)}, bf16[128,128]{1,0:T(8,128)(2,1)S(1)}, u32[]{:S(2)}, u32[]{:S(2)}) %collective-permute-start.2) | collective-permute-done | bytes 32800 | tf_op jit(solution)/shard_map/ppermute | solution.py:450
  62.8 1.1 collective-permute-start.25
  65.6 2.6 %collective-permute-start.15 = (bf16[128,512]{1,0:T(8,128)(2,1)S(1)}, bf16[128,512]{1,0:T(8,128)(2,1)S(1)}, u32[]{:S(2)}, u32[]{:S(2)}) collective-permute-start(bf16[128,512]{1,0:T(8,128)(2,1)S(1)} %get-tuple-element.41), channel_id=1, source_target_pairs={{0,16},{4,20},{8,24},{12,28},{16,0},{20,4},{24,8},{28,12},{1,17},{... | collective-permute-start | bytes 393224 | tf_op jit(solution)/shard_map/ppermute | solution.py:450
  68.3 1.3 %collective-permute-start.16 = (bf16[128,512]{1,0:T(8,128)(2,1)S(1)}, bf16[128,512]{1,0:T(8,128)(2,1)S(1)}, u32[]{:S(2)}, u32[]{:S(2)}) collective-permute-start(bf16[128,512]{1,0:T(8,128)(2,1)S(1)} %get-tuple-element.42), channel_id=1, source_target_pairs={{0,24},{4,28},{8,16},{12,20},{16,8},{20,12},{24,0},{28,4},{1,25},{... | collective-permute-start | bytes 393224 | tf_op jit(solution)/shard_map/ppermute | solution.py:450
  69.9 4.0 %collective-permute-done.25.w2 = bf16[1536,128]{1,0:T(8,128)(2,1)S(1)} collective-permute-done((bf16[1536,128]{1,0:T(8,128)(2,1)S(1)}, bf16[1536,128]{1,0:T(8,128)(2,1)S(1)}, u32[]{:S(2)}, u32[]{:S(2)}) %collective-permute-start.25) | collective-permute-done | bytes 393248 | tf_op jit(solution)/shard_map/ppermute | solution.py:450
  74.4 4.1 %collective-permute-done.15.refs_5_ = bf16[128,512]{1,0:T(8,128)(2,1)S(1)} collective-permute-done((bf16[128,512]{1,0:T(8,128)(2,1)S(1)}, bf16[128,512]{1,0:T(8,128)(2,1)S(1)}, u32[]{:S(2)}, u32[]{:S(2)}) %collective-permute-start.15) | collective-permute-done | bytes 131104 | tf_op jit(solution)/shard_map/ppermute | solution.py:450
  80.3 6.6 %all_gather.3.mid_ref.table_ref = bf16[512,512]{1,0:T(8,128)(2,1)S(1)} all-gather(bf16[128,512]{1,0:T(8,128)(2,1)S(1)} %shard_map.271.refs_0_), channel_id=1, replica_groups=mesh['lat'=8,'lon'=4] {'lon'}, dimensions={0}, use_global_device_ids=true | all-gather | bytes 655360 | tf_op jit(solution)/shard_map/all_gather | solution.py:505
  87.4 3.3 %collective-permute-start.27 = (bf16[64,512]{1,0:T(8,128)(2,1)S(1)}, bf16[64,512]{1,0:T(8,128)(2,1)S(1)}, u32[]{:S(2)}, u32[]{:S(2)}) collective-permute-start(bf16[64,512]{1,0:T(8,128)(2,1)S(1)} %get-tuple-element.47), channel_id=1, source_target_pairs={{0,28},{1,25},{2,30},{3,27},{4,24},{5,29},{6,26},{7,31},{8,20},{9,... | collective-permute-start | bytes 196616 | tf_op jit(solution)/shard_map/ppermute | solution.py:522
  90.7 1.2 collective-permute-start.28
  91.9 1.4 %collective-permute-start.29 = (bf16[64,512]{1,0:T(8,128)(2,1)S(1)}, bf16[64,512]{1,0:T(8,128)(2,1)S(1)}, u32[]{:S(2)}, u32[]{:S(2)}) collective-permute-start(bf16[64,512]{1,0:T(8,128)(2,1)S(1)} %get-tuple-element.49), channel_id=1, source_target_pairs={{0,12},{1,9},{2,14},{3,11},{4,8},{5,13},{6,10},{7,15},{8,4},{9,1},... | collective-permute-start | bytes 196616 | tf_op jit(solution)/shard_map/ppermute | solution.py:522
  93.3 1.2 collective-permute-done.27.refs_0_
  95.2 2.7 %collective-permute-done.28.refs_1_ = bf16[64,512]{1,0:T(8,128)(2,1)S(1)} collective-permute-done((bf16[64,512]{1,0:T(8,128)(2,1)S(1)}, bf16[64,512]{1,0:T(8,128)(2,1)S(1)}, u32[]{:S(2)}, u32[]{:S(2)}) %collective-permute-start.28) | collective-permute-done | bytes 65568 | tf_op jit(solution)/shard_map/ppermute | solution.py:522
  99.6 3.8 %collective-permute-done.33.v2 = bf16[512,128]{1,0:T(8,128)(2,1)S(1)} collective-permute-done((bf16[512,128]{1,0:T(8,128)(2,1)S(1)}, bf16[512,128]{1,0:T(8,128)(2,1)S(1)}, u32[]{:S(2)}, u32[]{:S(2)}) %collective-permute-start.33) | collective-permute-done | bytes 131104 | tf_op jit(solution)/shard_map/ppermute | solution.py:450
  104.4 3.0 %shard_map.272.pre_ref = f32[1024,512]{1,0:T(8,128)S(1)} custom-call(bf16[1024,512]{1,0:T(8,128)(2,1)S(1)} %copy-done, bf16[512,512]{1,0:T(8,128)(2,1)S(1)} %all_gather.3.mid_ref.table_ref, s32[1024,8]{1,0:T(8,128)S(1)} %copy-done.1, f32[2,512]{1,0:T(2,128)S(1)} %copy-done.13, bf16[1536,128]{1,0:T(8,128)(2,1)S(1)} %copy-done.2, ...), custom_call_target="tpu_custom_call" | custom-call | flops 1610612736 | bytes 4194304 | tf_op jit(solution)/shard_map/pallas_call | solution.py:525
  107.6 3.7 %shard_map.275 = (bf16[1024,512]{1,0:T(8,128)(2,1)}, bf16[2,128,512]{2,1,0:T(8,128)(2,1)S(1)}, bf16[128,512]{1,0:T(8,128)(2,1)S(1)}, bf16[128,512]{1,0:T(8,128)(2,1)S(1)}) custom-call(bf16[1024,512]{1,0:T(8,128)(2,1)S(1)} %copy-done, f32[1024,512]{1,0:T(8,128)S(1)} %shard_map.272.pre_ref, bf16[256,512]{1,0:T(8,128)(2,1)S(1)} %shard_map.274.halo_a, ...), custom_call_target="tpu_custom_call" | custom-call | flops 1610612736 | bytes 4194304 | tf_op jit(solution)/shard_map/pallas_call | solution.py:539
  113.4 4.0 %collective-permute-done.41.refs_12_ = bf16[128,512]{1,0:T(8,128)(2,1)S(1)} collective-permute-done((bf16[128,512]{1,0:T(8,128)(2,1)S(1)}, bf16[128,512]{1,0:T(8,128)(2,1)S(1)}, u32[]{:S(2)}, u32[]{:S(2)}) %collective-permute-start.41) | collective-permute-done | bytes 131104 | tf_op jit(solution)/shard_map/ppermute | solution.py:450
  119.1 4.3 %collective-permute-done.36.refs_3_ = bf16[128,512]{1,0:T(8,128)(2,1)S(1)} collective-permute-done((bf16[128,512]{1,0:T(8,128)(2,1)S(1)}, bf16[128,512]{1,0:T(8,128)(2,1)S(1)}, u32[]{:S(2)}, u32[]{:S(2)}) %collective-permute-start.36) | collective-permute-done | bytes 131104 | tf_op jit(solution)/shard_map/ppermute | solution.py:450
  126.2 2.1 %collective-permute-done.44.refs_2_ = bf16[128,128]{1,0:T(8,128)(2,1)S(1)} collective-permute-done((bf16[128,128]{1,0:T(8,128)(2,1)S(1)}, bf16[128,128]{1,0:T(8,128)(2,1)S(1)}, u32[]{:S(2)}, u32[]{:S(2)}) %collective-permute-start.44) | collective-permute-done | bytes 32800 | tf_op jit(solution)/shard_map/ppermute | solution.py:450
  (132 shorter events, 22.6 us)
Async XLA Ops:
  0.7 7.6 %collective-permute-start.5 = (bf16[512,128]{1,0:T(8,128)(2,1)}, bf16[512,128]{1,0:T(8,128)(2,1)S(1)}, u32[]{:S(2)}, u32[]{:S(2)}) collective-permute-start(bf16[512,128]{1,0:T(8,128)(2,1)} %w0.3), channel_id=1, source_target_pairs={{0,2},{1,3},{2,0},{3,1},{4,6},{5,7},{6,4},{7,5},{8,10},{9,11},{10,... | collective-permute-start | bytes 393224 | tf_op jit(solution)/shard_map/ppermute | solution.py:450
  3.7 6.5 %collective-permute-start.8 = (bf16[512,128]{1,0:T(8,128)(2,1)}, bf16[512,128]{1,0:T(8,128)(2,1)S(1)}, u32[]{:S(2)}, u32[]{:S(2)}) collective-permute-start(bf16[512,128]{1,0:T(8,128)(2,1)} %v0.2), channel_id=1, source_target_pairs={{0,2},{1,3},{2,0},{3,1},{4,6},{5,7},{6,4},{7,5},{8,10},{9,11},{10,... | collective-permute-start | bytes 393224 | tf_op jit(solution)/shard_map/ppermute | solution.py:450
  3.8 11.3 %collective-permute-start.4 = (bf16[512,128]{1,0:T(8,128)(2,1)}, bf16[512,128]{1,0:T(8,128)(2,1)S(1)}, u32[]{:S(2)}, u32[]{:S(2)}) collective-permute-start(bf16[512,128]{1,0:T(8,128)(2,1)} %w0.3), channel_id=1, source_target_pairs={{0,1},{1,0},{2,3},{3,2},{4,5},{5,4},{6,7},{7,6},{8,9},{9,8},{10,11... | collective-permute-start | bytes 393224 | tf_op jit(solution)/shard_map/ppermute | solution.py:450
  3.8 11.4 %collective-permute-start.7 = (bf16[512,128]{1,0:T(8,128)(2,1)}, bf16[512,128]{1,0:T(8,128)(2,1)S(1)}, u32[]{:S(2)}, u32[]{:S(2)}) collective-permute-start(bf16[512,128]{1,0:T(8,128)(2,1)} %v0.2), channel_id=1, source_target_pairs={{0,1},{1,0},{2,3},{3,2},{4,5},{5,4},{6,7},{7,6},{8,9},{9,8},{10,11... | collective-permute-start | bytes 393224 | tf_op jit(solution)/shard_map/ppermute | solution.py:450
  8.3 6.9 %collective-permute-start.6 = (bf16[512,128]{1,0:T(8,128)(2,1)S(1)}, bf16[512,128]{1,0:T(8,128)(2,1)S(1)}, u32[]{:S(2)}, u32[]{:S(2)}) collective-permute-start(bf16[512,128]{1,0:T(8,128)(2,1)S(1)} %collective-permute-done.5.w2), channel_id=1, source_target_pairs={{0,1},{1,0},{2,3},{3,2},{4,5},{5,4},{6,7},{7,6},{8,9},{9,8},{10,11... | collective-permute-start | bytes 393224 | tf_op jit(solution)/shard_map/ppermute | solution.py:450
  28.5 14.3 %collective-permute-start.13 = (bf16[2,4,64,512]{3,2,1,0:T(8,128)(2,1)S(1)}, bf16[2,4,64,512]{3,2,1,0:T(8,128)(2,1)S(1)}, u32[]{:S(2)}, u32[]{:S(2)}) collective-permute-start(bf16[2,4,64,512]{3,2,1,0:T(8,128)(2,1)S(1)} %get-tuple-element.39), channel_id=1, source_target_pairs={{0,4},{4,0},{8,12},{12,8},{16,20},{20,16},{24,28},{28,24},{1,5},{5... | collective-permute-start | bytes 1572872 | tf_op jit(solution)/shard_map/ppermute | solution.py:450
  30.4 14.9 %collective-permute-start.11 = (bf16[2,4,64,512]{3,2,1,0:T(8,128)(2,1)S(1)}, bf16[2,4,64,512]{3,2,1,0:T(8,128)(2,1)S(1)}, u32[]{:S(2)}, u32[]{:S(2)}) collective-permute-start(bf16[2,4,64,512]{3,2,1,0:T(8,128)(2,1)S(1)} %get-tuple-element.37), channel_id=1, source_target_pairs={{0,2},{1,3},{2,0},{3,1},{4,6},{5,7},{6,4},{7,5},{8,10},{9,11},{10,... | collective-permute-start | bytes 1572872 | tf_op jit(solution)/shard_map/ppermute | solution.py:450
  31.9 32.0 %collective-permute-start.19 = (bf16[1024,128]{1,0:T(8,128)(2,1)S(1)}, bf16[1024,128]{1,0:T(8,128)(2,1)S(1)}, u32[]{:S(2)}, u32[]{:S(2)}) collective-permute-start(bf16[1024,128]{1,0:T(8,128)(2,1)S(1)} %copy-done.4), channel_id=1, source_target_pairs={{0,2},{1,3},{2,0},{3,1},{4,6},{5,7},{6,4},{7,5},{8,10},{9,11},{10,... | collective-permute-start | bytes 786440 | tf_op jit(solution)/shard_map/ppermute | solution.py:450
  42.9 21.6 %collective-permute-start.14 = (bf16[4,64,512]{2,1,0:T(8,128)(2,1)S(1)}, bf16[4,64,512]{2,1,0:T(8,128)(2,1)S(1)}, u32[]{:S(2)}, u32[]{:S(2)}) collective-permute-start(bf16[4,64,512]{2,1,0:T(8,128)(2,1)S(1)} %fusion.1), channel_id=1, source_target_pairs={{0,2},{1,3},{2,0},{3,1},{4,6},{5,7},{6,4},{7,5},{8,10},{9,11},{10,... | collective-permute-start | bytes 786440 | tf_op jit(solution)/shard_map/ppermute | solution.py:450
  45.3 19.2 %collective-permute-start.12 = (bf16[4,64,512]{2,1,0:T(8,128)(2,1)S(1)}, bf16[4,64,512]{2,1,0:T(8,128)(2,1)S(1)}, u32[]{:S(2)}, u32[]{:S(2)}) collective-permute-start(bf16[4,64,512]{2,1,0:T(8,128)(2,1)S(1)} %fusion), channel_id=1, source_target_pairs={{0,4},{4,0},{8,12},{12,8},{16,20},{20,16},{24,28},{28,24},{1,5},{5... | collective-permute-start | bytes 786440 | tf_op jit(solution)/shard_map/ppermute | solution.py:450
  46.3 17.6 %collective-permute-start.22 = (bf16[128,512]{1,0:T(8,128)(2,1)S(1)}, bf16[128,512]{1,0:T(8,128)(2,1)S(1)}, u32[]{:S(2)}, u32[]{:S(2)}) collective-permute-start(bf16[128,512]{1,0:T(8,128)(2,1)S(1)} %copy-done.8), channel_id=1, source_target_pairs={{0,2},{1,3},{2,0},{3,1},{4,6},{5,7},{6,4},{7,5},{8,10},{9,11},{10,... | collective-permute-start | bytes 393224 | tf_op jit(solution)/shard_map/ppermute | solution.py:450
  48.6 10.5 %collective-permute-start.1 = (bf16[128,128]{1,0:T(8,128)(2,1)S(1)}, bf16[128,128]{1,0:T(8,128)(2,1)S(1)}, u32[]{:S(2)}, u32[]{:S(2)}) collective-permute-start(bf16[128,128]{1,0:T(8,128)(2,1)S(1)} %copy-done.26), channel_id=1, source_target_pairs={{0,2},{1,3},{2,0},{3,1},{4,6},{5,7},{6,4},{7,5},{8,10},{9,11},{10,... | collective-permute-start | bytes 98312 | tf_op jit(solution)/shard_map/ppermute | solution.py:450
  62.8 11.1 %collective-permute-start.25 = (bf16[1536,128]{1,0:T(8,128)(2,1)S(1)}, bf16[1536,128]{1,0:T(8,128)(2,1)S(1)}, u32[]{:S(2)}, u32[]{:S(2)}) collective-permute-start(bf16[1536,128]{1,0:T(8,128)(2,1)S(1)} %copy-done.2), channel_id=1, source_target_pairs={{0,2},{1,3},{2,0},{3,1},{4,6},{5,7},{6,4},{7,5},{8,10},{9,11},{10,... | collective-permute-start | bytes 1179656 | tf_op jit(solution)/shard_map/ppermute | solution.py:450
  63.9 5.7 %collective-permute-start.18 = (bf16[1024,128]{1,0:T(8,128)(2,1)S(1)}, bf16[1024,128]{1,0:T(8,128)(2,1)S(1)}, u32[]{:S(2)}, u32[]{:S(2)}) collective-permute-start(bf16[1024,128]{1,0:T(8,128)(2,1)S(1)} %copy-done.4), channel_id=1, source_target_pairs={{0,1},{1,0},{2,3},{3,2},{4,5},{5,4},{6,7},{7,6},{8,9},{9,8},{10,11... | collective-permute-start | bytes 786440 | tf_op jit(solution)/shard_map/ppermute | solution.py:450
  64.5 9.4 %collective-permute-start.20 = (bf16[1024,128]{1,0:T(8,128)(2,1)S(1)}, bf16[1024,128]{1,0:T(8,128)(2,1)S(1)}, u32[]{:S(2)}, u32[]{:S(2)}) collective-permute-start(bf16[1024,128]{1,0:T(8,128)(2,1)S(1)} %collective-permute-done.19.refs_12_), channel_id=1, source_target_pairs={{0,1},{1,0},{2,3},{3,2},{4,5},{5,4},{6,7},{7,6},{8,9},{9,8},{10,11... | collective-permute-start | bytes 786440 | tf_op jit(solution)/shard_map/ppermute | solution.py:450
  65.6 12.9 %collective-permute-start.15 = (bf16[128,512]{1,0:T(8,128)(2,1)S(1)}, bf16[128,512]{1,0:T(8,128)(2,1)S(1)}, u32[]{:S(2)}, u32[]{:S(2)}) collective-permute-start(bf16[128,512]{1,0:T(8,128)(2,1)S(1)} %get-tuple-element.41), channel_id=1, source_target_pairs={{0,16},{4,20},{8,24},{12,28},{16,0},{20,4},{24,8},{28,12},{1,17},{... | collective-permute-start | bytes 393224 | tf_op jit(solution)/shard_map/ppermute | solution.py:450
  68.3 10.3 %collective-permute-start.16 = (bf16[128,512]{1,0:T(8,128)(2,1)S(1)}, bf16[128,512]{1,0:T(8,128)(2,1)S(1)}, u32[]{:S(2)}, u32[]{:S(2)}) collective-permute-start(bf16[128,512]{1,0:T(8,128)(2,1)S(1)} %get-tuple-element.42), channel_id=1, source_target_pairs={{0,24},{4,28},{8,16},{12,20},{16,8},{20,12},{24,0},{28,4},{1,25},{... | collective-permute-start | bytes 393224 | tf_op jit(solution)/shard_map/ppermute | solution.py:450
  69.6 9.6 %collective-permute-start.17 = (bf16[128,512]{1,0:T(8,128)(2,1)S(1)}, bf16[128,512]{1,0:T(8,128)(2,1)S(1)}, u32[]{:S(2)}, u32[]{:S(2)}) collective-permute-start(bf16[128,512]{1,0:T(8,128)(2,1)S(1)} %get-tuple-element.43), channel_id=1, source_target_pairs={{0,8},{4,12},{8,0},{12,4},{16,24},{20,28},{24,16},{28,20},{1,9},{5... | collective-permute-start | bytes 393224 | tf_op jit(solution)/shard_map/ppermute | solution.py:450
  73.9 30.5 %collective-permute-start.24 = (bf16[1536,128]{1,0:T(8,128)(2,1)S(1)}, bf16[1536,128]{1,0:T(8,128)(2,1)S(1)}, u32[]{:S(2)}, u32[]{:S(2)}) collective-permute-start(bf16[1536,128]{1,0:T(8,128)(2,1)S(1)} %copy-done.2), channel_id=1, source_target_pairs={{0,1},{1,0},{2,3},{3,2},{4,5},{5,4},{6,7},{7,6},{8,9},{9,8},{10,11... | collective-permute-start | bytes 1179656 | tf_op jit(solution)/shard_map/ppermute | solution.py:450
  73.9 30.5 %collective-permute-start.26 = (bf16[1536,128]{1,0:T(8,128)(2,1)S(1)}, bf16[1536,128]{1,0:T(8,128)(2,1)S(1)}, u32[]{:S(2)}, u32[]{:S(2)}) collective-permute-start(bf16[1536,128]{1,0:T(8,128)(2,1)S(1)} %collective-permute-done.25.w2), channel_id=1, source_target_pairs={{0,1},{1,0},{2,3},{3,2},{4,5},{5,4},{6,7},{7,6},{8,9},{9,8},{10,11... | collective-permute-start | bytes 1179656 | tf_op jit(solution)/shard_map/ppermute | solution.py:450
  87.4 7.1 %collective-permute-start.27 = (bf16[64,512]{1,0:T(8,128)(2,1)S(1)}, bf16[64,512]{1,0:T(8,128)(2,1)S(1)}, u32[]{:S(2)}, u32[]{:S(2)}) collective-permute-start(bf16[64,512]{1,0:T(8,128)(2,1)S(1)} %get-tuple-element.47), channel_id=1, source_target_pairs={{0,28},{1,25},{2,30},{3,27},{4,24},{5,29},{6,26},{7,31},{8,20},{9,... | collective-permute-start | bytes 196616 | tf_op jit(solution)/shard_map/ppermute | solution.py:522
  90.7 7.1 %collective-permute-start.28 = (bf16[64,512]{1,0:T(8,128)(2,1)S(1)}, bf16[64,512]{1,0:T(8,128)(2,1)S(1)}, u32[]{:S(2)}, u32[]{:S(2)}) collective-permute-start(bf16[64,512]{1,0:T(8,128)(2,1)S(1)} %get-tuple-element.48), channel_id=1, source_target_pairs={{0,16},{1,21},{2,18},{3,23},{4,20},{5,17},{6,22},{7,19},{8,24},{9,... | collective-permute-start | bytes 196616 | tf_op jit(solution)/shard_map/ppermute | solution.py:522
  91.9 7.0 %collective-permute-start.29 = (bf16[64,512]{1,0:T(8,128)(2,1)S(1)}, bf16[64,512]{1,0:T(8,128)(2,1)S(1)}, u32[]{:S(2)}, u32[]{:S(2)}) collective-permute-start(bf16[64,512]{1,0:T(8,128)(2,1)S(1)} %get-tuple-element.49), channel_id=1, source_target_pairs={{0,12},{1,9},{2,14},{3,11},{4,8},{5,13},{6,10},{7,15},{8,4},{9,1},... | collective-permute-start | bytes 196616 | tf_op jit(solution)/shard_map/ppermute | solution.py:522
  97.9 5.5 %collective-permute-start.33 = (bf16[512,128]{1,0:T(8,128)(2,1)S(1)}, bf16[512,128]{1,0:T(8,128)(2,1)S(1)}, u32[]{:S(2)}, u32[]{:S(2)}) collective-permute-start(bf16[512,128]{1,0:T(8,128)(2,1)S(1)} %copy-done.6), channel_id=1, source_target_pairs={{0,2},{1,3},{2,0},{3,1},{4,6},{5,7},{6,4},{7,5},{8,10},{9,11},{10,... | collective-permute-start | bytes 393224 | tf_op jit(solution)/shard_map/ppermute | solution.py:450
  99.0 8.5 %collective-permute-start.31 = (bf16[256,512]{1,0:T(8,128)(2,1)S(1)}, bf16[256,512]{1,0:T(8,128)(2,1)S(1)}, u32[]{:S(2)}, u32[]{:S(2)}) collective-permute-start(bf16[256,512]{1,0:T(8,128)(2,1)S(1)} %shard_map.274.halo_a), channel_id=1, source_target_pairs={{0,1},{1,0},{2,3},{3,2},{4,5},{5,4},{6,7},{7,6},{8,9},{9,8},{10,11... | collective-permute-start | bytes 786440 | tf_op jit(solution)/shard_map/ppermute | solution.py:450
  99.1 8.4 %collective-permute-start.32 = (bf16[512,128]{1,0:T(8,128)(2,1)S(1)}, bf16[512,128]{1,0:T(8,128)(2,1)S(1)}, u32[]{:S(2)}, u32[]{:S(2)}) collective-permute-start(bf16[512,128]{1,0:T(8,128)(2,1)S(1)} %copy-done.6), channel_id=1, source_target_pairs={{0,1},{1,0},{2,3},{3,2},{4,5},{5,4},{6,7},{7,6},{8,9},{9,8},{10,11... | collective-permute-start | bytes 393224 | tf_op jit(solution)/shard_map/ppermute | solution.py:450
  103.4 14.0 %collective-permute-start.38 = (bf16[1024,128]{1,0:T(8,128)(2,1)S(1)}, bf16[1024,128]{1,0:T(8,128)(2,1)S(1)}, u32[]{:S(2)}, u32[]{:S(2)}) collective-permute-start(bf16[1024,128]{1,0:T(8,128)(2,1)S(1)} %copy-done.3), channel_id=1, source_target_pairs={{0,2},{1,3},{2,0},{3,1},{4,6},{5,7},{6,4},{7,5},{8,10},{9,11},{10,... | collective-permute-start | bytes 786440 | tf_op jit(solution)/shard_map/ppermute | solution.py:450
  111.3 6.6 %collective-permute-start.35 = (bf16[2,128,512]{2,1,0:T(8,128)(2,1)S(1)}, bf16[2,128,512]{2,1,0:T(8,128)(2,1)S(1)}, u32[]{:S(2)}, u32[]{:S(2)}) collective-permute-start(bf16[2,128,512]{2,1,0:T(8,128)(2,1)S(1)} %get-tuple-element.51), channel_id=1, source_target_pairs={{0,1},{1,0},{2,3},{3,2},{4,5},{5,4},{6,7},{7,6},{8,9},{9,8},{10,11... | collective-permute-start | bytes 786440 | tf_op jit(solution)/shard_map/ppermute | solution.py:450
  111.9 5.5 %collective-permute-start.41 = (bf16[128,512]{1,0:T(8,128)(2,1)S(1)}, bf16[128,512]{1,0:T(8,128)(2,1)S(1)}, u32[]{:S(2)}, u32[]{:S(2)}) collective-permute-start(bf16[128,512]{1,0:T(8,128)(2,1)S(1)} %copy-done.7), channel_id=1, source_target_pairs={{0,2},{1,3},{2,0},{3,1},{4,6},{5,7},{6,4},{7,5},{8,10},{9,11},{10,... | collective-permute-start | bytes 393224 | tf_op jit(solution)/shard_map/ppermute | solution.py:450
  112.9 6.1 %collective-permute-start.37 = (bf16[1024,128]{1,0:T(8,128)(2,1)S(1)}, bf16[1024,128]{1,0:T(8,128)(2,1)S(1)}, u32[]{:S(2)}, u32[]{:S(2)}) collective-permute-start(bf16[1024,128]{1,0:T(8,128)(2,1)S(1)} %copy-done.3), channel_id=1, source_target_pairs={{0,1},{1,0},{2,3},{3,2},{4,5},{5,4},{6,7},{7,6},{8,9},{9,8},{10,11... | collective-permute-start | bytes 786440 | tf_op jit(solution)/shard_map/ppermute | solution.py:450
  112.9 6.1 %collective-permute-start.40 = (bf16[128,512]{1,0:T(8,128)(2,1)S(1)}, bf16[128,512]{1,0:T(8,128)(2,1)S(1)}, u32[]{:S(2)}, u32[]{:S(2)}) collective-permute-start(bf16[128,512]{1,0:T(8,128)(2,1)S(1)} %copy-done.7), channel_id=1, source_target_pairs={{0,1},{1,0},{2,3},{3,2},{4,5},{5,4},{6,7},{7,6},{8,9},{9,8},{10,11... | collective-permute-start | bytes 393224 | tf_op jit(solution)/shard_map/ppermute | solution.py:450
  117.9 5.5 %collective-permute-start.36 = (bf16[128,512]{1,0:T(8,128)(2,1)S(1)}, bf16[128,512]{1,0:T(8,128)(2,1)S(1)}, u32[]{:S(2)}, u32[]{:S(2)}) collective-permute-start(bf16[128,512]{1,0:T(8,128)(2,1)S(1)} %fusion.2), channel_id=1, source_target_pairs={{0,2},{1,3},{2,0},{3,1},{4,6},{5,7},{6,4},{7,5},{8,10},{9,11},{10,... | collective-permute-start | bytes 393224 | tf_op jit(solution)/shard_map/ppermute | solution.py:450
  (42 other events, 565.8 us)

commit v5 on v4

--- a/solution.py
+++ b/solution.py
@@ -173,7 +173,7 @@
     rows = rows_ref[...]
     table = dot(rows, win[...]).astype(BF16)
     edges = meta_ref.shape[1]
-    block = CHUNK
+    block = 4 * CHUNK
     for i in range(edges // block):
         at = slice(i * block, (i + 1) * block)
         places = jnp.transpose(meta_ref[:, at].astype(F32))
@@ -322,7 +322,7 @@
 
 
 def near_kernel(edge_hbm, mid_ref, ends_ref, bias_ref, w0, w1, w2, w3, out_ref, win, edge_ref, sem):
-    block = CHUNK
+    block = 2 * CHUNK
     edges, width = edge_ref.shape
     loads = []
     for i in range(edges // block):
@@ -371,7 +371,7 @@
     flips = [jnp.where(core == 0, a, b) for a, b in (flips, flips[::-1])]
     names = [mesh_rows + (lat ^ flip) * halo_cap + lane % halo_cap for flip in flips]
     edges = edge_ref.shape[0]
-    block = 256
+    block = 2 * CHUNK
     for i in range(edges // block):
         at = slice(i * block, (i + 1) * block)
         pre = pre_ref[at, :]

time: 130 us -> 129 us (level)
  Pallas kernels: 26.3 us -> 24.9 us
  transfers between devices with their start and end apart: 46 -> 46, of which waited for: 20 -> 19; matrix products, arithmetic and copies ran while one was open for 0% -> 0% of each run, Pallas kernels for 13% -> 13%
where the time goes in v5:
time: 129 us; the launch traced here: 128 us
  waiting for transfers between devices  59.3 us (46%)
  starting transfers between devices  35.1 us (27%)
  Pallas kernels  24.9 us (19%)
  blocking collectives  6.82 us (5%)
    ppermute x42, waiting for transfers between devices, hop(): return lax.ppermute(values, axis, [(i, i ^ flip) for i in range(size)])  55.4 us
    ppermute x42, starting transfers between devices, hop(): return lax.ppermute(values, axis, [(i, i ^ flip) for i in range(size)])  28.6 us
    all_gather x1, blocking collectives, local(): mid_all = lax.all_gather(mid, LON, axis=0, tiled=True)  6.82 us
    pallas_call x2, Pallas kernels, node_sums(): call(functools.partial(sums_kernel, mesh_rows, 2 * edges // lat_count, ke...  6.55 us
    ppermute x4, starting transfers between devices, halo_hop(): return lax.ppermute(picked[j], (LAT, LON), pairs)  6.51 us
    pallas_call x1, Pallas kernels, local(): call(functools.partial(open_kernel, lat_count, mesh_rows), [like(edges //...  4.9 us
    pallas_call x1, Pallas kernels, local(): call(functools.partial(message_kernel, grid_feat.shape[0]), like(edges, w...  3.93 us
    ppermute x4, waiting for transfers between devices, halo_hop(): return lax.ppermute(picked[j], (LAT, LON), pairs)  3.91 us
  transfers between devices with their start and end apart: 46, of which 19 were waited for; matrix products, arithmetic and copies ran while one was open for 0% of the time, Pallas kernels for 13%

profile of v5, /device:TPU:0, one launch (start us, length us, event | category | flops | bytes accessed | tf_op | source)
XLA Modules:
  0.0 128.4 jit_solution(8737129965303541048)
XLA Ops:
  0.7 3.0 %collective-permute-start.5 = (bf16[512,128]{1,0:T(8,128)(2,1)}, bf16[512,128]{1,0:T(8,128)(2,1)S(1)}, u32[]{:S(2)}, u32[]{:S(2)}) collective-permute-start(bf16[512,128]{1,0:T(8,128)(2,1)} %w0.3), channel_id=1, source_target_pairs={{0,2},{1,3},{2,0},{3,1},{4,6},{5,7},{6,4},{7,5},{8,10},{9,11},{10,... | collective-permute-start | bytes 393224 | tf_op jit(solution)/shard_map/ppermute | solution.py:450
  4.3 4.0 %collective-permute-done.5.w2 = bf16[512,128]{1,0:T(8,128)(2,1)S(1)} collective-permute-done((bf16[512,128]{1,0:T(8,128)(2,1)}, bf16[512,128]{1,0:T(8,128)(2,1)S(1)}, u32[]{:S(2)}, u32[]{:S(2)}) %collective-permute-start.5) | collective-permute-done | bytes 131104 | tf_op jit(solution)/shard_map/ppermute | solution.py:450
  8.3 2.0 %collective-permute-done.8.v2 = bf16[512,128]{1,0:T(8,128)(2,1)S(1)} collective-permute-done((bf16[512,128]{1,0:T(8,128)(2,1)}, bf16[512,128]{1,0:T(8,128)(2,1)S(1)}, u32[]{:S(2)}, u32[]{:S(2)}) %collective-permute-start.8) | collective-permute-done | bytes 131104 | tf_op jit(solution)/shard_map/ppermute | solution.py:450
  10.2 4.9 %shard_map.266 = (s32[24,128]{1,0:T(8,128)}, bf16[16,2048]{1,0:T(8,128)(2,1)}, s32[1024,8]{1,0:T(8,128)}, s32[512,1]{1,0:T(8,128)}, bf16[128,128]{1,0:T(8,128)(2...) custom-call(s32[1,2048]{1,0:T(1,128)} %bitcast.24, s32[1,2048]{1,0:T(1,128)} %bitcast.25, ...), custom_call_target="tpu_custom_call" | custom-call | flops 1073741824 | bytes 4194304 | tf_op jit(solution)/shard_map/pallas_call | solution.py:460
  16.1 3.9 %shard_map.267.msg_a = bf16[2048,512]{1,0:T(8,128)(2,1)S(1)} custom-call(bf16[512,512]{1,0:T(8,128)(2,1)S(1)} %copy-done.17, bf16[16,2048]{1,0:T(8,128)(2,1)S(1)} %copy-done.24, bf16[4,512]{1,0:T(4,128)(2,1)S(1)} %copy-done.20, f32[2,512]{1,0:T(2,128)S(1)} %copy-done.21, f32[1,512]{1,0:T(1,128)S(1)} %bitcast.23, bf16[512,128]{1,0:T(8,128)(2,1)S(1)} %copy-done.18, ...), custom_call_target="tpu_custom_call" | custom-call | flops 2147483648 | bytes 4194304 | tf_op jit(solution)/shard_map/pallas_call | solution.py:482
  20.7 3.7 %collective-permute-done.3.start_b.table_b = s32[24,128]{1,0:T(8,128)S(1)} collective-permute-done((s32[24,128]{1,0:T(8,128)S(1)}, s32[24,128]{1,0:T(8,128)S(1)}, u32[]{:S(2)}, u32[]{:S(2)}) %collective-permute-start.3) | collective-permute-done | bytes 12320 | tf_op jit(solution)/shard_map/ppermute | solution.py:450
  24.4 3.3 %shard_map.269 = (bf16[2,4,64,512]{3,2,1,0:T(8,128)(2,1)S(1)}, bf16[2,4,64,512]{3,2,1,0:T(8,128)(2,1)S(1)}) custom-call(s32[24,128]{1,0:T(8,128)S(1)} %copy-done.5, s32[24,128]{1,0:T(8,128)S(1)} %collective-permute-done.3.start_b.table_b, s32[24,128]{1,0:T(8,128)S(1)} %copy-done.5, s32[24,128]{1,0:T(8,128)S(1)} %collective-permute-done.3.start_b.table_b, ...), custom_call_target="tpu_custom_call" | custom-call | flops 1073741824 | bytes 4194304 | tf_op jit(solution)/shard_map/pallas_call | solution.py:238
  27.7 1.8 %collective-permute-start.13 = (bf16[2,4,64,512]{3,2,1,0:T(8,128)(2,1)S(1)}, bf16[2,4,64,512]{3,2,1,0:T(8,128)(2,1)S(1)}, u32[]{:S(2)}, u32[]{:S(2)}) collective-permute-start(bf16[2,4,64,512]{3,2,1,0:T(8,128)(2,1)S(1)} %get-tuple-element.39), channel_id=1, source_target_pairs={{0,4},{4,0},{8,12},{12,8},{16,20},{20,16},{24,28},{28,24},{1,5},{5... | collective-permute-start | bytes 1572872 | tf_op jit(solution)/shard_map/ppermute | solution.py:450
  29.5 1.6 %collective-permute-start.11 = (bf16[2,4,64,512]{3,2,1,0:T(8,128)(2,1)S(1)}, bf16[2,4,64,512]{3,2,1,0:T(8,128)(2,1)S(1)}, u32[]{:S(2)}, u32[]{:S(2)}) collective-permute-start(bf16[2,4,64,512]{3,2,1,0:T(8,128)(2,1)S(1)} %get-tuple-element.37), channel_id=1, source_target_pairs={{0,2},{1,3},{2,0},{3,1},{4,6},{5,7},{6,4},{7,5},{8,10},{9,11},{10,... | collective-permute-start | bytes 1572872 | tf_op jit(solution)/shard_map/ppermute | solution.py:450
  31.6 3.3 %shard_map.268 = (bf16[2,4,64,512]{3,2,1,0:T(8,128)(2,1)S(1)}, bf16[2,4,64,512]{3,2,1,0:T(8,128)(2,1)S(1)}) custom-call(s32[24,128]{1,0:T(8,128)S(1)} %copy-done.5, s32[24,128]{1,0:T(8,128)S(1)} %collective-permute-done.3.start_b.table_b, s32[24,128]{1,0:T(8,128)S(1)} %copy-done.5, s32[24,128]{1,0:T(8,128)S(1)} %collective-permute-done.3.start_b.table_b, ...), custom_call_target="tpu_custom_call" | custom-call | flops 1073741824 | bytes 4194304 | tf_op jit(solution)/shard_map/pallas_call | solution.py:238
  34.9 7.1 %collective-permute-done.13.got_y = bf16[2,4,64,512]{3,2,1,0:T(8,128)(2,1)S(1)} collective-permute-done((bf16[2,4,64,512]{3,2,1,0:T(8,128)(2,1)S(1)}, bf16[2,4,64,512]{3,2,1,0:T(8,128)(2,1)S(1)}, u32[]{:S(2)}, u32[]{:S(2)}) %collective-permute-start.13) | collective-permute-done | bytes 524320 | tf_op jit(solution)/shard_map/ppermute | solution.py:450
  42.1 1.7 %collective-permute-start.14 = (bf16[4,64,512]{2,1,0:T(8,128)(2,1)S(1)}, bf16[4,64,512]{2,1,0:T(8,128)(2,1)S(1)}, u32[]{:S(2)}, u32[]{:S(2)}) collective-permute-start(bf16[4,64,512]{2,1,0:T(8,128)(2,1)S(1)} %fusion.1), channel_id=1, source_target_pairs={{0,2},{1,3},{2,0},{3,1},{4,6},{5,7},{6,4},{7,5},{8,10},{9,11},{10,... | collective-permute-start | bytes 786440 | tf_op jit(solution)/shard_map/ppermute | solution.py:450
  46.6 1.2 collective-permute-done.refs_1_
  48.7 9.6 %collective-permute-done.1.refs_2_ = bf16[128,128]{1,0:T(8,128)(2,1)S(1)} collective-permute-done((bf16[128,128]{1,0:T(8,128)(2,1)S(1)}, bf16[128,128]{1,0:T(8,128)(2,1)S(1)}, u32[]{:S(2)}, u32[]{:S(2)}) %collective-permute-start.1) | collective-permute-done | bytes 32800 | tf_op jit(solution)/shard_map/ppermute | solution.py:450
  58.6 3.3 %collective-permute-done.2.refs_3_ = bf16[128,128]{1,0:T(8,128)(2,1)S(1)} collective-permute-done((bf16[128,128]{1,0:T(8,128)(2,1)S(1)}, bf16[128,128]{1,0:T(8,128)(2,1)S(1)}, u32[]{:S(2)}, u32[]{:S(2)}) %collective-permute-start.2) | collective-permute-done | bytes 32800 | tf_op jit(solution)/shard_map/ppermute | solution.py:450
  64.8 2.6 %collective-permute-start.15 = (bf16[128,512]{1,0:T(8,128)(2,1)S(1)}, bf16[128,512]{1,0:T(8,128)(2,1)S(1)}, u32[]{:S(2)}, u32[]{:S(2)}) collective-permute-start(bf16[128,512]{1,0:T(8,128)(2,1)S(1)} %get-tuple-element.41), channel_id=1, source_target_pairs={{0,16},{4,20},{8,24},{12,28},{16,0},{20,4},{24,8},{28,12},{1,17},{... | collective-permute-start | bytes 393224 | tf_op jit(solution)/shard_map/ppermute | solution.py:450
  67.5 1.3 %collective-permute-start.16 = (bf16[128,512]{1,0:T(8,128)(2,1)S(1)}, bf16[128,512]{1,0:T(8,128)(2,1)S(1)}, u32[]{:S(2)}, u32[]{:S(2)}) collective-permute-start(bf16[128,512]{1,0:T(8,128)(2,1)S(1)} %get-tuple-element.42), channel_id=1, source_target_pairs={{0,24},{4,28},{8,16},{12,20},{16,8},{20,12},{24,0},{28,4},{1,25},{... | collective-permute-start | bytes 393224 | tf_op jit(solution)/shard_map/ppermute | solution.py:450
  69.1 4.0 %collective-permute-done.25.w2 = bf16[1536,128]{1,0:T(8,128)(2,1)S(1)} collective-permute-done((bf16[1536,128]{1,0:T(8,128)(2,1)S(1)}, bf16[1536,128]{1,0:T(8,128)(2,1)S(1)}, u32[]{:S(2)}, u32[]{:S(2)}) %collective-permute-start.25) | collective-permute-done | bytes 393248 | tf_op jit(solution)/shard_map/ppermute | solution.py:450
  73.6 4.1 %collective-permute-done.15.refs_5_ = bf16[128,512]{1,0:T(8,128)(2,1)S(1)} collective-permute-done((bf16[128,512]{1,0:T(8,128)(2,1)S(1)}, bf16[128,512]{1,0:T(8,128)(2,1)S(1)}, u32[]{:S(2)}, u32[]{:S(2)}) %collective-permute-start.15) | collective-permute-done | bytes 131104 | tf_op jit(solution)/shard_map/ppermute | solution.py:450
  79.3 6.8 %all_gather.3.mid_ref.table_ref = bf16[512,512]{1,0:T(8,128)(2,1)S(1)} all-gather(bf16[128,512]{1,0:T(8,128)(2,1)S(1)} %shard_map.271.refs_0_), channel_id=1, replica_groups=mesh['lat'=8,'lon'=4] {'lon'}, dimensions={0}, use_global_device_ids=true | all-gather | bytes 655360 | tf_op jit(solution)/shard_map/all_gather | solution.py:505
  86.7 3.3 %collective-permute-start.27 = (bf16[64,512]{1,0:T(8,128)(2,1)S(1)}, bf16[64,512]{1,0:T(8,128)(2,1)S(1)}, u32[]{:S(2)}, u32[]{:S(2)}) collective-permute-start(bf16[64,512]{1,0:T(8,128)(2,1)S(1)} %get-tuple-element.47), channel_id=1, source_target_pairs={{0,28},{1,25},{2,30},{3,27},{4,24},{5,29},{6,26},{7,31},{8,20},{9,... | collective-permute-start | bytes 196616 | tf_op jit(solution)/shard_map/ppermute | solution.py:522
  91.1 1.4 %collective-permute-start.29 = (bf16[64,512]{1,0:T(8,128)(2,1)S(1)}, bf16[64,512]{1,0:T(8,128)(2,1)S(1)}, u32[]{:S(2)}, u32[]{:S(2)}) collective-permute-start(bf16[64,512]{1,0:T(8,128)(2,1)S(1)} %get-tuple-element.49), channel_id=1, source_target_pairs={{0,12},{1,9},{2,14},{3,11},{4,8},{5,13},{6,10},{7,15},{8,4},{9,1},... | collective-permute-start | bytes 196616 | tf_op jit(solution)/shard_map/ppermute | solution.py:522
  92.5 1.2 collective-permute-done.27.refs_0_
  94.4 2.7 %collective-permute-done.28.refs_1_ = bf16[64,512]{1,0:T(8,128)(2,1)S(1)} collective-permute-done((bf16[64,512]{1,0:T(8,128)(2,1)S(1)}, bf16[64,512]{1,0:T(8,128)(2,1)S(1)}, u32[]{:S(2)}, u32[]{:S(2)}) %collective-permute-start.28) | collective-permute-done | bytes 65568 | tf_op jit(solution)/shard_map/ppermute | solution.py:522
  98.8 3.9 %collective-permute-done.33.v2 = bf16[512,128]{1,0:T(8,128)(2,1)S(1)} collective-permute-done((bf16[512,128]{1,0:T(8,128)(2,1)S(1)}, bf16[512,128]{1,0:T(8,128)(2,1)S(1)}, u32[]{:S(2)}, u32[]{:S(2)}) %collective-permute-start.33) | collective-permute-done | bytes 131104 | tf_op jit(solution)/shard_map/ppermute | solution.py:450
  103.6 2.8 %shard_map.272.pre_ref = f32[1024,512]{1,0:T(8,128)S(1)} custom-call(bf16[1024,512]{1,0:T(8,128)(2,1)S(1)} %copy-done, bf16[512,512]{1,0:T(8,128)(2,1)S(1)} %all_gather.3.mid_ref.table_ref, s32[1024,8]{1,0:T(8,128)S(1)} %copy-done.1, f32[2,512]{1,0:T(2,128)S(1)} %copy-done.13, bf16[1536,128]{1,0:T(8,128)(2,1)S(1)} %copy-done.2, ...), custom_call_target="tpu_custom_call" | custom-call | flops 1610612736 | bytes 4194304 | tf_op jit(solution)/shard_map/pallas_call | solution.py:525
  106.5 3.5 %shard_map.275 = (bf16[1024,512]{1,0:T(8,128)(2,1)}, bf16[2,128,512]{2,1,0:T(8,128)(2,1)S(1)}, bf16[128,512]{1,0:T(8,128)(2,1)S(1)}, bf16[128,512]{1,0:T(8,128)(2,1)S(1)}) custom-call(bf16[1024,512]{1,0:T(8,128)(2,1)S(1)} %copy-done, f32[1024,512]{1,0:T(8,128)S(1)} %shard_map.272.pre_ref, bf16[256,512]{1,0:T(8,128)(2,1)S(1)} %shard_map.274.halo_a, ...), custom_call_target="tpu_custom_call" | custom-call | flops 1610612736 | bytes 4194304 | tf_op jit(solution)/shard_map/pallas_call | solution.py:539
  112.3 3.8 %collective-permute-done.41.refs_12_ = bf16[128,512]{1,0:T(8,128)(2,1)S(1)} collective-permute-done((bf16[128,512]{1,0:T(8,128)(2,1)S(1)}, bf16[128,512]{1,0:T(8,128)(2,1)S(1)}, u32[]{:S(2)}, u32[]{:S(2)}) %collective-permute-start.41) | collective-permute-done | bytes 131104 | tf_op jit(solution)/shard_map/ppermute | solution.py:450
  116.7 1.2 collective-permute-start.36
  117.9 4.2 %collective-permute-done.36.refs_3_ = bf16[128,512]{1,0:T(8,128)(2,1)S(1)} collective-permute-done((bf16[128,512]{1,0:T(8,128)(2,1)S(1)}, bf16[128,512]{1,0:T(8,128)(2,1)S(1)}, u32[]{:S(2)}, u32[]{:S(2)}) %collective-permute-start.36) | collective-permute-done | bytes 131104 | tf_op jit(solution)/shard_map/ppermute | solution.py:450
  123.1 1.2 collective-permute-start.44
  125.0 2.1 %collective-permute-done.44.refs_2_ = bf16[128,128]{1,0:T(8,128)(2,1)S(1)} collective-permute-done((bf16[128,128]{1,0:T(8,128)(2,1)S(1)}, bf16[128,128]{1,0:T(8,128)(2,1)S(1)}, u32[]{:S(2)}, u32[]{:S(2)}) %collective-permute-start.44) | collective-permute-done | bytes 32800 | tf_op jit(solution)/shard_map/ppermute | solution.py:450
  (132 shorter events, 22.5 us)
Async XLA Ops:
  0.7 7.6 %collective-permute-start.5 = (bf16[512,128]{1,0:T(8,128)(2,1)}, bf16[512,128]{1,0:T(8,128)(2,1)S(1)}, u32[]{:S(2)}, u32[]{:S(2)}) collective-permute-start(bf16[512,128]{1,0:T(8,128)(2,1)} %w0.3), channel_id=1, source_target_pairs={{0,2},{1,3},{2,0},{3,1},{4,6},{5,7},{6,4},{7,5},{8,10},{9,11},{10,... | collective-permute-start | bytes 393224 | tf_op jit(solution)/shard_map/ppermute | solution.py:450
  3.7 6.5 %collective-permute-start.8 = (bf16[512,128]{1,0:T(8,128)(2,1)}, bf16[512,128]{1,0:T(8,128)(2,1)S(1)}, u32[]{:S(2)}, u32[]{:S(2)}) collective-permute-start(bf16[512,128]{1,0:T(8,128)(2,1)} %v0.2), channel_id=1, source_target_pairs={{0,2},{1,3},{2,0},{3,1},{4,6},{5,7},{6,4},{7,5},{8,10},{9,11},{10,... | collective-permute-start | bytes 393224 | tf_op jit(solution)/shard_map/ppermute | solution.py:450
  3.8 11.3 %collective-permute-start.4 = (bf16[512,128]{1,0:T(8,128)(2,1)}, bf16[512,128]{1,0:T(8,128)(2,1)S(1)}, u32[]{:S(2)}, u32[]{:S(2)}) collective-permute-start(bf16[512,128]{1,0:T(8,128)(2,1)} %w0.3), channel_id=1, source_target_pairs={{0,1},{1,0},{2,3},{3,2},{4,5},{5,4},{6,7},{7,6},{8,9},{9,8},{10,11... | collective-permute-start | bytes 393224 | tf_op jit(solution)/shard_map/ppermute | solution.py:450
  3.8 11.4 %collective-permute-start.7 = (bf16[512,128]{1,0:T(8,128)(2,1)}, bf16[512,128]{1,0:T(8,128)(2,1)S(1)}, u32[]{:S(2)}, u32[]{:S(2)}) collective-permute-start(bf16[512,128]{1,0:T(8,128)(2,1)} %v0.2), channel_id=1, source_target_pairs={{0,1},{1,0},{2,3},{3,2},{4,5},{5,4},{6,7},{7,6},{8,9},{9,8},{10,11... | collective-permute-start | bytes 393224 | tf_op jit(solution)/shard_map/ppermute | solution.py:450
  8.3 6.9 %collective-permute-start.6 = (bf16[512,128]{1,0:T(8,128)(2,1)S(1)}, bf16[512,128]{1,0:T(8,128)(2,1)S(1)}, u32[]{:S(2)}, u32[]{:S(2)}) collective-permute-start(bf16[512,128]{1,0:T(8,128)(2,1)S(1)} %collective-permute-done.5.w2), channel_id=1, source_target_pairs={{0,1},{1,0},{2,3},{3,2},{4,5},{5,4},{6,7},{7,6},{8,9},{9,8},{10,11... | collective-permute-start | bytes 393224 | tf_op jit(solution)/shard_map/ppermute | solution.py:450
  27.7 14.3 %collective-permute-start.13 = (bf16[2,4,64,512]{3,2,1,0:T(8,128)(2,1)S(1)}, bf16[2,4,64,512]{3,2,1,0:T(8,128)(2,1)S(1)}, u32[]{:S(2)}, u32[]{:S(2)}) collective-permute-start(bf16[2,4,64,512]{3,2,1,0:T(8,128)(2,1)S(1)} %get-tuple-element.39), channel_id=1, source_target_pairs={{0,4},{4,0},{8,12},{12,8},{16,20},{20,16},{24,28},{28,24},{1,5},{5... | collective-permute-start | bytes 1572872 | tf_op jit(solution)/shard_map/ppermute | solution.py:450
  29.5 14.9 %collective-permute-start.11 = (bf16[2,4,64,512]{3,2,1,0:T(8,128)(2,1)S(1)}, bf16[2,4,64,512]{3,2,1,0:T(8,128)(2,1)S(1)}, u32[]{:S(2)}, u32[]{:S(2)}) collective-permute-start(bf16[2,4,64,512]{3,2,1,0:T(8,128)(2,1)S(1)} %get-tuple-element.37), channel_id=1, source_target_pairs={{0,2},{1,3},{2,0},{3,1},{4,6},{5,7},{6,4},{7,5},{8,10},{9,11},{10,... | collective-permute-start | bytes 1572872 | tf_op jit(solution)/shard_map/ppermute | solution.py:450
  31.1 32.0 %collective-permute-start.19 = (bf16[1024,128]{1,0:T(8,128)(2,1)S(1)}, bf16[1024,128]{1,0:T(8,128)(2,1)S(1)}, u32[]{:S(2)}, u32[]{:S(2)}) collective-permute-start(bf16[1024,128]{1,0:T(8,128)(2,1)S(1)} %copy-done.4), channel_id=1, source_target_pairs={{0,2},{1,3},{2,0},{3,1},{4,6},{5,7},{6,4},{7,5},{8,10},{9,11},{10,... | collective-permute-start | bytes 786440 | tf_op jit(solution)/shard_map/ppermute | solution.py:450
  42.1 21.6 %collective-permute-start.14 = (bf16[4,64,512]{2,1,0:T(8,128)(2,1)S(1)}, bf16[4,64,512]{2,1,0:T(8,128)(2,1)S(1)}, u32[]{:S(2)}, u32[]{:S(2)}) collective-permute-start(bf16[4,64,512]{2,1,0:T(8,128)(2,1)S(1)} %fusion.1), channel_id=1, source_target_pairs={{0,2},{1,3},{2,0},{3,1},{4,6},{5,7},{6,4},{7,5},{8,10},{9,11},{10,... | collective-permute-start | bytes 786440 | tf_op jit(solution)/shard_map/ppermute | solution.py:450
  44.5 19.2 %collective-permute-start.12 = (bf16[4,64,512]{2,1,0:T(8,128)(2,1)S(1)}, bf16[4,64,512]{2,1,0:T(8,128)(2,1)S(1)}, u32[]{:S(2)}, u32[]{:S(2)}) collective-permute-start(bf16[4,64,512]{2,1,0:T(8,128)(2,1)S(1)} %fusion), channel_id=1, source_target_pairs={{0,4},{4,0},{8,12},{12,8},{16,20},{20,16},{24,28},{28,24},{1,5},{5... | collective-permute-start | bytes 786440 | tf_op jit(solution)/shard_map/ppermute | solution.py:450
  45.5 17.6 %collective-permute-start.22 = (bf16[128,512]{1,0:T(8,128)(2,1)S(1)}, bf16[128,512]{1,0:T(8,128)(2,1)S(1)}, u32[]{:S(2)}, u32[]{:S(2)}) collective-permute-start(bf16[128,512]{1,0:T(8,128)(2,1)S(1)} %copy-done.8), channel_id=1, source_target_pairs={{0,2},{1,3},{2,0},{3,1},{4,6},{5,7},{6,4},{7,5},{8,10},{9,11},{10,... | collective-permute-start | bytes 393224 | tf_op jit(solution)/shard_map/ppermute | solution.py:450
  47.8 10.5 %collective-permute-start.1 = (bf16[128,128]{1,0:T(8,128)(2,1)S(1)}, bf16[128,128]{1,0:T(8,128)(2,1)S(1)}, u32[]{:S(2)}, u32[]{:S(2)}) collective-permute-start(bf16[128,128]{1,0:T(8,128)(2,1)S(1)} %copy-done.26), channel_id=1, source_target_pairs={{0,2},{1,3},{2,0},{3,1},{4,6},{5,7},{6,4},{7,5},{8,10},{9,11},{10,... | collective-permute-start | bytes 98312 | tf_op jit(solution)/shard_map/ppermute | solution.py:450
  62.0 11.1 %collective-permute-start.25 = (bf16[1536,128]{1,0:T(8,128)(2,1)S(1)}, bf16[1536,128]{1,0:T(8,128)(2,1)S(1)}, u32[]{:S(2)}, u32[]{:S(2)}) collective-permute-start(bf16[1536,128]{1,0:T(8,128)(2,1)S(1)} %copy-done.2), channel_id=1, source_target_pairs={{0,2},{1,3},{2,0},{3,1},{4,6},{5,7},{6,4},{7,5},{8,10},{9,11},{10,... | collective-permute-start | bytes 1179656 | tf_op jit(solution)/shard_map/ppermute | solution.py:450
  63.1 5.7 %collective-permute-start.18 = (bf16[1024,128]{1,0:T(8,128)(2,1)S(1)}, bf16[1024,128]{1,0:T(8,128)(2,1)S(1)}, u32[]{:S(2)}, u32[]{:S(2)}) collective-permute-start(bf16[1024,128]{1,0:T(8,128)(2,1)S(1)} %copy-done.4), channel_id=1, source_target_pairs={{0,1},{1,0},{2,3},{3,2},{4,5},{5,4},{6,7},{7,6},{8,9},{9,8},{10,11... | collective-permute-start | bytes 786440 | tf_op jit(solution)/shard_map/ppermute | solution.py:450
  63.7 9.4 %collective-permute-start.20 = (bf16[1024,128]{1,0:T(8,128)(2,1)S(1)}, bf16[1024,128]{1,0:T(8,128)(2,1)S(1)}, u32[]{:S(2)}, u32[]{:S(2)}) collective-permute-start(bf16[1024,128]{1,0:T(8,128)(2,1)S(1)} %collective-permute-done.19.refs_12_), channel_id=1, source_target_pairs={{0,1},{1,0},{2,3},{3,2},{4,5},{5,4},{6,7},{7,6},{8,9},{9,8},{10,11... | collective-permute-start | bytes 786440 | tf_op jit(solution)/shard_map/ppermute | solution.py:450
  64.8 12.9 %collective-permute-start.15 = (bf16[128,512]{1,0:T(8,128)(2,1)S(1)}, bf16[128,512]{1,0:T(8,128)(2,1)S(1)}, u32[]{:S(2)}, u32[]{:S(2)}) collective-permute-start(bf16[128,512]{1,0:T(8,128)(2,1)S(1)} %get-tuple-element.41), channel_id=1, source_target_pairs={{0,16},{4,20},{8,24},{12,28},{16,0},{20,4},{24,8},{28,12},{1,17},{... | collective-permute-start | bytes 393224 | tf_op jit(solution)/shard_map/ppermute | solution.py:450
  67.5 10.3 %collective-permute-start.16 = (bf16[128,512]{1,0:T(8,128)(2,1)S(1)}, bf16[128,512]{1,0:T(8,128)(2,1)S(1)}, u32[]{:S(2)}, u32[]{:S(2)}) collective-permute-start(bf16[128,512]{1,0:T(8,128)(2,1)S(1)} %get-tuple-element.42), channel_id=1, source_target_pairs={{0,24},{4,28},{8,16},{12,20},{16,8},{20,12},{24,0},{28,4},{1,25},{... | collective-permute-start | bytes 393224 | tf_op jit(solution)/shard_map/ppermute | solution.py:450
  68.8 9.6 %collective-permute-start.17 = (bf16[128,512]{1,0:T(8,128)(2,1)S(1)}, bf16[128,512]{1,0:T(8,128)(2,1)S(1)}, u32[]{:S(2)}, u32[]{:S(2)}) collective-permute-start(bf16[128,512]{1,0:T(8,128)(2,1)S(1)} %get-tuple-element.43), channel_id=1, source_target_pairs={{0,8},{4,12},{8,0},{12,4},{16,24},{20,28},{24,16},{28,20},{1,9},{5... | collective-permute-start | bytes 393224 | tf_op jit(solution)/shard_map/ppermute | solution.py:450
  73.1 30.4 %collective-permute-start.24 = (bf16[1536,128]{1,0:T(8,128)(2,1)S(1)}, bf16[1536,128]{1,0:T(8,128)(2,1)S(1)}, u32[]{:S(2)}, u32[]{:S(2)}) collective-permute-start(bf16[1536,128]{1,0:T(8,128)(2,1)S(1)} %copy-done.2), channel_id=1, source_target_pairs={{0,1},{1,0},{2,3},{3,2},{4,5},{5,4},{6,7},{7,6},{8,9},{9,8},{10,11... | collective-permute-start | bytes 1179656 | tf_op jit(solution)/shard_map/ppermute | solution.py:450
  73.1 30.4 %collective-permute-start.26 = (bf16[1536,128]{1,0:T(8,128)(2,1)S(1)}, bf16[1536,128]{1,0:T(8,128)(2,1)S(1)}, u32[]{:S(2)}, u32[]{:S(2)}) collective-permute-start(bf16[1536,128]{1,0:T(8,128)(2,1)S(1)} %collective-permute-done.25.w2), channel_id=1, source_target_pairs={{0,1},{1,0},{2,3},{3,2},{4,5},{5,4},{6,7},{7,6},{8,9},{9,8},{10,11... | collective-permute-start | bytes 1179656 | tf_op jit(solution)/shard_map/ppermute | solution.py:450
  86.7 7.1 %collective-permute-start.27 = (bf16[64,512]{1,0:T(8,128)(2,1)S(1)}, bf16[64,512]{1,0:T(8,128)(2,1)S(1)}, u32[]{:S(2)}, u32[]{:S(2)}) collective-permute-start(bf16[64,512]{1,0:T(8,128)(2,1)S(1)} %get-tuple-element.47), channel_id=1, source_target_pairs={{0,28},{1,25},{2,30},{3,27},{4,24},{5,29},{6,26},{7,31},{8,20},{9,... | collective-permute-start | bytes 196616 | tf_op jit(solution)/shard_map/ppermute | solution.py:522
  90.0 7.1 %collective-permute-start.28 = (bf16[64,512]{1,0:T(8,128)(2,1)S(1)}, bf16[64,512]{1,0:T(8,128)(2,1)S(1)}, u32[]{:S(2)}, u32[]{:S(2)}) collective-permute-start(bf16[64,512]{1,0:T(8,128)(2,1)S(1)} %get-tuple-element.48), channel_id=1, source_target_pairs={{0,16},{1,21},{2,18},{3,23},{4,20},{5,17},{6,22},{7,19},{8,24},{9,... | collective-permute-start | bytes 196616 | tf_op jit(solution)/shard_map/ppermute | solution.py:522
  91.1 7.0 %collective-permute-start.29 = (bf16[64,512]{1,0:T(8,128)(2,1)S(1)}, bf16[64,512]{1,0:T(8,128)(2,1)S(1)}, u32[]{:S(2)}, u32[]{:S(2)}) collective-permute-start(bf16[64,512]{1,0:T(8,128)(2,1)S(1)} %get-tuple-element.49), channel_id=1, source_target_pairs={{0,12},{1,9},{2,14},{3,11},{4,8},{5,13},{6,10},{7,15},{8,4},{9,1},... | collective-permute-start | bytes 196616 | tf_op jit(solution)/shard_map/ppermute | solution.py:522
  97.1 5.6 %collective-permute-start.33 = (bf16[512,128]{1,0:T(8,128)(2,1)S(1)}, bf16[512,128]{1,0:T(8,128)(2,1)S(1)}, u32[]{:S(2)}, u32[]{:S(2)}) collective-permute-start(bf16[512,128]{1,0:T(8,128)(2,1)S(1)} %copy-done.6), channel_id=1, source_target_pairs={{0,2},{1,3},{2,0},{3,1},{4,6},{5,7},{6,4},{7,5},{8,10},{9,11},{10,... | collective-permute-start | bytes 393224 | tf_op jit(solution)/shard_map/ppermute | solution.py:450
  98.2 8.3 %collective-permute-start.31 = (bf16[256,512]{1,0:T(8,128)(2,1)S(1)}, bf16[256,512]{1,0:T(8,128)(2,1)S(1)}, u32[]{:S(2)}, u32[]{:S(2)}) collective-permute-start(bf16[256,512]{1,0:T(8,128)(2,1)S(1)} %shard_map.274.halo_a), channel_id=1, source_target_pairs={{0,1},{1,0},{2,3},{3,2},{4,5},{5,4},{6,7},{7,6},{8,9},{9,8},{10,11... | collective-permute-start | bytes 786440 | tf_op jit(solution)/shard_map/ppermute | solution.py:450
  98.3 8.2 %collective-permute-start.32 = (bf16[512,128]{1,0:T(8,128)(2,1)S(1)}, bf16[512,128]{1,0:T(8,128)(2,1)S(1)}, u32[]{:S(2)}, u32[]{:S(2)}) collective-permute-start(bf16[512,128]{1,0:T(8,128)(2,1)S(1)} %copy-done.6), channel_id=1, source_target_pairs={{0,1},{1,0},{2,3},{3,2},{4,5},{5,4},{6,7},{7,6},{8,9},{9,8},{10,11... | collective-permute-start | bytes 393224 | tf_op jit(solution)/shard_map/ppermute | solution.py:450
  102.6 13.5 %collective-permute-start.38 = (bf16[1024,128]{1,0:T(8,128)(2,1)S(1)}, bf16[1024,128]{1,0:T(8,128)(2,1)S(1)}, u32[]{:S(2)}, u32[]{:S(2)}) collective-permute-start(bf16[1024,128]{1,0:T(8,128)(2,1)S(1)} %copy-done.3), channel_id=1, source_target_pairs={{0,2},{1,3},{2,0},{3,1},{4,6},{5,7},{6,4},{7,5},{8,10},{9,11},{10,... | collective-permute-start | bytes 786440 | tf_op jit(solution)/shard_map/ppermute | solution.py:450
  110.1 6.6 %collective-permute-start.35 = (bf16[2,128,512]{2,1,0:T(8,128)(2,1)S(1)}, bf16[2,128,512]{2,1,0:T(8,128)(2,1)S(1)}, u32[]{:S(2)}, u32[]{:S(2)}) collective-permute-start(bf16[2,128,512]{2,1,0:T(8,128)(2,1)S(1)} %get-tuple-element.51), channel_id=1, source_target_pairs={{0,1},{1,0},{2,3},{3,2},{4,5},{5,4},{6,7},{7,6},{8,9},{9,8},{10,11... | collective-permute-start | bytes 786440 | tf_op jit(solution)/shard_map/ppermute | solution.py:450
  110.6 5.5 %collective-permute-start.41 = (bf16[128,512]{1,0:T(8,128)(2,1)S(1)}, bf16[128,512]{1,0:T(8,128)(2,1)S(1)}, u32[]{:S(2)}, u32[]{:S(2)}) collective-permute-start(bf16[128,512]{1,0:T(8,128)(2,1)S(1)} %copy-done.7), channel_id=1, source_target_pairs={{0,2},{1,3},{2,0},{3,1},{4,6},{5,7},{6,4},{7,5},{8,10},{9,11},{10,... | collective-permute-start | bytes 393224 | tf_op jit(solution)/shard_map/ppermute | solution.py:450
  111.8 6.1 %collective-permute-start.37 = (bf16[1024,128]{1,0:T(8,128)(2,1)S(1)}, bf16[1024,128]{1,0:T(8,128)(2,1)S(1)}, u32[]{:S(2)}, u32[]{:S(2)}) collective-permute-start(bf16[1024,128]{1,0:T(8,128)(2,1)S(1)} %copy-done.3), channel_id=1, source_target_pairs={{0,1},{1,0},{2,3},{3,2},{4,5},{5,4},{6,7},{7,6},{8,9},{9,8},{10,11... | collective-permute-start | bytes 786440 | tf_op jit(solution)/shard_map/ppermute | solution.py:450
  111.8 6.1 %collective-permute-start.40 = (bf16[128,512]{1,0:T(8,128)(2,1)S(1)}, bf16[128,512]{1,0:T(8,128)(2,1)S(1)}, u32[]{:S(2)}, u32[]{:S(2)}) collective-permute-start(bf16[128,512]{1,0:T(8,128)(2,1)S(1)} %copy-done.7), channel_id=1, source_target_pairs={{0,1},{1,0},{2,3},{3,2},{4,5},{5,4},{6,7},{7,6},{8,9},{9,8},{10,11... | collective-permute-start | bytes 393224 | tf_op jit(solution)/shard_map/ppermute | solution.py:450
  116.7 5.5 %collective-permute-start.36 = (bf16[128,512]{1,0:T(8,128)(2,1)S(1)}, bf16[128,512]{1,0:T(8,128)(2,1)S(1)}, u32[]{:S(2)}, u32[]{:S(2)}) collective-permute-start(bf16[128,512]{1,0:T(8,128)(2,1)S(1)} %fusion.2), channel_id=1, source_target_pairs={{0,2},{1,3},{2,0},{3,1},{4,6},{5,7},{6,4},{7,5},{8,10},{9,11},{10,... | collective-permute-start | bytes 393224 | tf_op jit(solution)/shard_map/ppermute | solution.py:450
  (42 other events, 564.0 us)
